TPU v7x, 512 devices: a whole 4x4x16 slice. The times are simulated.
512 devices in a mesh: row: 32 (over y, z_lo), col: 16 (over z_hi, x, core).
Axes of the slice: x: 4, y: 4, z: 16 (z_hi: 2, z_lo: 8; z = z_hi * 8 + z_lo), core: 2. Of those that a mesh axis runs over, the one named last changes fastest.
Arguments:
- embeddings: bfloat16 [5, 192, 32768], P(None, None, ('row', 'col')), may hold values from -6 to 6
- scale_weights: float32 [5], replicated, may hold values from 0.1 to 0.5
- vectors: bfloat16 [32, 32768], P(None, ('row', 'col')), may hold values from -6 to 6
Outputs:
- product: float32 [32, 32768], P(None, ('row', 'col'))
All inputs are finite; a program needn't handle non-finite values.
Results may differ from a plain program's by a relative error of at most 0.011.
Values may be sent and summed in bfloat16 or wider, within the bound.
No kernel may reach another device: no remote copies, remote signals or barrier semaphores. Data moves between devices by JAX's collectives and lax.ppermute only.
A program may use at most 64 MiB of HBM per device.

v0:
```python
import math

import jax
import jax.numpy as jnp
from jax import lax
from jax.sharding import Mesh
from jax.sharding import PartitionSpec as P

COL = ("col_0", "col_1", "col_2")
ROW_COL = ("row", "col_0", "col_1", "col_2")


SHARP = 3.5


def sent_to_all(x, axis):
    copies = jnp.broadcast_to(x, (lax.axis_size(axis), *x.shape))
    return lax.all_to_all(copies, axis, split_axis=0, concat_axis=0, tiled=True)


def in_order(parts, dim):
    parts = jnp.moveaxis(parts, 0, dim)
    lengths = parts.shape
    return parts.reshape(*lengths[:dim], lengths[dim] * lengths[dim + 1], *lengths[dim + 2 :])


def gather_axes(x, axes, dim):
    far, near = axes
    initial = sent_to_all(x, far)
    parts = jnp.swapaxes(sent_to_all(initial, near), 0, 1)
    return in_order(parts.reshape(-1, *x.shape), dim)


def cut_along(x, dim, length):
    lengths = x.shape
    parts = x.reshape(*lengths[:dim], length, lengths[dim] // length, *lengths[dim + 1 :])
    return jnp.moveaxis(parts, dim, 0)


def sent_and_summed(x, axis, dim):
    length = lax.axis_size(axis)
    parts = lax.all_to_all(cut_along(x, dim, length), axis, 0, 0, tiled=True)
    return jnp.sum(parts, axis=0)


def prepare(embeddings, scale_weights):
    values = embeddings.astype(jnp.float32)
    units = values * lax.rsqrt(jnp.sum(values * values, axis=1, keepdims=True) + 1e-06)
    unit = lax.optimization_barrier(units.astype(jnp.bfloat16))
    weighted = (scale_weights[:, None, None] * unit.astype(jnp.float32)).astype(jnp.bfloat16)
    segments = embeddings.shape[2]
    return (weighted.reshape(-1, segments), unit.reshape(-1, segments))


def tile_terms(row_panel, column_panel, column_vectors, row_ids, column_ids, sharpness):
    cosine = lax.dot_general(
        row_panel, column_panel, (((0,), (0,)), ((), ())), preferred_element_type=jnp.float32
    )
    affinity = jnp.where(
        row_ids[:, None] == column_ids[None, :], jnp.zeros_like(cosine), jnp.exp(sharpness * cosine)
    )
    degree = jnp.sum(affinity, axis=1)
    numerator = lax.dot_general(
        column_vectors,
        affinity.astype(jnp.bfloat16),
        (((1,), (1,)), ((), ())),
        preferred_element_type=jnp.float32,
    )
    return (numerator, degree)


def blocked(row_panel, column_panel, column_vectors, row_ids, column_ids, sharpness):
    width = column_panel.shape[1]
    stride = math.gcd(width, 512)
    numerator = jnp.zeros((column_vectors.shape[0], row_panel.shape[1]), jnp.float32)
    degree = jnp.zeros((row_panel.shape[1],), jnp.float32)
    for offset in range(0, width, stride):
        extra_numerator, extra_degree = tile_terms(
            row_panel,
            column_panel[:, offset : offset + stride],
            column_vectors[:, offset : offset + stride],
            row_ids,
            column_ids[offset : offset + stride],
            sharpness,
        )
        numerator = numerator + extra_numerator
        degree = degree + extra_degree
    return (numerator, degree)


def shards(embeddings, scale_weights, vectors):
    segments = embeddings.shape[2]
    col_count = lax.axis_size(COL)
    row_index = lax.axis_index("row")
    col_index = lax.axis_index(COL)
    sharpness = SHARP * math.sqrt(embeddings.shape[1])
    weighted, unit = prepare(embeddings, scale_weights)

    def positions_of(panel):
        return jnp.arange(panel.shape[1], dtype=jnp.int32)

    own_panel = gather_axes(weighted, (("col_0", "col_1"), "col_2"), 1)
    own_ids = row_index * (col_count * segments) + positions_of(own_panel)
    partner_panel, partner_vectors = (
        lax.all_gather(unit, "row", axis=1, tiled=True),
        lax.all_gather(vectors, "row", axis=1, tiled=True),
    )
    positions = positions_of(partner_panel)
    numerator, degree = blocked(
        own_panel,
        partner_panel,
        partner_vectors,
        own_ids,
        (positions // segments * col_count + col_index) * segments + positions % segments,
        sharpness,
    )
    numerator, degree = (sent_and_summed(numerator, COL, 1), sent_and_summed(degree, COL, 0))
    return numerator / degree[None, :]


def solution(mesh):
    torus = Mesh(
        mesh.devices.reshape(mesh.shape["row"], 2, 4, 2), ("row", "col_0", "col_1", "col_2")
    )
    in_specs = (P(None, None, ROW_COL), P(), P(None, ROW_COL))
    out_specs = P(None, ROW_COL)
    return jax.shard_map(
        shards, mesh=torus, in_specs=in_specs, out_specs=out_specs, check_vma=False
    )
```

profile of v0, /device:TPU:1, one launch (start us, length us, event | category | flops | bytes accessed | tf_op | source)
XLA Modules:
  0.0 335.7 jit_solution(3633449502251878632)
XLA Ops:
  6.5 1.0 fusion.10
  7.6 1.0 fusion.11
  8.7 0.8 reshape.81
  9.6 0.8 multiply_convert_fusion
  10.6 1.1 broadcast_in_dim.4
  11.7 18.1 %all-to-all-start = ((bf16[8,960,64]{1,2,0:T(8,128)(2,1)}), bf16[8,960,64]{1,2,0:T(8,128)(2,1)S(1)}, u32[]{:S(2)}, u32[]{:S(2)}) async-start(bf16[8,960,64]{1,2,0:T(8,128)(2,1)} %broadcast_in_dim.4), calls=%async_computation | async-start | bytes 2097152 | tf_op jit(solution)/shard_map/all_to_all | solution.py:18
  29.8 160.5 %all-gather = bf16[32,64,32]{1,2,0:T(8,128)(2,1)S(1)} all-gather(bf16[1,64,32]{1,2,0:T(8,128)(2,1)S(1)} %bitcast.41), channel_id=1, replica_groups=mesh['row'=32,'col_0'=2,'col_1'=4,'col_2'=2] {'row'}, dimensions={0}, use_global_device_ids=true | all-gather | bytes 135168 | tf_op jit(solution)/shard_map/all_gather | solution.py:106
  190.8 0.3 broadcast_in_dim.5
  191.1 20.2 %all_to_all.21 = bf16[2,8,960,64]{2,3,1,0:T(8,128)(2,1)S(1)} all-to-all(bf16[2,8,960,64]{2,3,1,0:T(8,128)(2,1)S(1)} %broadcast_in_dim.5), channel_id=1, replica_groups=mesh['row'=32,'col_0'=2,'col_1'=4,'col_2'=2] {'col_2'}, dimensions={0} | all-to-all | bytes 3932160 | tf_op jit(solution)/shard_map/all_to_all | solution.py:18
  211.5 37.9 %all-gather.3.cloned.1.call-done = bf16[960,2048]{0,1:T(8,128)(2,1)} async-done(((bf16[960,64]{0,1:T(8,128)(2,1)}), bf16[960,2048]{0,1:T(8,128)(2,1)}) %all-gather.3.cloned.1.call-update) | async-done | bytes 3932176 | tf_op jit(solution)/shard_map/all_gather | solution.py:105
  249.4 2.9 fusion.30
  252.3 2.5 fusion.31
  254.8 2.5 fusion.29
  257.3 2.5 fusion.28
  259.8 0.7 add.112
  260.5 33.1 %all-to-all-start.3 = ((f32[16,1,64]{2,1,0:T(1,128)}), f32[16,1,64]{2,1,0:T(1,128)S(1)}, u32[]{:S(2)}, u32[]{:S(2)}) async-start(f32[16,1,64]{2,1,0:T(1,128)} %add.112), calls=%async_computation.3 | async-start | bytes 16384 | tf_op jit(solution)/shard_map/all_to_all | solution.py:42
  293.9 1.5 convolution_add_fusion.2
  296.2 0.8 reshape.85
  297.0 10.7 %all-to-all-done.3 = f32[16,1,64]{2,1,0:T(1,128)S(1)} async-done(((f32[16,1,64]{2,1,0:T(1,128)}), f32[16,1,64]{2,1,0:T(1,128)S(1)}, u32[]{:S(2)}, u32[]{:S(2)}) %all-to-all-start.3) | async-done | bytes 4128 | tf_op jit(solution)/shard_map/all_to_all | solution.py:42
  307.8 4.0 %all-to-all-start.2 = ((f32[16,1,2048]{2,1,0:T(1,128)}), f32[16,1,2048]{2,1,0:T(1,128)S(1)}, u32[]{:S(2)}, u32[]{:S(2)}) async-start(f32[16,1,2048]{2,1,0:T(1,128)} %reshape.85), calls=%async_computation.2 | async-start | bytes 262144 | tf_op jit(solution)/shard_map/all_to_all | solution.py:42
  311.8 14.9 %all-to-all-done.2 = f32[16,1,2048]{2,1,0:T(1,128)S(1)} async-done(((f32[16,1,2048]{2,1,0:T(1,128)}), f32[16,1,2048]{2,1,0:T(1,128)S(1)}, u32[]{:S(2)}, u32[]{:S(2)}) %all-to-all-start.2) | async-done | bytes 131104 | tf_op jit(solution)/shard_map/all_to_all | solution.py:42
  326.7 0.5 broadcast.43
  327.2 1.0 reduce.1
  328.3 0.6 broadcast_divide_fusion
  (30 shorter events, 2.2 us)
Async XLA Ops:
  6.5 242.9 %all-gather.3.cloned.1.call-start = ((), (), s32[]{:S(2)}) async-start(), calls=%async_computation.4 | async-start | bytes 4325376 | tf_op jit(solution)/shard_map/all_gather | solution.py:105
  10.3 19.5 %copy-start.2 = (bf16[32,64]{1,0:T(8,128)(2,1)S(1)}, bf16[32,64]{1,0:T(8,128)(2,1)}, u32[]{:S(2)}) copy-start(bf16[32,64]{1,0:T(8,128)(2,1)} %param.5) | copy-start | bytes 12292
  11.7 179.1 %all-to-all-start = ((bf16[8,960,64]{1,2,0:T(8,128)(2,1)}), bf16[8,960,64]{1,2,0:T(8,128)(2,1)S(1)}, u32[]{:S(2)}, u32[]{:S(2)}) async-start(bf16[8,960,64]{1,2,0:T(8,128)(2,1)} %broadcast_in_dim.4), calls=%async_computation | async-start | bytes 2097152 | tf_op jit(solution)/shard_map/all_to_all | solution.py:18
  249.4 2.9 copy-start.3
  259.8 35.6 %copy-start = (bf16[1024,512]{0,1:T(8,128)(2,1)S(1)}, bf16[1024,512]{0,1:T(8,128)(2,1)}, u32[]{:S(2)}) copy-start(bf16[1024,512]{0,1:T(8,128)(2,1)} %get-tuple-element.12) | copy-start | bytes 3145732
  259.8 35.9 %copy-start.1 = (bf16[1024,512]{0,1:T(8,128)(2,1)S(1)}, bf16[1024,512]{0,1:T(8,128)(2,1)}, u32[]{:S(2)}) copy-start(bf16[1024,512]{0,1:T(8,128)(2,1)} %get-tuple-element.10) | copy-start | bytes 3145732
  260.5 47.3 %all-to-all-start.3 = ((f32[16,1,64]{2,1,0:T(1,128)}), f32[16,1,64]{2,1,0:T(1,128)S(1)}, u32[]{:S(2)}, u32[]{:S(2)}) async-start(f32[16,1,64]{2,1,0:T(1,128)} %add.112), calls=%async_computation.3 | async-start | bytes 16384 | tf_op jit(solution)/shard_map/all_to_all | solution.py:42
  307.8 18.9 %all-to-all-start.2 = ((f32[16,1,2048]{2,1,0:T(1,128)}), f32[16,1,2048]{2,1,0:T(1,128)S(1)}, u32[]{:S(2)}, u32[]{:S(2)}) async-start(f32[16,1,2048]{2,1,0:T(1,128)} %reshape.85), calls=%async_computation.2 | async-start | bytes 262144 | tf_op jit(solution)/shard_map/all_to_all | solution.py:42
Sparse Core Ops, SparseCore 0:
  9.7 239.6 all-gather.2
where the time goes:
time: 336 us
  blocking collectives  181 us (54%)
  waiting for transfers between devices  63.5 us (19%)
  starting transfers between devices  55.2 us (16%)
  between operations  13.6 us (4%)
  matrix products  12.8 us (4%)
  local copies, waits for them, and re-layouts  5.49 us (2%)
  other arithmetic  4.46 us (1%)
    all_gather x1, blocking collectives, shards(): lax.all_gather(vectors, 'row', axis=1, tiled=True)  161 us
    all_gather x1, waiting for transfers between devices, shards(): lax.all_gather(unit, 'row', axis=1, tiled=True)  37.9 us
    all_to_all x2, starting transfers between devices, sent_and_summed(): parts = lax.all_to_all(cut_along(x, dim, length), axis, 0, 0, tiled=True)  37.1 us
    all_to_all x2, waiting for transfers between devices, sent_and_summed(): parts = lax.all_to_all(cut_along(x, dim, length), axis, 0, 0, tiled=True)  25.6 us
    all_to_all x1, blocking collectives, sent_to_all(): return lax.all_to_all(copies, axis, split_axis=0, concat_axis=0, tiled=True)  20.2 us
    all_to_all x1, starting transfers between devices, sent_to_all(): return lax.all_to_all(copies, axis, split_axis=0, concat_axis=0, tiled=True)  18.1 us
    dot_general x4, matrix products, tile_terms(): lax.dot_general(row_panel, column_panel, (((0,), (0,)), ((), ())), prefer...  10.4 us
  transfers between devices with their start and end apart: 4, of which 3 were waited for; matrix products, arithmetic and copies ran while one was open for 2% of the time, Pallas kernels for 0%

commit v1 on v0

v1 whole, which is shorter than its diff:
```python
import math

import jax
import jax.numpy as jnp
from jax import lax
from jax.experimental import pallas as pl
from jax.experimental.pallas import tpu as pltpu
from jax.sharding import Mesh
from jax.sharding import PartitionSpec as P

SHARP = 3.5
AXES = ("y", "zl", "zh", "x", "core")
PLANE = ("y", "x")
LINE = ("zh", "zl", "core")
LANES = 1024
TILE = 256
VMEM = pl.BlockSpec(memory_space=pltpu.VMEM)
SMEM = pl.BlockSpec(memory_space=pltpu.SMEM)


def grant(mib):
    return pltpu.CompilerParams(vmem_limit_bytes=mib << 20)


def prepare_kernel(weights_ref, embeddings_ref, vectors_ref, rows_ref, item_ref):
    scales, segments, dim = embeddings_ref.shape
    vecs = vectors_ref.shape[0]
    units, weighted = [], []
    for scale in range(scales):
        values = embeddings_ref[scale].astype(jnp.float32)
        norm = jnp.sum(values * values, axis=1, keepdims=True) + 1e-06
        unit = (values * lax.rsqrt(norm)).astype(jnp.bfloat16).astype(jnp.float32)
        units.append(unit)
        weighted.append(weights_ref[scale] * unit)
    vectors = vectors_ref[...].astype(jnp.float32)
    top = jnp.max(jnp.abs(vectors), axis=1, keepdims=True)
    power = jnp.ceil(jnp.log2(jnp.maximum(top, 2.0**-120)))
    scaled = vectors * jnp.exp2(-power)
    powers = jnp.broadcast_to(power, (vecs, segments))
    extra = jnp.concatenate([scaled, powers], axis=0).T
    rest = LANES - scales * dim
    zeros = jnp.zeros((segments, rest), jnp.float32)
    row_item = jnp.concatenate(weighted + [zeros], axis=1).astype(jnp.bfloat16)
    for peer in range(rows_ref.shape[0]):
        rows_ref[peer] = row_item
    tail = [jnp.zeros((segments, rest - 2 * vecs), jnp.float32)] if rest > 2 * vecs else []
    item_ref[...] = jnp.concatenate(units + [extra] + tail, axis=1)


def tile_kernel(depth, vecs, sharpness, starts_ref, rows_ref, columns_ref, out_ref):
    row_start, column_start = starts_ref[0], starts_ref[1]
    segments = starts_ref[2]
    row_count, column_count = rows_ref.shape[0], columns_ref.shape[0]
    row_place = lax.broadcasted_iota(jnp.int32, (row_count, 1), 0) - row_start
    row_place = jnp.where((row_place >= 0) & (row_place < segments), row_place, -1)
    total = jnp.zeros((row_count, 128), jnp.float32)
    for start in range(0, column_count, TILE):
        columns = columns_ref[start : start + TILE, :]
        cosine = lax.dot_general(
            rows_ref[...], columns, (((1,), (1,)), ((), ())), preferred_element_type=jnp.float32
        )
        place = lax.broadcasted_iota(jnp.int32, (1, TILE), 1) + (start - column_start)
        place = jnp.where((place >= 0) & (place < segments), place, -2)
        affinity = jnp.where(row_place == place, 0.0, jnp.exp2(cosine * sharpness))
        tail = columns[:, depth:].astype(jnp.float32)
        vectors = tail[:, :vecs] * jnp.exp2(tail[:, vecs : 2 * vecs])
        ones = jnp.ones((TILE, 1), jnp.float32)
        blank = jnp.zeros((TILE, 127 - vecs), jnp.float32)
        right = jnp.concatenate([vectors, ones, blank], axis=1).astype(jnp.bfloat16)
        total += jnp.dot(
            affinity.astype(jnp.bfloat16), right, preferred_element_type=jnp.float32
        )
    out_ref[...] = total.reshape(out_ref.shape)


def finish_kernel(parts_ref, out_ref):
    vecs = out_ref.shape[0]
    total = jnp.sum(parts_ref[...], axis=0).T
    out_ref[...] = total[:vecs] / total[vecs : vecs + 1]


def shards(embeddings, scale_weights, vectors):
    scales, dim, segments = embeddings.shape
    vecs = vectors.shape[0]
    peers = lax.axis_size(PLANE)
    line = lax.axis_size(LINE)
    sharpness = SHARP * math.sqrt(dim) * math.log2(math.e)
    row_copies, item = pl.pallas_call(
        prepare_kernel,
        out_shape=(
            jax.ShapeDtypeStruct((peers, segments, LANES), jnp.bfloat16),
            jax.ShapeDtypeStruct((segments, LANES), jnp.float32),
        ),
        in_specs=[SMEM, VMEM, VMEM],
        out_specs=(VMEM, VMEM),
        compiler_params=grant(4),
        name="prepare",
    )(scale_weights, jnp.swapaxes(embeddings, 1, 2), vectors)
    rows = lax.all_to_all(row_copies, PLANE, 0, 0, tiled=True)
    columns = lax.all_gather(item.astype(jnp.float16), LINE, axis=0, tiled=True)
    columns = columns.astype(jnp.bfloat16)
    starts = jnp.stack(
        [
            lax.axis_index(PLANE) * segments,
            lax.axis_index(LINE) * segments,
            jnp.int32(segments),
        ]
    )
    sums = pl.pallas_call(
        lambda *refs: tile_kernel(scales * dim, vecs, sharpness, *refs),
        out_shape=jax.ShapeDtypeStruct((peers, segments, 128), jnp.float32),
        in_specs=[SMEM, VMEM, VMEM],
        out_specs=VMEM,
        compiler_params=grant(16),
        name="tile",
    )(starts, rows.reshape(peers * segments, LANES), columns)
    parts = lax.all_to_all(sums, PLANE, 0, 0, tiled=True)
    return pl.pallas_call(
        finish_kernel,
        out_shape=jax.ShapeDtypeStruct((vecs, segments), jnp.float32),
        in_specs=[VMEM],
        out_specs=VMEM,
        compiler_params=grant(2),
        name="finish",
    )(parts)


def solution(mesh):
    torus = Mesh(mesh.devices.reshape(4, 8, 2, 4, 2), AXES)
    return jax.shard_map(
        shards,
        mesh=torus,
        in_specs=(P(None, None, AXES), P(), P(None, AXES)),
        out_specs=P(None, AXES),
        check_vma=False,
    )
```

time: 336 us -> 93.5 us (0.28)
  blocking collectives: 181 us -> 68 us
  waiting for transfers between devices: 63.5 us -> 0.01 us
  starting transfers between devices: 55.2 us -> 7.57 us
  between operations: 13.6 us -> 0.05 us
  matrix products: 12.8 us -> 0 us
  Pallas kernels: 0 us -> 8.54 us
    all_gather x1, blocking collectives: 161 us -> 50.3 us  [shards(): columns = lax.all_gather(item.astype(jnp.float16), LINE, axis=0, tiled=True)]
    all_to_all x3 -> x1, starting transfers between devices: 55.2 us -> 7.57 us  [shards(): rows = lax.all_to_all(row_copies, PLANE, 0, 0, tiled=True)]
    all_gather x1 -> x0, waiting for transfers between devices: 37.9 us -> none  [shards(): lax.all_gather(unit, 'row', axis=1, tiled=True)]
    all_to_all x3 -> x1, waiting for transfers between devices: 25.6 us -> 0.01 us  [shards(): rows = lax.all_to_all(row_copies, PLANE, 0, 0, tiled=True)]
    dot_general x8 -> x0, matrix products: 12.8 us -> none  [the longest x4 10.4 us: tile_terms(): lax.dot_general(row_panel, column_panel, (((0,), (0,)), ((), ())), prefer...]
    pallas_call x0 -> x3, Pallas kernels: none -> 8.54 us  [the longest x1 6.86 us: shards(): pl.pallas_call(lambda *refs: tile_kernel(scales * dim, vecs, sharpness, *...]
    unnamed x11 -> x10, local copies, waits for them, and re-layouts: 1.22 us -> 5.78 us
  transfers between devices with their start and end apart: 4 -> 1, of which waited for: 3 -> 0; matrix products, arithmetic and copies ran while one was open for 2% -> 3% of each run, Pallas kernels for 0% -> 0%
where the time goes in v1:
time: 93.5 us; the launch traced here: 93.2 us
  blocking collectives  68 us (73%)
  Pallas kernels  8.54 us (9%)
  starting transfers between devices  7.57 us (8%)
  local copies, waits for them, and re-layouts  5.78 us (6%)
  other arithmetic  3.26 us (3%)
    all_gather x1, blocking collectives, shards(): columns = lax.all_gather(item.astype(jnp.float16), LINE, axis=0, tiled=True)  50.3 us
    all_to_all x1, blocking collectives, shards(): parts = lax.all_to_all(sums, PLANE, 0, 0, tiled=True)  17.8 us
    all_to_all x1, starting transfers between devices, shards(): rows = lax.all_to_all(row_copies, PLANE, 0, 0, tiled=True)  7.57 us
    pallas_call x1, Pallas kernels, shards(): pl.pallas_call(lambda *refs: tile_kernel(scales * dim, vecs, sharpness, *...  6.86 us
    unnamed x10, local copies, waits for them, and re-layouts  5.78 us
    convert_element_type x1, other arithmetic, shards(): columns = columns.astype(jnp.bfloat16)  3.17 us
  transfers between devices with their start and end apart: 1, of which 0 were waited for; matrix products, arithmetic and copies ran while one was open for 3% of the time, Pallas kernels for 0%

profile of v1, /device:TPU:1, one launch (start us, length us, event | category | flops | bytes accessed | tf_op | source)
XLA Modules:
  0.0 93.2 jit_solution(16768292785634142323)
XLA Ops:
  0.0 0.0 copy-start.2
  0.0 0.9 copy-done.2
  0.9 0.0 copy-start.3
  0.9 0.7 copy-done.3
  1.6 0.0 copy-start.4
  1.6 0.7 copy-done.4
  2.3 1.0 %prepare.1 = (bf16[16,64,1024]{2,1,0:T(8,128)(2,1)S(1)}, f32[64,1024]{1,0:T(8,128)S(1)}) custom-call(f32[5]{0:T(128)S(1)} %copy-done.4, bf16[5,64,192]{2,1,0:T(8,128)(2,1)S(1)} %bitcast.5, bf16[32,64]{1,0:T(8,128)(2,1)S(1)} %copy-done.3), custom_call_target="tpu_custom_call" | custom-call | tf_op jit(solution)/shard_map/prepare/pallas_call | solution.py:88
  3.2 0.0 copy-start.1
  3.2 1.3 %copy-done.1 = bf16[16,64,1024]{2,1,0:T(8,128)(2,1)} copy-done((bf16[16,64,1024]{2,1,0:T(8,128)(2,1)}, bf16[16,64,1024]{2,1,0:T(8,128)(2,1)S(1)}, u32[]{:S(2)}) %copy-start.1) | copy-done | bytes 2097176
  4.6 7.6 %all-to-all-start = ((bf16[16,64,1024]{2,1,0:T(8,128)(2,1)}), bf16[16,64,1024]{2,1,0:T(8,128)(2,1)S(1)}, u32[]{:S(2)}, u32[]{:S(2)}) async-start(bf16[16,64,1024]{2,1,0:T(8,128)(2,1)} %copy-done.1), calls=%async_computation | async-start | bytes 4194304 | tf_op jit(solution)/shard_map/all_to_all | solution.py:99
  12.2 50.3 %all-gather.1 = f16[2048,1024]{1,0:T(8,128)(2,1)S(1)} all-gather(f16[64,1024]{1,0:T(8,128)(2,1)S(1)} %convert_element_type.6), channel_id=1, replica_groups=mesh['y'=4,'zl'=8,'zh'=2,'x'=4,'core'=2] {'zh','zl','core'}, dimensions={0}, use_global_device_ids=true | all-gather | bytes 4325376 | tf_op jit(solution)/shard_map/all_gather | solution.py:100
  62.4 3.2 %convert_element_type.7.refs_2_ = bf16[2048,1024]{1,0:T(8,128)(2,1)} convert(f16[2048,1024]{1,0:T(8,128)(2,1)S(1)} %all-gather.1) | non-fusion elementwise | flops 2097152 | bytes 8388608 | tf_op jit(solution)/shard_map/convert_element_type | solution.py:101
  65.6 0.1 pad_add_fusion.refs_0_
  65.7 0.0 all-to-all-done
  65.7 0.0 copy-start
  65.7 2.2 %copy-done = bf16[2048,1024]{1,0:T(8,128)(2,1)S(1)} copy-done((bf16[2048,1024]{1,0:T(8,128)(2,1)S(1)}, bf16[2048,1024]{1,0:T(8,128)(2,1)}, u32[]{:S(2)}) %copy-start) | copy-done | bytes 4194328
  67.9 6.9 %tile.1 = f32[16,64,128]{2,1,0:T(8,128)S(1)} custom-call(s32[3]{0:T(128)S(1)} %pad_add_fusion.refs_0_, bf16[1024,1024]{1,0:T(8,128)(2,1)S(1)} %bitcast.4, bf16[2048,1024]{1,0:T(8,128)(2,1)S(1)} %copy-done), custom_call_target="tpu_custom_call" | custom-call | tf_op jit(solution)/shard_map/tile/pallas_call | solution.py:109
  74.7 17.8 %all_to_all.10.parts_ref = f32[16,64,128]{2,1,0:T(8,128)S(1)} all-to-all(f32[16,64,128]{2,1,0:T(8,128)S(1)} %tile.1), channel_id=1, replica_groups=mesh['y'=4,'zl'=8,'zh'=2,'x'=4,'core'=2] {'y','x'}, dimensions={0} | all-to-all | bytes 1048576 | tf_op jit(solution)/shard_map/all_to_all | solution.py:117
  92.5 0.7 finish.1
  (1 shorter events, 0.0 us)
Async XLA Ops:
  0.0 0.9 copy-start.2
  0.9 0.7 copy-start.3
  1.6 0.7 copy-start.4
  3.2 1.3 %copy-start.1 = (bf16[16,64,1024]{2,1,0:T(8,128)(2,1)}, bf16[16,64,1024]{2,1,0:T(8,128)(2,1)S(1)}, u32[]{:S(2)}) copy-start(bf16[16,64,1024]{2,1,0:T(8,128)(2,1)S(1)} %get-tuple-element.7) | copy-start | bytes 6291460
  4.6 61.1 %all-to-all-start = ((bf16[16,64,1024]{2,1,0:T(8,128)(2,1)}), bf16[16,64,1024]{2,1,0:T(8,128)(2,1)S(1)}, u32[]{:S(2)}, u32[]{:S(2)}) async-start(bf16[16,64,1024]{2,1,0:T(8,128)(2,1)} %copy-done.1), calls=%async_computation | async-start | bytes 4194304 | tf_op jit(solution)/shard_map/all_to_all | solution.py:99
  65.7 2.2 %copy-start = (bf16[2048,1024]{1,0:T(8,128)(2,1)S(1)}, bf16[2048,1024]{1,0:T(8,128)(2,1)}, u32[]{:S(2)}) copy-start(bf16[2048,1024]{1,0:T(8,128)(2,1)} %convert_element_type.7.refs_2_) | copy-start | bytes 12582916

commit v2 on v1

v2 whole, which is shorter than its diff:
```python
import math

import jax
import jax.numpy as jnp
from jax import lax
from jax.experimental import pallas as pl
from jax.experimental.pallas import tpu as pltpu
from jax.sharding import Mesh
from jax.sharding import PartitionSpec as P

SHARP = 3.5
AXES = ("y", "zl", "zh", "x", "core")
PLANE = ("y", "x")
LINE = ("zh", "zl", "core")
LANES = 1024
TILE = 256
STRIP = 256
VMEM = pl.BlockSpec(memory_space=pltpu.VMEM)
HBM = pl.BlockSpec(memory_space=pltpu.HBM)
SMEM = pl.BlockSpec(memory_space=pltpu.SMEM)


def grant(mib):
    return pltpu.CompilerParams(vmem_limit_bytes=mib << 20)


def prepare_kernel(
    weights_hbm, embeddings_hbm, vectors_hbm, rows_hbm, item_ref,
    weights_ref, embeddings_ref, vectors_ref, row_ref, in_sems, out_sems
):
    loads = [
        pltpu.make_async_copy(source, target, in_sems.at[place])
        for place, (source, target) in enumerate(
            [
                (weights_hbm, weights_ref),
                (embeddings_hbm, embeddings_ref),
                (vectors_hbm, vectors_ref),
            ]
        )
    ]
    for load in loads:
        load.start()
    for load in loads:
        load.wait()
    scales, segments, dim = embeddings_ref.shape
    vecs = vectors_ref.shape[0]
    units, weighted = [], []
    for scale in range(scales):
        values = embeddings_ref[scale].astype(jnp.float32)
        norm = jnp.sum(values * values, axis=1, keepdims=True) + 1e-06
        unit = (values * lax.rsqrt(norm)).astype(jnp.bfloat16).astype(jnp.float32)
        units.append(unit)
        weighted.append(weights_ref[0, scale] * unit)
    rest = LANES - scales * dim
    zeros = jnp.zeros((segments, rest), jnp.float32)
    row_ref[...] = jnp.concatenate(weighted + [zeros], axis=1).astype(jnp.bfloat16)
    stores = [
        pltpu.make_async_copy(row_ref, rows_hbm.at[peer], out_sems.at[peer])
        for peer in range(rows_hbm.shape[0])
    ]
    for store in stores:
        store.start()
    vectors = vectors_ref[...].astype(jnp.float32)
    top = jnp.max(jnp.abs(vectors), axis=1, keepdims=True)
    power = jnp.ceil(jnp.log2(jnp.maximum(top, 2.0**-120)))
    scaled = vectors * jnp.exp2(-power)
    powers = jnp.broadcast_to(power, (vecs, segments))
    extra = jnp.concatenate([scaled, powers], axis=0).T
    tail = [jnp.zeros((segments, rest - 2 * vecs), jnp.float32)] if rest > 2 * vecs else []
    item_ref[...] = jnp.concatenate(units + [extra] + tail, axis=1)
    for store in stores:
        store.wait()


def tile_kernel(depth, vecs, sharpness, starts_ref, rows_ref, columns_ref, out_ref):
    row_count, column_count = rows_ref.shape[0], columns_ref.shape[0]
    row_start, column_start, segments = starts_ref[0], starts_ref[1], starts_ref[2]
    width = out_ref.shape[2] // 2
    row_place = lax.broadcasted_iota(jnp.int32, (row_count, 1), 0) - row_start
    row_place = jnp.where((row_place >= 0) & (row_place < segments), row_place, -1)
    totals = [jnp.zeros((STRIP, 128), jnp.float32) for _ in range(row_count // STRIP)]
    for start in range(0, column_count, TILE):
        place = lax.broadcasted_iota(jnp.int32, (1, TILE), 1) + (start - column_start)
        place = jnp.where((place >= 0) & (place < segments), place, -2)
        columns = columns_ref[start : start + TILE, :]
        tail = columns[:, depth:].astype(jnp.float32)
        vectors = tail[:, :vecs] * jnp.exp2(tail[:, vecs : 2 * vecs])
        ones = jnp.ones((TILE, 1), jnp.float32)
        blank = jnp.zeros((TILE, 127 - vecs), jnp.float32)
        right = jnp.concatenate([vectors, ones, blank], axis=1).astype(jnp.bfloat16)
        for strip in range(len(totals)):
            span = slice(strip * STRIP, (strip + 1) * STRIP)
            cosine = lax.dot_general(
                rows_ref[span, :],
                columns,
                (((1,), (1,)), ((), ())),
                preferred_element_type=jnp.float32,
            )
            affinity = jnp.where(row_place[span] == place, 0.0, jnp.exp2(cosine * sharpness))
            totals[strip] += jnp.dot(
                affinity.astype(jnp.bfloat16), right, preferred_element_type=jnp.float32
            )
    half = vecs // 2
    for strip, total in enumerate(totals):
        sums = total.T
        for peer in range(STRIP // width):
            part = sums[: vecs + 1, peer * width : (peer + 1) * width]
            place = strip * (STRIP // width) + peer
            out_ref[place, :half, :width] = part[:half]
            out_ref[place, :half, width:] = part[half:vecs]
            out_ref[place, half : half + 1, :width] = part[vecs:]
            out_ref[place, half : half + 1, width:] = part[vecs:]


def finish_kernel(parts_ref, out_ref):
    half, width = out_ref.shape[0] // 2, out_ref.shape[1]
    total = jnp.sum(parts_ref[...], axis=0)
    product = total[:half] / total[half : half + 1]
    out_ref[:half] = product[:, :width]
    out_ref[half:] = product[:, width:]


def shards(embeddings, scale_weights, vectors):
    scales, dim, segments = embeddings.shape
    vecs = vectors.shape[0]
    peers = lax.axis_size(PLANE)
    packed = vecs // 2 + 8
    sharpness = SHARP * math.sqrt(dim) * math.log2(math.e)
    row_copies, item = pl.pallas_call(
        prepare_kernel,
        out_shape=(
            jax.ShapeDtypeStruct((peers, segments, LANES), jnp.bfloat16),
            jax.ShapeDtypeStruct((segments, LANES), jnp.float32),
        ),
        in_specs=[HBM, HBM, HBM],
        out_specs=(HBM, VMEM),
        scratch_shapes=[
            pltpu.SMEM((1, scales), jnp.float32),
            pltpu.VMEM((scales, segments, dim), jnp.bfloat16),
            pltpu.VMEM((vecs, segments), jnp.bfloat16),
            pltpu.VMEM((segments, LANES), jnp.bfloat16),
            pltpu.SemaphoreType.DMA((3,)),
            pltpu.SemaphoreType.DMA((peers,)),
        ],
        compiler_params=grant(60),
        name="prepare",
    )(scale_weights[None], jnp.swapaxes(embeddings, 1, 2), vectors)
    rows = lax.all_to_all(row_copies, PLANE, 0, 0, tiled=True)
    columns = lax.all_gather(item.astype(jnp.float16), LINE, axis=0, tiled=True)
    columns = columns.astype(jnp.bfloat16)
    starts = jnp.stack(
        [
            lax.axis_index(PLANE) * segments,
            lax.axis_index(LINE) * segments,
            jnp.int32(segments),
        ]
    )
    row_count, column_count = peers * segments, columns.shape[0]
    sums = pl.pallas_call(
        lambda *refs: tile_kernel(scales * dim, vecs, sharpness, *refs),
        out_shape=jax.ShapeDtypeStruct((peers, packed, 2 * segments), jnp.float32),
        in_specs=[SMEM, VMEM, VMEM],
        out_specs=VMEM,
        compiler_params=grant(16),
        name="tile",
    )(starts, rows.reshape(row_count, LANES), columns)
    parts = lax.all_to_all(sums, PLANE, 0, 0, tiled=True)
    return pl.pallas_call(
        finish_kernel,
        out_shape=jax.ShapeDtypeStruct((vecs, segments), jnp.float32),
        in_specs=[VMEM],
        out_specs=VMEM,
        compiler_params=grant(2),
        name="finish",
    )(parts)


def solution(mesh):
    torus = Mesh(mesh.devices.reshape(4, 8, 2, 4, 2), AXES)
    return jax.shard_map(
        shards,
        mesh=torus,
        in_specs=(P(None, None, AXES), P(), P(None, AXES)),
        out_specs=P(None, AXES),
        check_vma=False,
    )
```

time: 93.5 us -> 95 us (1.016)
  Pallas kernels: 8.54 us -> 16.8 us
  local copies, waits for them, and re-layouts: 5.78 us -> 2.19 us
  blocking collectives: 68 us -> 64.8 us
    pallas_call x1, Pallas kernels: 6.86 us -> 12.8 us  [shards(): pl.pallas_call(lambda *refs: tile_kernel(scales * dim, vecs, sharpness, *...]
    unnamed x10 -> x4, local copies, waits for them, and re-layouts: 5.78 us -> 2.19 us
    all_to_all x1, blocking collectives: 17.8 us -> 14.5 us  [shards(): parts = lax.all_to_all(sums, PLANE, 0, 0, tiled=True)]
    pallas_call x1, Pallas kernels: 0.97 us -> 3.3 us  [shards(): pl.pallas_call(prepare_kernel, out_shape=(jax.ShapeDtypeStruct((peers, se...]
where the time goes in v2:
time: 95 us; the launch traced here: 94.8 us
  blocking collectives  64.8 us (68%)
  Pallas kernels  16.8 us (18%)
  starting transfers between devices  7.72 us (8%)
  other arithmetic  3.26 us (3%)
  local copies, waits for them, and re-layouts  2.19 us (2%)
    all_gather x1, blocking collectives, shards(): columns = lax.all_gather(item.astype(jnp.float16), LINE, axis=0, tiled=True)  50.3 us
    all_to_all x1, blocking collectives, shards(): parts = lax.all_to_all(sums, PLANE, 0, 0, tiled=True)  14.5 us
    pallas_call x1, Pallas kernels, shards(): pl.pallas_call(lambda *refs: tile_kernel(scales * dim, vecs, sharpness, *...  12.8 us
    all_to_all x1, starting transfers between devices, shards(): rows = lax.all_to_all(row_copies, PLANE, 0, 0, tiled=True)  7.72 us
    pallas_call x1, Pallas kernels, shards(): pl.pallas_call(prepare_kernel, out_shape=(jax.ShapeDtypeStruct((peers, se...  3.3 us
    convert_element_type x1, other arithmetic, shards(): columns = columns.astype(jnp.bfloat16)  3.16 us
    unnamed x4, local copies, waits for them, and re-layouts  2.19 us
  transfers between devices with their start and end apart: 1, of which 0 were waited for; matrix products, arithmetic and copies ran while one was open for 3% of the time, Pallas kernels for 0%

profile of v2, /device:TPU:1, one launch (start us, length us, event | category | flops | bytes accessed | tf_op | source)
XLA Modules:
  0.0 94.8 jit_solution(3011197948088817251)
XLA Ops:
  0.0 3.3 %prepare.1 = (bf16[16,64,1024]{2,1,0:T(8,128)(2,1)}, f32[64,1024]{1,0:T(8,128)}) custom-call(f32[1,5]{1,0:T(1,128)} %bitcast.7, bf16[5,64,192]{2,1,0:T(8,128)(2,1)} %bitcast.6, bf16[32,64]{1,0:T(8,128)(2,1)} %vectors_hbm.1), custom_call_target="tpu_custom_call" | custom-call | tf_op jit(solution)/shard_map/prepare/pallas_call | solution.py:129
  3.3 0.0 copy-start.1
  3.3 7.7 %all-to-all-start = ((bf16[16,64,1024]{2,1,0:T(8,128)(2,1)}), bf16[16,64,1024]{2,1,0:T(8,128)(2,1)S(1)}, u32[]{:S(2)}, u32[]{:S(2)}) async-start(bf16[16,64,1024]{2,1,0:T(8,128)(2,1)} %get-tuple-element.7), calls=%async_computation | async-start | bytes 4194304 | tf_op jit(solution)/shard_map/all_to_all | solution.py:148
  11.1 0.0 copy-done.1
  11.1 50.3 %all-gather.1 = f16[2048,1024]{1,0:T(8,128)(2,1)S(1)} all-gather(f16[64,1024]{1,0:T(8,128)(2,1)S(1)} %convert_element_type.6), channel_id=1, replica_groups=mesh['y'=4,'zl'=8,'zh'=2,'x'=4,'core'=2] {'zh','zl','core'}, dimensions={0}, use_global_device_ids=true | all-gather | bytes 4325376 | tf_op jit(solution)/shard_map/all_gather | solution.py:149
  61.3 3.2 %convert_element_type.7.refs_2_ = bf16[2048,1024]{1,0:T(8,128)(2,1)} convert(f16[2048,1024]{1,0:T(8,128)(2,1)S(1)} %all-gather.1) | non-fusion elementwise | flops 2097152 | bytes 8388608 | tf_op jit(solution)/shard_map/convert_element_type | solution.py:150
  64.5 0.1 pad_add_fusion.refs_0_
  64.6 0.0 all-to-all-done
  64.6 0.0 copy-start
  64.6 2.2 %copy-done = bf16[2048,1024]{1,0:T(8,128)(2,1)S(1)} copy-done((bf16[2048,1024]{1,0:T(8,128)(2,1)S(1)}, bf16[2048,1024]{1,0:T(8,128)(2,1)}, u32[]{:S(2)}) %copy-start) | copy-done | bytes 4194328
  66.8 12.8 %tile.1 = f32[16,24,128]{2,1,0:T(8,128)S(1)} custom-call(s32[3]{0:T(128)S(1)} %pad_add_fusion.refs_0_, bf16[1024,1024]{1,0:T(8,128)(2,1)S(1)} %bitcast.5, bf16[2048,1024]{1,0:T(8,128)(2,1)S(1)} %copy-done), custom_call_target="tpu_custom_call" | custom-call | tf_op jit(solution)/shard_map/tile/pallas_call | solution.py:159
  79.6 14.5 %all_to_all.10.parts_ref = f32[16,24,128]{2,1,0:T(8,128)S(1)} all-to-all(f32[16,24,128]{2,1,0:T(8,128)S(1)} %tile.1), channel_id=1, replica_groups=mesh['y'=4,'zl'=8,'zh'=2,'x'=4,'core'=2] {'y','x'}, dimensions={0} | all-to-all | bytes 393216 | tf_op jit(solution)/shard_map/all_to_all | solution.py:167
  94.1 0.7 finish.1
  (1 shorter events, 0.0 us)
Async XLA Ops:
  3.3 7.7 %copy-start.1 = (f32[64,1024]{1,0:T(8,128)S(1)}, f32[64,1024]{1,0:T(8,128)}, u32[]{:S(2)}) copy-start(f32[64,1024]{1,0:T(8,128)} %get-tuple-element.8) | copy-start | bytes 786436
  3.3 61.3 %all-to-all-start = ((bf16[16,64,1024]{2,1,0:T(8,128)(2,1)}), bf16[16,64,1024]{2,1,0:T(8,128)(2,1)S(1)}, u32[]{:S(2)}, u32[]{:S(2)}) async-start(bf16[16,64,1024]{2,1,0:T(8,128)(2,1)} %get-tuple-element.7), calls=%async_computation | async-start | bytes 4194304 | tf_op jit(solution)/shard_map/all_to_all | solution.py:148
  64.6 2.2 %copy-start = (bf16[2048,1024]{1,0:T(8,128)(2,1)S(1)}, bf16[2048,1024]{1,0:T(8,128)(2,1)}, u32[]{:S(2)}) copy-start(bf16[2048,1024]{1,0:T(8,128)(2,1)} %convert_element_type.7.refs_2_) | copy-start | bytes 12582916

commit v3 on v2

--- a/solution.py
+++ b/solution.py
@@ -13,8 +13,7 @@
 PLANE = ("y", "x")
 LINE = ("zh", "zl", "core")
 LANES = 1024
-TILE = 256
-STRIP = 256
+TILE = 512
 VMEM = pl.BlockSpec(memory_space=pltpu.VMEM)
 HBM = pl.BlockSpec(memory_space=pltpu.HBM)
 SMEM = pl.BlockSpec(memory_space=pltpu.SMEM)
@@ -78,7 +77,7 @@
     width = out_ref.shape[2] // 2
     row_place = lax.broadcasted_iota(jnp.int32, (row_count, 1), 0) - row_start
     row_place = jnp.where((row_place >= 0) & (row_place < segments), row_place, -1)
-    totals = [jnp.zeros((STRIP, 128), jnp.float32) for _ in range(row_count // STRIP)]
+    total = jnp.zeros((row_count, 128), jnp.float32)
     for start in range(0, column_count, TILE):
         place = lax.broadcasted_iota(jnp.int32, (1, TILE), 1) + (start - column_start)
         place = jnp.where((place >= 0) & (place < segments), place, -2)
@@ -88,28 +87,21 @@
         ones = jnp.ones((TILE, 1), jnp.float32)
         blank = jnp.zeros((TILE, 127 - vecs), jnp.float32)
         right = jnp.concatenate([vectors, ones, blank], axis=1).astype(jnp.bfloat16)
-        for strip in range(len(totals)):
-            span = slice(strip * STRIP, (strip + 1) * STRIP)
-            cosine = lax.dot_general(
-                rows_ref[span, :],
-                columns,
-                (((1,), (1,)), ((), ())),
-                preferred_element_type=jnp.float32,
-            )
-            affinity = jnp.where(row_place[span] == place, 0.0, jnp.exp2(cosine * sharpness))
-            totals[strip] += jnp.dot(
-                affinity.astype(jnp.bfloat16), right, preferred_element_type=jnp.float32
-            )
+        cosine = lax.dot_general(
+            rows_ref[...], columns, (((1,), (1,)), ((), ())), preferred_element_type=jnp.float32
+        )
+        affinity = jnp.where(row_place == place, 0.0, jnp.exp2(cosine * sharpness))
+        total += jnp.dot(
+            affinity.astype(jnp.bfloat16), right, preferred_element_type=jnp.float32
+        )
     half = vecs // 2
-    for strip, total in enumerate(totals):
-        sums = total.T
-        for peer in range(STRIP // width):
-            part = sums[: vecs + 1, peer * width : (peer + 1) * width]
-            place = strip * (STRIP // width) + peer
-            out_ref[place, :half, :width] = part[:half]
-            out_ref[place, :half, width:] = part[half:vecs]
-            out_ref[place, half : half + 1, :width] = part[vecs:]
-            out_ref[place, half : half + 1, width:] = part[vecs:]
+    sums = total.T
+    for peer in range(out_ref.shape[0]):
+        part = sums[: vecs + 1, peer * width : (peer + 1) * width]
+        out_ref[peer, :half, :width] = part[:half]
+        out_ref[peer, :half, width:] = part[half:vecs]
+        out_ref[peer, half : half + 1, :width] = part[vecs:]
+        out_ref[peer, half : half + 1, width:] = part[vecs:]
 
 
 def finish_kernel(parts_ref, out_ref):
@@ -161,7 +153,7 @@
         out_shape=jax.ShapeDtypeStruct((peers, packed, 2 * segments), jnp.float32),
         in_specs=[SMEM, VMEM, VMEM],
         out_specs=VMEM,
-        compiler_params=grant(16),
+        compiler_params=grant(24),
         name="tile",
     )(starts, rows.reshape(row_count, LANES), columns)
     parts = lax.all_to_all(sums, PLANE, 0, 0, tiled=True)

time: 95 us -> 88.8 us (0.935)
  Pallas kernels: 16.8 us -> 10.5 us
    pallas_call x1, Pallas kernels: 12.8 us -> 6.5 us  [shards(): pl.pallas_call(lambda *refs: tile_kernel(scales * dim, vecs, sharpness, *...]
  transfers between devices with their start and end apart: 1 -> 1, of which waited for: 0 -> 0; matrix products, arithmetic and copies ran while one was open for 3% -> 4% of each run, Pallas kernels for 0% -> 0%
where the time goes in v3:
time: 88.8 us; the launch traced here: 88.5 us
  blocking collectives  64.8 us (73%)
  Pallas kernels  10.5 us (12%)
  starting transfers between devices  7.72 us (9%)
  other arithmetic  3.26 us (4%)
  local copies, waits for them, and re-layouts  2.19 us (2%)
    all_gather x1, blocking collectives, shards(): columns = lax.all_gather(item.astype(jnp.float16), LINE, axis=0, tiled=True)  50.3 us
    all_to_all x1, blocking collectives, shards(): parts = lax.all_to_all(sums, PLANE, 0, 0, tiled=True)  14.5 us
    all_to_all x1, starting transfers between devices, shards(): rows = lax.all_to_all(row_copies, PLANE, 0, 0, tiled=True)  7.72 us
    pallas_call x1, Pallas kernels, shards(): pl.pallas_call(lambda *refs: tile_kernel(scales * dim, vecs, sharpness, *...  6.5 us
    pallas_call x1, Pallas kernels, shards(): pl.pallas_call(prepare_kernel, out_shape=(jax.ShapeDtypeStruct((peers, se...  3.3 us
    convert_element_type x1, other arithmetic, shards(): columns = columns.astype(jnp.bfloat16)  3.16 us
    unnamed x4, local copies, waits for them, and re-layouts  2.19 us
  transfers between devices with their start and end apart: 1, of which 0 were waited for; matrix products, arithmetic and copies ran while one was open for 4% of the time, Pallas kernels for 0%

profile of v3, /device:TPU:1, one launch (start us, length us, event | category | flops | bytes accessed | tf_op | source)
XLA Modules:
  0.0 88.5 jit_solution(8966523404085538916)
XLA Ops:
  0.0 3.3 %prepare.1 = (bf16[16,64,1024]{2,1,0:T(8,128)(2,1)}, f32[64,1024]{1,0:T(8,128)}) custom-call(f32[1,5]{1,0:T(1,128)} %bitcast.7, bf16[5,64,192]{2,1,0:T(8,128)(2,1)} %bitcast.6, bf16[32,64]{1,0:T(8,128)(2,1)} %vectors_hbm.1), custom_call_target="tpu_custom_call" | custom-call | tf_op jit(solution)/shard_map/prepare/pallas_call | solution.py:121
  3.3 0.0 copy-start.1
  3.3 7.7 %all-to-all-start = ((bf16[16,64,1024]{2,1,0:T(8,128)(2,1)}), bf16[16,64,1024]{2,1,0:T(8,128)(2,1)S(1)}, u32[]{:S(2)}, u32[]{:S(2)}) async-start(bf16[16,64,1024]{2,1,0:T(8,128)(2,1)} %get-tuple-element.7), calls=%async_computation | async-start | bytes 4194304 | tf_op jit(solution)/shard_map/all_to_all | solution.py:140
  11.1 0.0 copy-done.1
  11.1 50.3 %all-gather.1 = f16[2048,1024]{1,0:T(8,128)(2,1)S(1)} all-gather(f16[64,1024]{1,0:T(8,128)(2,1)S(1)} %convert_element_type.6), channel_id=1, replica_groups=mesh['y'=4,'zl'=8,'zh'=2,'x'=4,'core'=2] {'zh','zl','core'}, dimensions={0}, use_global_device_ids=true | all-gather | bytes 4325376 | tf_op jit(solution)/shard_map/all_gather | solution.py:141
  61.3 3.2 %convert_element_type.7.refs_2_ = bf16[2048,1024]{1,0:T(8,128)(2,1)} convert(f16[2048,1024]{1,0:T(8,128)(2,1)S(1)} %all-gather.1) | non-fusion elementwise | flops 2097152 | bytes 8388608 | tf_op jit(solution)/shard_map/convert_element_type | solution.py:142
  64.5 0.1 pad_add_fusion.refs_0_
  64.6 0.0 all-to-all-done
  64.6 0.0 copy-start
  64.6 2.2 %copy-done = bf16[2048,1024]{1,0:T(8,128)(2,1)S(1)} copy-done((bf16[2048,1024]{1,0:T(8,128)(2,1)S(1)}, bf16[2048,1024]{1,0:T(8,128)(2,1)}, u32[]{:S(2)}) %copy-start) | copy-done | bytes 4194328
  66.8 6.5 %tile.1 = f32[16,24,128]{2,1,0:T(8,128)S(1)} custom-call(s32[3]{0:T(128)S(1)} %pad_add_fusion.refs_0_, bf16[1024,1024]{1,0:T(8,128)(2,1)S(1)} %bitcast.5, bf16[2048,1024]{1,0:T(8,128)(2,1)S(1)} %copy-done), custom_call_target="tpu_custom_call" | custom-call | tf_op jit(solution)/shard_map/tile/pallas_call | solution.py:151
  73.3 14.5 %all_to_all.10.parts_ref = f32[16,24,128]{2,1,0:T(8,128)S(1)} all-to-all(f32[16,24,128]{2,1,0:T(8,128)S(1)} %tile.1), channel_id=1, replica_groups=mesh['y'=4,'zl'=8,'zh'=2,'x'=4,'core'=2] {'y','x'}, dimensions={0} | all-to-all | bytes 393216 | tf_op jit(solution)/shard_map/all_to_all | solution.py:159
  87.8 0.7 finish.1
  (1 shorter events, 0.0 us)
Async XLA Ops:
  3.3 7.7 %copy-start.1 = (f32[64,1024]{1,0:T(8,128)S(1)}, f32[64,1024]{1,0:T(8,128)}, u32[]{:S(2)}) copy-start(f32[64,1024]{1,0:T(8,128)} %get-tuple-element.8) | copy-start | bytes 786436
  3.3 61.3 %all-to-all-start = ((bf16[16,64,1024]{2,1,0:T(8,128)(2,1)}), bf16[16,64,1024]{2,1,0:T(8,128)(2,1)S(1)}, u32[]{:S(2)}, u32[]{:S(2)}) async-start(bf16[16,64,1024]{2,1,0:T(8,128)(2,1)} %get-tuple-element.7), calls=%async_computation | async-start | bytes 4194304 | tf_op jit(solution)/shard_map/all_to_all | solution.py:140
  64.6 2.2 %copy-start = (bf16[2048,1024]{1,0:T(8,128)(2,1)S(1)}, bf16[2048,1024]{1,0:T(8,128)(2,1)}, u32[]{:S(2)}) copy-start(bf16[2048,1024]{1,0:T(8,128)(2,1)} %convert_element_type.7.refs_2_) | copy-start | bytes 12582916

commit v4 on v3

v4 whole, which is shorter than its diff:
```python
import math

import jax
import jax.numpy as jnp
from jax import lax
from jax.experimental import pallas as pl
from jax.experimental.pallas import tpu as pltpu
from jax.sharding import Mesh
from jax.sharding import PartitionSpec as P

SHARP = 3.5
AXES = ("y", "zl", "zh", "x", "core")
PLANE = ("y", "x")
LINE = ("zh", "zl", "core")
LANES = 1024
TILE = 512
FIRST = 256
PART = 32
VMEM = pl.BlockSpec(memory_space=pltpu.VMEM)
HBM = pl.BlockSpec(memory_space=pltpu.HBM)
SMEM = pl.BlockSpec(memory_space=pltpu.SMEM)


def grant(mib):
    return pltpu.CompilerParams(vmem_limit_bytes=mib << 20)


def prepare_kernel(
    weights_hbm, embeddings_hbm, vectors_hbm, rows_hbm, item_hbm,
    weights_ref, embeddings_ref, vectors_ref, row_ref, item_ref, in_sems, out_sems, item_sem
):
    scales, segments, dim = embeddings_ref.shape
    vecs, peers = vectors_ref.shape[0], rows_hbm.shape[0]
    count = segments // PART
    loads = [
        pltpu.make_async_copy(weights_hbm, weights_ref, in_sems.at[0]),
        pltpu.make_async_copy(vectors_hbm, vectors_ref, in_sems.at[1]),
    ] + [
        pltpu.make_async_copy(
            embeddings_hbm.at[:, part * PART : (part + 1) * PART],
            embeddings_ref.at[:, part * PART : (part + 1) * PART],
            in_sems.at[2 + part],
        )
        for part in range(count)
    ]
    for load in loads[2:] + loads[:2]:
        load.start()
    rest = LANES - scales * dim
    row_ref[:, scales * dim :] = jnp.zeros((segments, rest), jnp.bfloat16)
    loads[0].wait()
    stores = []
    for part in range(count):
        loads[2 + part].wait()
        span = slice(part * PART, (part + 1) * PART)
        units, weighted = [], []
        for scale in range(scales):
            values = embeddings_ref[scale, span, :].astype(jnp.float32)
            norm = jnp.sum(values * values, axis=1, keepdims=True) + 1e-06
            unit = (values * lax.rsqrt(norm)).astype(jnp.bfloat16).astype(jnp.float32)
            units.append(unit)
            weighted.append(weights_ref[0, scale] * unit)
        row_ref[span, : scales * dim] = jnp.concatenate(weighted, axis=1).astype(jnp.bfloat16)
        for peer in range(peers):
            store = pltpu.make_async_copy(
                row_ref.at[span], rows_hbm.at[peer, span], out_sems.at[part, peer]
            )
            store.start()
            stores.append(store)
        item_ref[span, : scales * dim] = jnp.concatenate(units, axis=1).astype(jnp.bfloat16)
    loads[1].wait()
    vectors = vectors_ref[...].astype(jnp.float32)
    top = jnp.max(jnp.abs(vectors), axis=1, keepdims=True)
    power = jnp.ceil(jnp.log2(jnp.maximum(top, 2.0**-120)))
    scaled = vectors * jnp.exp2(-power)
    powers = jnp.broadcast_to(power, (vecs, segments))
    extra = jnp.concatenate([scaled, powers], axis=0).T
    if rest > 2 * vecs:
        tail = jnp.zeros((segments, rest - 2 * vecs), jnp.float32)
        extra = jnp.concatenate([extra, tail], axis=1)
    item_ref[:, scales * dim :] = extra.astype(jnp.bfloat16)
    keep = pltpu.make_async_copy(item_ref, item_hbm, item_sem)
    keep.start()
    for store in stores:
        store.wait()
    keep.wait()


def tile_kernel(
    depth, vecs, sharpness, starts_ref, rows_ref, columns_hbm, out_ref, columns_ref, sems
):
    bounds = [0] + list(range(FIRST, columns_ref.shape[0], TILE)) + [columns_ref.shape[0]]
    spans = [slice(start, stop) for start, stop in zip(bounds[:-1], bounds[1:])]
    loads = [
        pltpu.make_async_copy(columns_hbm.at[span], columns_ref.at[span], sems.at[place])
        for place, span in enumerate(spans)
    ]
    for load in loads:
        load.start()
    row_count = rows_ref.shape[0]
    row_start, column_start, segments = starts_ref[0], starts_ref[1], starts_ref[2]
    width = out_ref.shape[2] // 2
    row_place = lax.broadcasted_iota(jnp.int32, (row_count, 1), 0) - row_start
    row_place = jnp.where((row_place >= 0) & (row_place < segments), row_place, -1)
    total = jnp.zeros((row_count, 128), jnp.float32)
    for span, load in zip(spans, loads):
        load.wait()
        size = span.stop - span.start
        place = lax.broadcasted_iota(jnp.int32, (1, size), 1) + (span.start - column_start)
        place = jnp.where((place >= 0) & (place < segments), place, -2)
        columns = columns_ref[span, :]
        tail = columns[:, depth:].astype(jnp.float32)
        vectors = tail[:, :vecs] * jnp.exp2(tail[:, vecs : 2 * vecs])
        ones = jnp.ones((size, 1), jnp.float32)
        blank = jnp.zeros((size, 127 - vecs), jnp.float32)
        right = jnp.concatenate([vectors, ones, blank], axis=1).astype(jnp.bfloat16)
        cosine = lax.dot_general(
            rows_ref[...], columns, (((1,), (1,)), ((), ())), preferred_element_type=jnp.float32
        )
        affinity = jnp.where(row_place == place, 0.0, jnp.exp2(cosine * sharpness))
        total += jnp.dot(
            affinity.astype(jnp.bfloat16), right, preferred_element_type=jnp.float32
        )
    half = vecs // 2
    sums = total.T
    for peer in range(out_ref.shape[0]):
        part = sums[: vecs + 1, peer * width : (peer + 1) * width]
        out_ref[peer, :half, :width] = part[:half]
        out_ref[peer, :half, width:] = part[half:vecs]
        out_ref[peer, half : half + 1, :width] = part[vecs:]
        out_ref[peer, half : half + 1, width:] = part[vecs:]


def finish_kernel(parts_ref, out_ref):
    half, width = out_ref.shape[0] // 2, out_ref.shape[1]
    total = jnp.sum(parts_ref[...], axis=0)
    product = total[:half] / total[half : half + 1]
    out_ref[:half] = product[:, :width]
    out_ref[half:] = product[:, width:]


def shards(embeddings, scale_weights, vectors):
    scales, dim, segments = embeddings.shape
    vecs = vectors.shape[0]
    peers = lax.axis_size(PLANE)
    packed = vecs // 2 + 8
    sharpness = SHARP * math.sqrt(dim) * math.log2(math.e)
    row_copies, item = pl.pallas_call(
        prepare_kernel,
        out_shape=(
            jax.ShapeDtypeStruct((peers, segments, LANES), jnp.bfloat16),
            jax.ShapeDtypeStruct((segments, LANES), jnp.bfloat16),
        ),
        in_specs=[HBM, HBM, HBM],
        out_specs=(HBM, HBM),
        scratch_shapes=[
            pltpu.SMEM((1, scales), jnp.float32),
            pltpu.VMEM((scales, segments, dim), jnp.bfloat16),
            pltpu.VMEM((vecs, segments), jnp.bfloat16),
            pltpu.VMEM((segments, LANES), jnp.bfloat16),
            pltpu.VMEM((segments, LANES), jnp.bfloat16),
            pltpu.SemaphoreType.DMA((2 + segments // PART,)),
            pltpu.SemaphoreType.DMA((segments // PART, peers)),
            pltpu.SemaphoreType.DMA(()),
        ],
        compiler_params=grant(60),
        name="prepare",
    )(scale_weights[None], jnp.swapaxes(embeddings, 1, 2), vectors)
    rows = lax.all_to_all(row_copies, PLANE, 0, 0, tiled=True)
    item = item.astype(jnp.float16).reshape(segments // 8, 8, LANES)
    columns = lax.all_gather(item, LINE, axis=0, tiled=True)
    columns = columns.astype(jnp.bfloat16).reshape(-1, LANES)
    starts = jnp.stack(
        [
            lax.axis_index(PLANE) * segments,
            lax.axis_index(LINE) * segments,
            jnp.int32(segments),
        ]
    )
    row_count, column_count = peers * segments, columns.shape[0]
    sums = pl.pallas_call(
        lambda *refs: tile_kernel(scales * dim, vecs, sharpness, *refs),
        out_shape=jax.ShapeDtypeStruct((peers, packed, 2 * segments), jnp.float32),
        in_specs=[SMEM, VMEM, HBM],
        out_specs=VMEM,
        scratch_shapes=[
            pltpu.VMEM((column_count, LANES), jnp.bfloat16),
            pltpu.SemaphoreType.DMA((column_count // TILE + 1,)),
        ],
        compiler_params=grant(48),
        name="tile",
    )(starts, rows.reshape(row_count, LANES), columns)
    parts = lax.all_to_all(sums, PLANE, 0, 0, tiled=True)
    return pl.pallas_call(
        finish_kernel,
        out_shape=jax.ShapeDtypeStruct((vecs, segments), jnp.float32),
        in_specs=[VMEM],
        out_specs=VMEM,
        compiler_params=grant(2),
        name="finish",
    )(parts)


def solution(mesh):
    torus = Mesh(mesh.devices.reshape(4, 8, 2, 4, 2), AXES)
    return jax.shard_map(
        shards,
        mesh=torus,
        in_specs=(P(None, None, AXES), P(), P(None, AXES)),
        out_specs=P(None, AXES),
        check_vma=False,
    )
```

time: 88.8 us -> 89.6 us (level)
  Pallas kernels: 10.5 us -> 13.6 us
  local copies, waits for them, and re-layouts: 2.19 us -> 0.01 us
    pallas_call x1, Pallas kernels: 6.5 us -> 10.2 us  [shards(): pl.pallas_call(lambda *refs: tile_kernel(scales * dim, vecs, sharpness, *...]
    reshape x0 -> x2, other arithmetic: none -> 3.19 us  [the longest x1 3.17 us: shards(): columns = columns.astype(jnp.bfloat16).reshape(-1, LANES)]
    convert_element_type x2 -> x0, other arithmetic: 3.18 us -> none  [the longest x1 3.16 us: shards(): columns = columns.astype(jnp.bfloat16)]
    unnamed x4 -> x2, local copies, waits for them, and re-layouts: 2.19 us -> 0.01 us
where the time goes in v4:
time: 89.6 us; the launch traced here: 89.4 us
  blocking collectives  64.7 us (72%)
  Pallas kernels  13.6 us (15%)
  starting transfers between devices  7.72 us (9%)
  other arithmetic  3.27 us (4%)
    all_gather x1, blocking collectives, shards(): columns = lax.all_gather(item, LINE, axis=0, tiled=True)  50.2 us
    all_to_all x1, blocking collectives, shards(): parts = lax.all_to_all(sums, PLANE, 0, 0, tiled=True)  14.5 us
    pallas_call x1, Pallas kernels, shards(): pl.pallas_call(lambda *refs: tile_kernel(scales * dim, vecs, sharpness, *...  10.2 us
    all_to_all x1, starting transfers between devices, shards(): rows = lax.all_to_all(row_copies, PLANE, 0, 0, tiled=True)  7.72 us
    reshape x1, other arithmetic, shards(): columns = columns.astype(jnp.bfloat16).reshape(-1, LANES)  3.17 us
    pallas_call x1, Pallas kernels, shards(): pl.pallas_call(prepare_kernel, out_shape=(jax.ShapeDtypeStruct((peers, se...  2.73 us
  transfers between devices with their start and end apart: 1, of which 0 were waited for; matrix products, arithmetic and copies ran while one was open for 4% of the time, Pallas kernels for 0%

profile of v4, /device:TPU:1, one launch (start us, length us, event | category | flops | bytes accessed | tf_op | source)
XLA Modules:
  0.0 89.4 jit_solution(5650912604320067132)
XLA Ops:
  0.0 2.7 %prepare.1 = (bf16[16,64,1024]{2,1,0:T(8,128)(2,1)}, bf16[64,1024]{1,0:T(8,128)(2,1)}) custom-call(f32[1,5]{1,0:T(1,128)} %bitcast.11, bf16[5,64,192]{2,1,0:T(8,128)(2,1)} %bitcast.10, bf16[32,64]{1,0:T(8,128)(2,1)} %vectors_hbm.1), custom_call_target="tpu_custom_call" | custom-call | tf_op jit(solution)/shard_map/prepare/pallas_call | solution.py:147
  2.7 0.0 copy-start
  2.7 7.7 %all-to-all-start = ((bf16[16,64,1024]{2,1,0:T(8,128)(2,1)}), bf16[16,64,1024]{2,1,0:T(8,128)(2,1)S(1)}, u32[]{:S(2)}, u32[]{:S(2)}) async-start(bf16[16,64,1024]{2,1,0:T(8,128)(2,1)} %get-tuple-element.7), calls=%async_computation | async-start | bytes 4194304 | tf_op jit(solution)/shard_map/all_to_all | solution.py:168
  10.5 0.0 copy-done
  10.5 0.1 pad_add_fusion.refs_0_
  10.6 50.2 %all-gather.1 = f16[256,8,1024]{2,1,0:T(8,128)(2,1)S(1)} all-gather(f16[8,8,1024]{2,1,0:T(8,128)(2,1)S(1)} %convert_bitcast_fusion.1), channel_id=1, replica_groups=mesh['y'=4,'zl'=8,'zh'=2,'x'=4,'core'=2] {'zh','zl','core'}, dimensions={0}, use_global_device_ids=true | all-gather | bytes 4325376 | tf_op jit(solution)/shard_map/all_gather | solution.py:170
  60.8 3.2 %convert_bitcast_fusion.refs_2_ = bf16[2048,1024]{1,0:T(8,128)(2,1)} fusion(f16[256,8,1024]{2,1,0:T(8,128)(2,1)S(1)} %all-gather.1), kind=kLoop, calls=%fused_computation | loop fusion | flops 2097152 | bytes 8388608 | tf_op jit(solution)/shard_map/reshape | solution.py:171
  64.0 0.0 all-to-all-done
  64.0 10.2 %tile.1 = f32[16,24,128]{2,1,0:T(8,128)S(1)} custom-call(s32[3]{0:T(128)S(1)} %pad_add_fusion.refs_0_, bf16[1024,1024]{1,0:T(8,128)(2,1)S(1)} %bitcast.9, bf16[2048,1024]{1,0:T(8,128)(2,1)} %convert_bitcast_fusion.refs_2_), custom_call_target="tpu_custom_call" | custom-call | tf_op jit(solution)/shard_map/tile/pallas_call | solution.py:180
  74.2 14.5 %all_to_all.10.parts_ref = f32[16,24,128]{2,1,0:T(8,128)S(1)} all-to-all(f32[16,24,128]{2,1,0:T(8,128)S(1)} %tile.1), channel_id=1, replica_groups=mesh['y'=4,'zl'=8,'zh'=2,'x'=4,'core'=2] {'y','x'}, dimensions={0} | all-to-all | bytes 393216 | tf_op jit(solution)/shard_map/all_to_all | solution.py:192
  88.7 0.7 finish.1
  (1 shorter events, 0.0 us)
Async XLA Ops:
  2.7 7.7 %copy-start = (bf16[64,1024]{1,0:T(8,128)(2,1)S(1)}, bf16[64,1024]{1,0:T(8,128)(2,1)}, u32[]{:S(2)}) copy-start(bf16[64,1024]{1,0:T(8,128)(2,1)} %get-tuple-element.8) | copy-start | bytes 393220
  2.7 61.3 %all-to-all-start = ((bf16[16,64,1024]{2,1,0:T(8,128)(2,1)}), bf16[16,64,1024]{2,1,0:T(8,128)(2,1)S(1)}, u32[]{:S(2)}, u32[]{:S(2)}) async-start(bf16[16,64,1024]{2,1,0:T(8,128)(2,1)} %get-tuple-element.7), calls=%async_computation | async-start | bytes 4194304 | tf_op jit(solution)/shard_map/all_to_all | solution.py:168

commit v5 on v4

--- a/solution.py
+++ b/solution.py
@@ -8,13 +8,13 @@
 from jax.sharding import Mesh
 from jax.sharding import PartitionSpec as P
 
+
 SHARP = 3.5
 AXES = ("y", "zl", "zh", "x", "core")
 PLANE = ("y", "x")
-LINE = ("zh", "zl", "core")
+LINE = ("zh", "zl")
 LANES = 1024
 TILE = 512
-FIRST = 256
 PART = 32
 VMEM = pl.BlockSpec(memory_space=pltpu.VMEM)
 HBM = pl.BlockSpec(memory_space=pltpu.HBM)
@@ -85,43 +85,46 @@
     keep.wait()
 
 
-def tile_kernel(
-    depth, vecs, sharpness, starts_ref, rows_ref, columns_hbm, out_ref, columns_ref, sems
-):
-    bounds = [0] + list(range(FIRST, columns_ref.shape[0], TILE)) + [columns_ref.shape[0]]
-    spans = [slice(start, stop) for start, stop in zip(bounds[:-1], bounds[1:])]
-    loads = [
-        pltpu.make_async_copy(columns_hbm.at[span], columns_ref.at[span], sems.at[place])
-        for place, span in enumerate(spans)
-    ]
-    for load in loads:
-        load.start()
-    row_count = rows_ref.shape[0]
-    row_start, column_start, segments = starts_ref[0], starts_ref[1], starts_ref[2]
-    width = out_ref.shape[2] // 2
-    row_place = lax.broadcasted_iota(jnp.int32, (row_count, 1), 0) - row_start
-    row_place = jnp.where((row_place >= 0) & (row_place < segments), row_place, -1)
-    total = jnp.zeros((row_count, 128), jnp.float32)
-    for span, load in zip(spans, loads):
-        load.wait()
-        size = span.stop - span.start
-        place = lax.broadcasted_iota(jnp.int32, (1, size), 1) + (span.start - column_start)
-        place = jnp.where((place >= 0) & (place < segments), place, -2)
-        columns = columns_ref[span, :]
+def affinity_sums(rows_ref, columns_ref, depth, vecs, sharpness, places):
+    total = jnp.zeros((rows_ref.shape[0], 128), jnp.float32)
+    for start in range(0, columns_ref.shape[0], TILE):
+        columns = columns_ref[start : start + TILE, :]
         tail = columns[:, depth:].astype(jnp.float32)
         vectors = tail[:, :vecs] * jnp.exp2(tail[:, vecs : 2 * vecs])
-        ones = jnp.ones((size, 1), jnp.float32)
-        blank = jnp.zeros((size, 127 - vecs), jnp.float32)
+        ones = jnp.ones((TILE, 1), jnp.float32)
+        blank = jnp.zeros((TILE, 127 - vecs), jnp.float32)
         right = jnp.concatenate([vectors, ones, blank], axis=1).astype(jnp.bfloat16)
         cosine = lax.dot_general(
             rows_ref[...], columns, (((1,), (1,)), ((), ())), preferred_element_type=jnp.float32
         )
-        affinity = jnp.where(row_place == place, 0.0, jnp.exp2(cosine * sharpness))
+        affinity = jnp.exp2(cosine * sharpness)
+        if places is not None:
+            row_place, column_place = places
+            affinity = jnp.where(row_place == column_place(start), 0.0, affinity)
         total += jnp.dot(
             affinity.astype(jnp.bfloat16), right, preferred_element_type=jnp.float32
         )
-    half = vecs // 2
-    sums = total.T
+    return total
+
+
+def own_kernel(depth, vecs, sharpness, starts_ref, rows_ref, columns_ref, out_ref):
+    row_start, column_start, segments = starts_ref[0], starts_ref[1], starts_ref[2]
+    row_place = lax.broadcasted_iota(jnp.int32, (rows_ref.shape[0], 1), 0) - row_start
+    row_place = jnp.where((row_place >= 0) & (row_place < segments), row_place, -1)
+
+    def column_place(start):
+        place = lax.broadcasted_iota(jnp.int32, (1, TILE), 1) + (start - column_start)
+        return jnp.where((place >= 0) & (place < segments), place, -2)
+
+    out_ref[...] = affinity_sums(
+        rows_ref, columns_ref, depth, vecs, sharpness, (row_place, column_place)
+    )
+
+
+def other_kernel(depth, vecs, sharpness, rows_ref, columns_ref, first_ref, out_ref):
+    total = affinity_sums(rows_ref, columns_ref, depth, vecs, sharpness, None)
+    sums = (first_ref[...] + total).T
+    half, width = vecs // 2, out_ref.shape[2] // 2
     for peer in range(out_ref.shape[0]):
         part = sums[: vecs + 1, peer * width : (peer + 1) * width]
         out_ref[peer, :half, :width] = part[:half]
@@ -169,6 +172,7 @@
     item = item.astype(jnp.float16).reshape(segments // 8, 8, LANES)
     columns = lax.all_gather(item, LINE, axis=0, tiled=True)
     columns = columns.astype(jnp.bfloat16).reshape(-1, LANES)
+    others = lax.ppermute(columns, "core", [(0, 1), (1, 0)])
     starts = jnp.stack(
         [
             lax.axis_index(PLANE) * segments,
@@ -176,19 +180,25 @@
             jnp.int32(segments),
         ]
     )
-    row_count, column_count = peers * segments, columns.shape[0]
+    row_count = peers * segments
+    rows = rows.reshape(row_count, LANES)
+    settings = (scales * dim, vecs, sharpness)
+    first = pl.pallas_call(
+        lambda *refs: own_kernel(*settings, *refs),
+        out_shape=jax.ShapeDtypeStruct((row_count, 128), jnp.float32),
+        in_specs=[SMEM, VMEM, VMEM],
+        out_specs=VMEM,
+        compiler_params=grant(24),
+        name="own",
+    )(starts, rows, columns)
     sums = pl.pallas_call(
-        lambda *refs: tile_kernel(scales * dim, vecs, sharpness, *refs),
+        lambda *refs: other_kernel(*settings, *refs),
         out_shape=jax.ShapeDtypeStruct((peers, packed, 2 * segments), jnp.float32),
-        in_specs=[SMEM, VMEM, HBM],
+        in_specs=[VMEM, VMEM, VMEM],
         out_specs=VMEM,
-        scratch_shapes=[
-            pltpu.VMEM((column_count, LANES), jnp.bfloat16),
-            pltpu.SemaphoreType.DMA((column_count // TILE + 1,)),
-        ],
-        compiler_params=grant(48),
-        name="tile",
-    )(starts, rows.reshape(row_count, LANES), columns)
+        compiler_params=grant(24),
+        name="other",
+    )(rows, others, first)
     parts = lax.all_to_all(sums, PLANE, 0, 0, tiled=True)
     return pl.pallas_call(
         finish_kernel,

time: 89.6 us -> 120 us (1.34)
  waiting for transfers between devices: 0.01 us -> 33.2 us
  blocking collectives: 64.7 us -> 55 us
  starting transfers between devices: 7.72 us -> 14.8 us
    all_to_all x1, waiting for transfers between devices: 0.01 us -> 33.2 us  [shards(): rows = lax.all_to_all(row_copies, PLANE, 0, 0, tiled=True)]
    ppermute x0 -> x1, starting transfers between devices: none -> 8.08 us  [shards(): others = lax.ppermute(columns, 'core', [(0, 1), (1, 0)])]
    all_gather x1, blocking collectives: 50.2 us -> 44.6 us  [shards(): columns = lax.all_gather(item, LINE, axis=0, tiled=True)]
    all_to_all x1, blocking collectives: 14.5 us -> 10.4 us  [shards(): parts = lax.all_to_all(sums, PLANE, 0, 0, tiled=True)]
    reshape x1, other arithmetic: 3.17 us -> 1.88 us  [shards(): columns = columns.astype(jnp.bfloat16).reshape(-1, LANES)]
    pallas_call x1 -> x2, Pallas kernels: 10.2 us -> 9.9 us  [the longest x1 5.18 us: shards(): pl.pallas_call(lambda *refs: own_kernel(*settings, *refs), out_shape=jax....]
  transfers between devices with their start and end apart: 1 -> 2, of which waited for: 0 -> 1; matrix products, arithmetic and copies ran while one was open for 4% -> 0% of each run, Pallas kernels for 0% -> 4%
where the time goes in v5:
time: 120 us; the launch traced here: 119 us
  blocking collectives  55 us (46%)
  waiting for transfers between devices  33.2 us (28%)
  starting transfers between devices  14.8 us (12%)
  Pallas kernels  13.4 us (11%)
  other arithmetic  2.88 us (2%)
    all_gather x1, blocking collectives, shards(): columns = lax.all_gather(item, LINE, axis=0, tiled=True)  44.6 us
    all_to_all x1, waiting for transfers between devices, shards(): rows = lax.all_to_all(row_copies, PLANE, 0, 0, tiled=True)  33.2 us
    all_to_all x1, blocking collectives, shards(): parts = lax.all_to_all(sums, PLANE, 0, 0, tiled=True)  10.4 us
    ppermute x1, starting transfers between devices, shards(): others = lax.ppermute(columns, 'core', [(0, 1), (1, 0)])  8.08 us
    all_to_all x1, starting transfers between devices, shards(): rows = lax.all_to_all(row_copies, PLANE, 0, 0, tiled=True)  6.77 us
    pallas_call x1, Pallas kernels, shards(): pl.pallas_call(lambda *refs: own_kernel(*settings, *refs), out_shape=jax....  5.18 us
    pallas_call x1, Pallas kernels, shards(): pl.pallas_call(lambda *refs: other_kernel(*settings, *refs), out_shape=ja...  4.72 us
    pallas_call x1, Pallas kernels, shards(): pl.pallas_call(prepare_kernel, out_shape=(jax.ShapeDtypeStruct((peers, se...  2.77 us
  transfers between devices with their start and end apart: 2, of which 1 were waited for; matrix products, arithmetic and copies ran while one was open for 0% of the time, Pallas kernels for 4%

profile of v5, /device:TPU:1, one launch (start us, length us, event | category | flops | bytes accessed | tf_op | source)
XLA Modules:
  0.0 119.3 jit_solution(3101434807277405793)
XLA Ops:
  0.0 2.8 %prepare.1 = (bf16[16,64,1024]{2,1,0:T(8,128)(2,1)}, bf16[64,1024]{1,0:T(8,128)(2,1)}) custom-call(f32[1,5]{1,0:T(1,128)} %bitcast.12, bf16[5,64,192]{2,1,0:T(8,128)(2,1)} %bitcast.11, bf16[32,64]{1,0:T(8,128)(2,1)} %vectors_hbm.1), custom_call_target="tpu_custom_call" | custom-call | tf_op jit(solution)/shard_map/prepare/pallas_call | solution.py:150
  2.8 0.9 convert_bitcast_fusion.1
  3.7 44.6 %all-gather.1 = f16[128,8,1024]{2,1,0:T(8,128)(2,1)S(1)} all-gather(f16[8,8,1024]{2,1,0:T(8,128)(2,1)S(1)} %convert_bitcast_fusion.1), channel_id=1, replica_groups=mesh['y'=4,'zl'=8,'zh'=2,'x'=4,'core'=2] {'zh','zl'}, dimensions={0}, use_global_device_ids=true | all-gather | bytes 2228224 | tf_op jit(solution)/shard_map/all_gather | solution.py:173
  48.3 1.9 %convert_bitcast_fusion.refs_2_ = bf16[1024,1024]{1,0:T(8,128)(2,1)} fusion(f16[128,8,1024]{2,1,0:T(8,128)(2,1)S(1)} %all-gather.1), kind=kLoop, calls=%fused_computation | loop fusion | flops 1048576 | bytes 4194304 | tf_op jit(solution)/shard_map/reshape | solution.py:174
  50.2 8.1 %collective-permute-start = (bf16[1024,1024]{1,0:T(8,128)(2,1)}, bf16[1024,1024]{1,0:T(8,128)(2,1)}, u32[]{:S(2)}, u32[]{:S(2)}) collective-permute-start(bf16[1024,1024]{1,0:T(8,128)(2,1)} %convert_bitcast_fusion.refs_2_), channel_id=1, source_target_pairs={{0,1},{1,0},{2,3},{3,2},{4,5},{5,4},{6,7},{7,6},{8,9},{9,8},{10,11... | collective-permute-start | bytes 6291464 | tf_op jit(solution)/shard_map/ppermute | solution.py:175
  58.3 6.8 %all-to-all-start = ((bf16[16,64,1024]{2,1,0:T(8,128)(2,1)}), bf16[16,64,1024]{2,1,0:T(8,128)(2,1)S(1)}, u32[]{:S(2)}, u32[]{:S(2)}) async-start(bf16[16,64,1024]{2,1,0:T(8,128)(2,1)} %get-tuple-element.7), calls=%async_computation | async-start | bytes 4194304 | tf_op jit(solution)/shard_map/all_to_all | solution.py:171
  65.1 0.1 pad_add_fusion.refs_0_
  65.2 33.2 %all-to-all-done = bf16[16,64,1024]{2,1,0:T(8,128)(2,1)S(1)} async-done(((bf16[16,64,1024]{2,1,0:T(8,128)(2,1)}), bf16[16,64,1024]{2,1,0:T(8,128)(2,1)S(1)}, u32[]{:S(2)}, u32[]{:S(2)}) %all-to-all-start) | async-done | bytes 2097184 | tf_op jit(solution)/shard_map/all_to_all | solution.py:171
  98.4 5.2 %own.1.refs_2_ = f32[1024,128]{1,0:T(8,128)S(1)} custom-call(s32[3]{0:T(128)S(1)} %pad_add_fusion.refs_0_, bf16[1024,1024]{1,0:T(8,128)(2,1)S(1)} %bitcast.9, bf16[1024,1024]{1,0:T(8,128)(2,1)} %convert_bitcast_fusion.refs_2_), custom_call_target="tpu_custom_call" | custom-call | tf_op jit(solution)/shard_map/own/pallas_call | solution.py:186
  103.5 0.0 collective-permute-done.refs_1_
  103.6 4.7 %other.1 = f32[16,24,128]{2,1,0:T(8,128)S(1)} custom-call(bf16[1024,1024]{1,0:T(8,128)(2,1)S(1)} %bitcast.10, bf16[1024,1024]{1,0:T(8,128)(2,1)} %collective-permute-done.refs_1_, f32[1024,128]{1,0:T(8,128)S(1)} %own.1.refs_2_), custom_call_target="tpu_custom_call" | custom-call | tf_op jit(solution)/shard_map/other/pallas_call | solution.py:194
  108.3 10.4 %all_to_all.10.parts_ref = f32[16,24,128]{2,1,0:T(8,128)S(1)} all-to-all(f32[16,24,128]{2,1,0:T(8,128)S(1)} %other.1), channel_id=1, replica_groups=mesh['y'=4,'zl'=8,'zh'=2,'x'=4,'core'=2] {'y','x'}, dimensions={0} | all-to-all | bytes 393216 | tf_op jit(solution)/shard_map/all_to_all | solution.py:202
  118.6 0.7 finish.1
Async XLA Ops:
  50.2 53.3 %collective-permute-start = (bf16[1024,1024]{1,0:T(8,128)(2,1)}, bf16[1024,1024]{1,0:T(8,128)(2,1)}, u32[]{:S(2)}, u32[]{:S(2)}) collective-permute-start(bf16[1024,1024]{1,0:T(8,128)(2,1)} %convert_bitcast_fusion.refs_2_), channel_id=1, source_target_pairs={{0,1},{1,0},{2,3},{3,2},{4,5},{5,4},{6,7},{7,6},{8,9},{9,8},{10,11... | collective-permute-start | bytes 6291464 | tf_op jit(solution)/shard_map/ppermute | solution.py:175
  58.3 40.0 %all-to-all-start = ((bf16[16,64,1024]{2,1,0:T(8,128)(2,1)}), bf16[16,64,1024]{2,1,0:T(8,128)(2,1)S(1)}, u32[]{:S(2)}, u32[]{:S(2)}) async-start(bf16[16,64,1024]{2,1,0:T(8,128)(2,1)} %get-tuple-element.7), calls=%async_computation | async-start | bytes 4194304 | tf_op jit(solution)/shard_map/all_to_all | solution.py:171

commit v6 on v4

--- a/solution.py
+++ b/solution.py
@@ -14,7 +14,6 @@
 LINE = ("zh", "zl", "core")
 LANES = 1024
 TILE = 512
-FIRST = 256
 PART = 32
 VMEM = pl.BlockSpec(memory_space=pltpu.VMEM)
 HBM = pl.BlockSpec(memory_space=pltpu.HBM)
@@ -85,33 +84,21 @@
     keep.wait()
 
 
-def tile_kernel(
-    depth, vecs, sharpness, starts_ref, rows_ref, columns_hbm, out_ref, columns_ref, sems
-):
-    bounds = [0] + list(range(FIRST, columns_ref.shape[0], TILE)) + [columns_ref.shape[0]]
-    spans = [slice(start, stop) for start, stop in zip(bounds[:-1], bounds[1:])]
-    loads = [
-        pltpu.make_async_copy(columns_hbm.at[span], columns_ref.at[span], sems.at[place])
-        for place, span in enumerate(spans)
-    ]
-    for load in loads:
-        load.start()
-    row_count = rows_ref.shape[0]
+def tile_kernel(depth, vecs, sharpness, starts_ref, rows_ref, columns_ref, out_ref):
+    row_count, column_count = rows_ref.shape[0], columns_ref.shape[0]
     row_start, column_start, segments = starts_ref[0], starts_ref[1], starts_ref[2]
     width = out_ref.shape[2] // 2
     row_place = lax.broadcasted_iota(jnp.int32, (row_count, 1), 0) - row_start
     row_place = jnp.where((row_place >= 0) & (row_place < segments), row_place, -1)
     total = jnp.zeros((row_count, 128), jnp.float32)
-    for span, load in zip(spans, loads):
-        load.wait()
-        size = span.stop - span.start
-        place = lax.broadcasted_iota(jnp.int32, (1, size), 1) + (span.start - column_start)
+    for start in range(0, column_count, TILE):
+        place = lax.broadcasted_iota(jnp.int32, (1, TILE), 1) + (start - column_start)
         place = jnp.where((place >= 0) & (place < segments), place, -2)
-        columns = columns_ref[span, :]
+        columns = columns_ref[start : start + TILE, :]
         tail = columns[:, depth:].astype(jnp.float32)
         vectors = tail[:, :vecs] * jnp.exp2(tail[:, vecs : 2 * vecs])
-        ones = jnp.ones((size, 1), jnp.float32)
-        blank = jnp.zeros((size, 127 - vecs), jnp.float32)
+        ones = jnp.ones((TILE, 1), jnp.float32)
+        blank = jnp.zeros((TILE, 127 - vecs), jnp.float32)
         right = jnp.concatenate([vectors, ones, blank], axis=1).astype(jnp.bfloat16)
         cosine = lax.dot_general(
             rows_ref[...], columns, (((1,), (1,)), ((), ())), preferred_element_type=jnp.float32
@@ -168,6 +155,7 @@
     rows = lax.all_to_all(row_copies, PLANE, 0, 0, tiled=True)
     item = item.astype(jnp.float16).reshape(segments // 8, 8, LANES)
     columns = lax.all_gather(item, LINE, axis=0, tiled=True)
+    rows, columns = lax.optimization_barrier((rows, columns))
     columns = columns.astype(jnp.bfloat16).reshape(-1, LANES)
     starts = jnp.stack(
         [
@@ -180,13 +168,9 @@
     sums = pl.pallas_call(
         lambda *refs: tile_kernel(scales * dim, vecs, sharpness, *refs),
         out_shape=jax.ShapeDtypeStruct((peers, packed, 2 * segments), jnp.float32),
-        in_specs=[SMEM, VMEM, HBM],
+        in_specs=[SMEM, VMEM, VMEM],
         out_specs=VMEM,
-        scratch_shapes=[
-            pltpu.VMEM((column_count, LANES), jnp.bfloat16),
-            pltpu.SemaphoreType.DMA((column_count // TILE + 1,)),
-        ],
-        compiler_params=grant(48),
+        compiler_params=grant(24),
         name="tile",
     )(starts, rows.reshape(row_count, LANES), columns)
     parts = lax.all_to_all(sums, PLANE, 0, 0, tiled=True)

time: 89.6 us -> 87.7 us (0.979)
  Pallas kernels: 13.6 us -> 9.97 us
  blocking collectives: 64.7 us -> 66.3 us
    pallas_call x1, Pallas kernels: 10.2 us -> 6.54 us  [shards(): pl.pallas_call(lambda *refs: tile_kernel(scales * dim, vecs, sharpness, *...]
    all_gather x1, blocking collectives: 50.2 us -> 51.8 us  [shards(): columns = lax.all_gather(item, LINE, axis=0, tiled=True)]
  transfers between devices with their start and end apart: 1 -> 1, of which waited for: 0 -> 0; matrix products, arithmetic and copies ran while one was open for 4% -> 0% of each run, Pallas kernels for 0% -> 0%
where the time goes in v6:
time: 87.7 us; the launch traced here: 87.5 us
  blocking collectives  66.3 us (76%)
  Pallas kernels  9.97 us (11%)
  starting transfers between devices  7.72 us (9%)
  other arithmetic  3.44 us (4%)
    all_gather x1, blocking collectives, shards(): columns = lax.all_gather(item, LINE, axis=0, tiled=True)  51.8 us
    all_to_all x1, blocking collectives, shards(): parts = lax.all_to_all(sums, PLANE, 0, 0, tiled=True)  14.5 us
    all_to_all x1, starting transfers between devices, shards(): rows = lax.all_to_all(row_copies, PLANE, 0, 0, tiled=True)  7.72 us
    pallas_call x1, Pallas kernels, shards(): pl.pallas_call(lambda *refs: tile_kernel(scales * dim, vecs, sharpness, *...  6.54 us
    reshape x1, other arithmetic, shards(): columns = columns.astype(jnp.bfloat16).reshape(-1, LANES)  3.33 us
    pallas_call x1, Pallas kernels, shards(): pl.pallas_call(prepare_kernel, out_shape=(jax.ShapeDtypeStruct((peers, se...  2.73 us
  transfers between devices with their start and end apart: 1, of which 0 were waited for; matrix products, arithmetic and copies ran while one was open for 0% of the time, Pallas kernels for 0%

profile of v6, /device:TPU:1, one launch (start us, length us, event | category | flops | bytes accessed | tf_op | source)
XLA Modules:
  0.0 87.5 jit_solution(8723060398804895625)
XLA Ops:
  0.0 2.7 %prepare.1 = (bf16[16,64,1024]{2,1,0:T(8,128)(2,1)}, bf16[64,1024]{1,0:T(8,128)(2,1)}) custom-call(f32[1,5]{1,0:T(1,128)} %bitcast.11, bf16[5,64,192]{2,1,0:T(8,128)(2,1)} %bitcast.10, bf16[32,64]{1,0:T(8,128)(2,1)} %vectors_hbm.1), custom_call_target="tpu_custom_call" | custom-call | tf_op jit(solution)/shard_map/prepare/pallas_call | solution.py:134
  2.7 0.0 copy-start
  2.7 7.7 %all-to-all-start = ((bf16[16,64,1024]{2,1,0:T(8,128)(2,1)}), bf16[16,64,1024]{2,1,0:T(8,128)(2,1)S(1)}, u32[]{:S(2)}, u32[]{:S(2)}) async-start(bf16[16,64,1024]{2,1,0:T(8,128)(2,1)} %get-tuple-element.9), calls=%async_computation | async-start | bytes 4194304 | tf_op jit(solution)/shard_map/all_to_all | solution.py:155
  10.5 0.0 copy-done
  10.5 0.1 pad_add_fusion.refs_0_
  10.6 51.8 %all-gather.1 = f16[256,8,1024]{2,1,0:T(8,128)(2,1)} all-gather(f16[8,8,1024]{2,1,0:T(8,128)(2,1)S(1)} %convert_bitcast_fusion.1), channel_id=1, replica_groups=mesh['y'=4,'zl'=8,'zh'=2,'x'=4,'core'=2] {'zh','zl','core'}, dimensions={0}, use_global_device_ids=true | all-gather | bytes 4325376 | tf_op jit(solution)/shard_map/all_gather | solution.py:157
  62.4 0.0 all-to-all-done
  62.4 3.3 %convert_bitcast_fusion.refs_2_ = bf16[2048,1024]{1,0:T(8,128)(2,1)S(1)} fusion(f16[256,8,1024]{2,1,0:T(8,128)(2,1)} %all-gather.1), kind=kLoop, calls=%fused_computation | loop fusion | flops 2097152 | bytes 8388608 | tf_op jit(solution)/shard_map/reshape | solution.py:159
  65.7 6.5 %tile.1 = f32[16,24,128]{2,1,0:T(8,128)S(1)} custom-call(s32[3]{0:T(128)S(1)} %pad_add_fusion.refs_0_, bf16[1024,1024]{1,0:T(8,128)(2,1)S(1)} %bitcast.9, bf16[2048,1024]{1,0:T(8,128)(2,1)S(1)} %convert_bitcast_fusion.refs_2_), custom_call_target="tpu_custom_call" | custom-call | tf_op jit(solution)/shard_map/tile/pallas_call | solution.py:168
  72.2 14.5 %all_to_all.10.parts_ref = f32[16,24,128]{2,1,0:T(8,128)S(1)} all-to-all(f32[16,24,128]{2,1,0:T(8,128)S(1)} %tile.1), channel_id=1, replica_groups=mesh['y'=4,'zl'=8,'zh'=2,'x'=4,'core'=2] {'y','x'}, dimensions={0} | all-to-all | bytes 393216 | tf_op jit(solution)/shard_map/all_to_all | solution.py:176
  86.8 0.7 finish.1
  (1 shorter events, 0.0 us)
Async XLA Ops:
  2.7 7.7 %copy-start = (bf16[64,1024]{1,0:T(8,128)(2,1)S(1)}, bf16[64,1024]{1,0:T(8,128)(2,1)}, u32[]{:S(2)}) copy-start(bf16[64,1024]{1,0:T(8,128)(2,1)} %get-tuple-element.10) | copy-start | bytes 393220
  2.7 59.6 %all-to-all-start = ((bf16[16,64,1024]{2,1,0:T(8,128)(2,1)}), bf16[16,64,1024]{2,1,0:T(8,128)(2,1)S(1)}, u32[]{:S(2)}, u32[]{:S(2)}) async-start(bf16[16,64,1024]{2,1,0:T(8,128)(2,1)} %get-tuple-element.9), calls=%async_computation | async-start | bytes 4194304 | tf_op jit(solution)/shard_map/all_to_all | solution.py:155

commit v7 on v6

--- a/solution.py
+++ b/solution.py
@@ -13,11 +13,9 @@
 PLANE = ("y", "x")
 LINE = ("zh", "zl", "core")
 LANES = 1024
-TILE = 512
 PART = 32
 VMEM = pl.BlockSpec(memory_space=pltpu.VMEM)
 HBM = pl.BlockSpec(memory_space=pltpu.HBM)
-SMEM = pl.BlockSpec(memory_space=pltpu.SMEM)
 
 
 def grant(mib):
@@ -84,37 +82,27 @@
     keep.wait()
 
 
-def tile_kernel(depth, vecs, sharpness, starts_ref, rows_ref, columns_ref, out_ref):
-    row_count, column_count = rows_ref.shape[0], columns_ref.shape[0]
-    row_start, column_start, segments = starts_ref[0], starts_ref[1], starts_ref[2]
-    width = out_ref.shape[2] // 2
-    row_place = lax.broadcasted_iota(jnp.int32, (row_count, 1), 0) - row_start
-    row_place = jnp.where((row_place >= 0) & (row_place < segments), row_place, -1)
-    total = jnp.zeros((row_count, 128), jnp.float32)
-    for start in range(0, column_count, TILE):
-        place = lax.broadcasted_iota(jnp.int32, (1, TILE), 1) + (start - column_start)
-        place = jnp.where((place >= 0) & (place < segments), place, -2)
-        columns = columns_ref[start : start + TILE, :]
-        tail = columns[:, depth:].astype(jnp.float32)
-        vectors = tail[:, :vecs] * jnp.exp2(tail[:, vecs : 2 * vecs])
-        ones = jnp.ones((TILE, 1), jnp.float32)
-        blank = jnp.zeros((TILE, 127 - vecs), jnp.float32)
-        right = jnp.concatenate([vectors, ones, blank], axis=1).astype(jnp.bfloat16)
-        cosine = lax.dot_general(
-            rows_ref[...], columns, (((1,), (1,)), ((), ())), preferred_element_type=jnp.float32
-        )
-        affinity = jnp.where(row_place == place, 0.0, jnp.exp2(cosine * sharpness))
-        total += jnp.dot(
-            affinity.astype(jnp.bfloat16), right, preferred_element_type=jnp.float32
-        )
-    half = vecs // 2
+def sums_kernel(vecs, affinity_ref, tail_ref, out_ref):
+    count = tail_ref.shape[0]
+    tail = tail_ref[...].astype(jnp.float32)
+    vectors = tail[:, :vecs] * jnp.exp2(tail[:, vecs : 2 * vecs])
+    ones = jnp.ones((count, 1), jnp.float32)
+    blank = jnp.zeros((count, 127 - vecs), jnp.float32)
+    right = jnp.concatenate([vectors, ones, blank], axis=1).astype(jnp.bfloat16)
+    total = jnp.dot(affinity_ref[...], right, preferred_element_type=jnp.float32)
     sums = total.T
+    half, width = vecs // 2, out_ref.shape[2] // 2
     for peer in range(out_ref.shape[0]):
         part = sums[: vecs + 1, peer * width : (peer + 1) * width]
         out_ref[peer, :half, :width] = part[:half]
         out_ref[peer, :half, width:] = part[half:vecs]
         out_ref[peer, half : half + 1, :width] = part[vecs:]
         out_ref[peer, half : half + 1, width:] = part[vecs:]
+
+
+def places(count, start, segments, outside):
+    place = jnp.arange(count, dtype=jnp.int32) - start
+    return jnp.where((place >= 0) & (place < segments), place, outside)
 
 
 def finish_kernel(parts_ref, out_ref):
@@ -156,23 +144,26 @@
     item = item.astype(jnp.float16).reshape(segments // 8, 8, LANES)
     columns = lax.all_gather(item, LINE, axis=0, tiled=True)
     rows, columns = lax.optimization_barrier((rows, columns))
-    columns = columns.astype(jnp.bfloat16).reshape(-1, LANES)
-    starts = jnp.stack(
-        [
-            lax.axis_index(PLANE) * segments,
-            lax.axis_index(LINE) * segments,
-            jnp.int32(segments),
-        ]
+    columns = columns.reshape(-1, LANES)
+    row_count, column_count = peers * segments, columns.shape[0]
+    cosine = lax.dot_general(
+        rows.reshape(row_count, LANES),
+        columns.astype(jnp.bfloat16),
+        (((1,), (1,)), ((), ())),
+        preferred_element_type=jnp.float32,
     )
-    row_count, column_count = peers * segments, columns.shape[0]
+    row_places = places(row_count, lax.axis_index(PLANE) * segments, segments, -1)
+    column_places = places(column_count, lax.axis_index(LINE) * segments, segments, -2)
+    same = row_places[:, None] == column_places[None, :]
+    affinity = jnp.where(same, 0.0, jnp.exp2(cosine * sharpness)).astype(jnp.bfloat16)
     sums = pl.pallas_call(
-        lambda *refs: tile_kernel(scales * dim, vecs, sharpness, *refs),
+        lambda *refs: sums_kernel(vecs, *refs),
         out_shape=jax.ShapeDtypeStruct((peers, packed, 2 * segments), jnp.float32),
-        in_specs=[SMEM, VMEM, VMEM],
+        in_specs=[VMEM, VMEM],
         out_specs=VMEM,
-        compiler_params=grant(24),
-        name="tile",
-    )(starts, rows.reshape(row_count, LANES), columns)
+        compiler_params=grant(16),
+        name="sums",
+    )(affinity, columns[:, scales * dim :].astype(jnp.bfloat16))
     parts = lax.all_to_all(sums, PLANE, 0, 0, tiled=True)
     return pl.pallas_call(
         finish_kernel,

time: 87.7 us -> 88.3 us (level)
  matrix products: 0 us -> 7.62 us
  Pallas kernels: 9.97 us -> 4.99 us
  other arithmetic: 3.44 us -> 1.29 us
    dot_general x0 -> x1, matrix products: none -> 7.62 us  [shards(): lax.dot_general(rows.reshape(row_count, LANES), columns.astype(jnp.bfloat...]
    pallas_call x1, Pallas kernels: 6.54 us -> 1.56 us  [shards(): pl.pallas_call(lambda *refs: sums_kernel(vecs, *refs), out_shape=jax.Shap...]
    reshape x1 -> x0, other arithmetic: 3.33 us -> none  [shards(): columns = columns.astype(jnp.bfloat16).reshape(-1, LANES)]
    convert_element_type x0 -> x1, other arithmetic: none -> 1.25 us  [shards(): columns[:, scales * dim:].astype(jnp.bfloat16)]
where the time goes in v7:
time: 88.3 us; the launch traced here: 88 us
  blocking collectives  66.3 us (75%)
  starting transfers between devices  7.72 us (9%)
  matrix products  7.62 us (9%)
  Pallas kernels  4.99 us (6%)
  other arithmetic  1.29 us (1%)
    all_gather x1, blocking collectives, shards(): columns = lax.all_gather(item, LINE, axis=0, tiled=True)  51.8 us
    all_to_all x1, blocking collectives, shards(): parts = lax.all_to_all(sums, PLANE, 0, 0, tiled=True)  14.5 us
    all_to_all x1, starting transfers between devices, shards(): rows = lax.all_to_all(row_copies, PLANE, 0, 0, tiled=True)  7.72 us
    dot_general x1, matrix products, shards(): lax.dot_general(rows.reshape(row_count, LANES), columns.astype(jnp.bfloat...  7.62 us
    pallas_call x1, Pallas kernels, shards(): pl.pallas_call(prepare_kernel, out_shape=(jax.ShapeDtypeStruct((peers, se...  2.73 us
  transfers between devices with their start and end apart: 1, of which 0 were waited for; matrix products, arithmetic and copies ran while one was open for 0% of the time, Pallas kernels for 0%

profile of v7, /device:TPU:1, one launch (start us, length us, event | category | flops | bytes accessed | tf_op | source)
XLA Modules:
  0.0 88.0 jit_solution(17574461781897770667)
XLA Ops:
  0.0 2.7 %prepare.1 = (bf16[16,64,1024]{2,1,0:T(8,128)(2,1)}, bf16[64,1024]{1,0:T(8,128)(2,1)}) custom-call(f32[1,5]{1,0:T(1,128)} %bitcast.13, bf16[5,64,192]{2,1,0:T(8,128)(2,1)} %bitcast.12, bf16[32,64]{1,0:T(8,128)(2,1)} %vectors_hbm.1), custom_call_target="tpu_custom_call" | custom-call | tf_op jit(solution)/shard_map/prepare/pallas_call | solution.py:122
  2.7 0.0 copy-start
  2.7 7.7 %all-to-all-start = ((bf16[16,64,1024]{2,1,0:T(8,128)(2,1)}), bf16[16,64,1024]{2,1,0:T(8,128)(2,1)S(1)}, u32[]{:S(2)}, u32[]{:S(2)}) async-start(bf16[16,64,1024]{2,1,0:T(8,128)(2,1)} %get-tuple-element.9), calls=%async_computation | async-start | bytes 4194304 | tf_op jit(solution)/shard_map/all_to_all | solution.py:143
  10.5 0.0 copy-done
  10.6 51.8 %all-gather.1 = f16[256,8,1024]{2,1,0:T(8,128)(2,1)} all-gather(f16[8,8,1024]{2,1,0:T(8,128)(2,1)S(1)} %convert_bitcast_fusion), channel_id=1, replica_groups=mesh['y'=4,'zl'=8,'zh'=2,'x'=4,'core'=2] {'zh','zl','core'}, dimensions={0}, use_global_device_ids=true | all-gather | bytes 4325376 | tf_op jit(solution)/shard_map/all_gather | solution.py:145
  62.3 0.0 all-to-all-done
  62.3 1.2 %slice_convert_fusion.refs_1_ = bf16[2048,64]{1,0:T(8,128)(2,1)S(1)} fusion(f16[2048,1024]{1,0:T(8,128)(2,1)} %bitcast.10), kind=kLoop, calls=%fused_computation.3 | loop fusion | flops 131072 | bytes 524288 | tf_op jit(solution)/shard_map/convert_element_type | solution.py:166
  63.6 7.6 %select_convert_fusion.refs_0_ = bf16[1024,2048]{1,0:T(8,128)(2,1)S(1)} fusion(bf16[1024,1024]{1,0:T(8,128)(2,1)S(1)} %bitcast.11, f16[256,8,1024]{2,1,0:T(8,128)(2,1)} %all-gather.1, s32[2048]{0:T(1024)S(1)} %fusion.2, s32[1024]{0:T(1024)S(1)} %fusion.6), kind=kOutput, calls=%fused_computation | convolution fusion | flops 4305453056 | bytes 10498048 | tf_op jit(solution)/shard_map/dot_general | solution.py:149
  71.2 1.6 %sums.1 = f32[16,24,128]{2,1,0:T(8,128)S(1)} custom-call(bf16[1024,2048]{1,0:T(8,128)(2,1)S(1)} %select_convert_fusion.refs_0_, bf16[2048,64]{1,0:T(8,128)(2,1)S(1)} %slice_convert_fusion.refs_1_), custom_call_target="tpu_custom_call" | custom-call | tf_op jit(solution)/shard_map/sums/pallas_call | solution.py:159
  72.8 14.5 %all_to_all.10.parts_ref = f32[16,24,128]{2,1,0:T(8,128)S(1)} all-to-all(f32[16,24,128]{2,1,0:T(8,128)S(1)} %sums.1), channel_id=1, replica_groups=mesh['y'=4,'zl'=8,'zh'=2,'x'=4,'core'=2] {'y','x'}, dimensions={0} | all-to-all | bytes 393216 | tf_op jit(solution)/shard_map/all_to_all | solution.py:167
  87.3 0.7 finish.1
  (3 shorter events, 0.0 us)
Async XLA Ops:
  2.7 7.8 %copy-start = (bf16[64,1024]{1,0:T(8,128)(2,1)S(1)}, bf16[64,1024]{1,0:T(8,128)(2,1)}, u32[]{:S(2)}) copy-start(bf16[64,1024]{1,0:T(8,128)(2,1)} %get-tuple-element.10) | copy-start | bytes 393220
  2.7 59.6 %all-to-all-start = ((bf16[16,64,1024]{2,1,0:T(8,128)(2,1)}), bf16[16,64,1024]{2,1,0:T(8,128)(2,1)S(1)}, u32[]{:S(2)}, u32[]{:S(2)}) async-start(bf16[16,64,1024]{2,1,0:T(8,128)(2,1)} %get-tuple-element.9), calls=%async_computation | async-start | bytes 4194304 | tf_op jit(solution)/shard_map/all_to_all | solution.py:143

commit v8 on v7

--- a/solution.py
+++ b/solution.py
@@ -14,6 +14,7 @@
 LINE = ("zh", "zl", "core")
 LANES = 1024
 PART = 32
+SMEM = pl.BlockSpec(memory_space=pltpu.SMEM)
 VMEM = pl.BlockSpec(memory_space=pltpu.VMEM)
 HBM = pl.BlockSpec(memory_space=pltpu.HBM)
 
@@ -82,27 +83,29 @@
     keep.wait()
 
 
-def sums_kernel(vecs, affinity_ref, tail_ref, out_ref):
+def sums_kernel(vecs, width, starts_ref, affinity_ref, tail_ref, out_ref, total_ref):
     count = tail_ref.shape[0]
     tail = tail_ref[...].astype(jnp.float32)
     vectors = tail[:, :vecs] * jnp.exp2(tail[:, vecs : 2 * vecs])
     ones = jnp.ones((count, 1), jnp.float32)
     blank = jnp.zeros((count, 127 - vecs), jnp.float32)
     right = jnp.concatenate([vectors, ones, blank], axis=1).astype(jnp.bfloat16)
-    total = jnp.dot(affinity_ref[...], right, preferred_element_type=jnp.float32)
-    sums = total.T
-    half, width = vecs // 2, out_ref.shape[2] // 2
+    total_ref[...] = jnp.dot(affinity_ref[...], right, preferred_element_type=jnp.float32)
+    own = pl.ds(pl.multiple_of(starts_ref[0], width), width)
+    row_place = lax.broadcasted_iota(jnp.int32, (width, 1), 0)
+    column_place = lax.broadcasted_iota(jnp.int32, (1, count), 1) - starts_ref[1]
+    kept = jnp.where(row_place == column_place, 0.0, affinity_ref[own, :].astype(jnp.float32))
+    total_ref[own, :] = jnp.dot(
+        kept.astype(jnp.bfloat16), right, preferred_element_type=jnp.float32
+    )
+    sums = total_ref[...].T
+    half = vecs // 2
     for peer in range(out_ref.shape[0]):
         part = sums[: vecs + 1, peer * width : (peer + 1) * width]
         out_ref[peer, :half, :width] = part[:half]
         out_ref[peer, :half, width:] = part[half:vecs]
         out_ref[peer, half : half + 1, :width] = part[vecs:]
         out_ref[peer, half : half + 1, width:] = part[vecs:]
-
-
-def places(count, start, segments, outside):
-    place = jnp.arange(count, dtype=jnp.int32) - start
-    return jnp.where((place >= 0) & (place < segments), place, outside)
 
 
 def finish_kernel(parts_ref, out_ref):
@@ -143,27 +146,25 @@
     rows = lax.all_to_all(row_copies, PLANE, 0, 0, tiled=True)
     item = item.astype(jnp.float16).reshape(segments // 8, 8, LANES)
     columns = lax.all_gather(item, LINE, axis=0, tiled=True)
-    rows, columns = lax.optimization_barrier((rows, columns))
     columns = columns.reshape(-1, LANES)
-    row_count, column_count = peers * segments, columns.shape[0]
+    row_count = peers * segments
     cosine = lax.dot_general(
         rows.reshape(row_count, LANES),
         columns.astype(jnp.bfloat16),
         (((1,), (1,)), ((), ())),
         preferred_element_type=jnp.float32,
     )
-    row_places = places(row_count, lax.axis_index(PLANE) * segments, segments, -1)
-    column_places = places(column_count, lax.axis_index(LINE) * segments, segments, -2)
-    same = row_places[:, None] == column_places[None, :]
-    affinity = jnp.where(same, 0.0, jnp.exp2(cosine * sharpness)).astype(jnp.bfloat16)
+    affinity = jnp.exp2(cosine * sharpness).astype(jnp.bfloat16)
+    starts = jnp.stack([lax.axis_index(PLANE) * segments, lax.axis_index(LINE) * segments])
     sums = pl.pallas_call(
-        lambda *refs: sums_kernel(vecs, *refs),
+        lambda *refs: sums_kernel(vecs, segments, *refs),
         out_shape=jax.ShapeDtypeStruct((peers, packed, 2 * segments), jnp.float32),
-        in_specs=[VMEM, VMEM],
+        in_specs=[SMEM, VMEM, VMEM],
         out_specs=VMEM,
+        scratch_shapes=[pltpu.VMEM((row_count, 128), jnp.float32)],
         compiler_params=grant(16),
         name="sums",
-    )(affinity, columns[:, scales * dim :].astype(jnp.bfloat16))
+    )(starts, affinity, columns[:, scales * dim :].astype(jnp.bfloat16))
     parts = lax.all_to_all(sums, PLANE, 0, 0, tiled=True)
     return pl.pallas_call(
         finish_kernel,

time: 88.3 us -> 87.9 us (level)
  local copies, waits for them, and re-layouts: 0.01 us -> 1.94 us
  blocking collectives: 66.3 us -> 64.7 us
  other arithmetic: 1.29 us -> 0.33 us
    unnamed x2 -> x4, local copies, waits for them, and re-layouts: 0.01 us -> 1.94 us
    all_gather x1, blocking collectives: 51.8 us -> 50.2 us  [shards(): columns = lax.all_gather(item, LINE, axis=0, tiled=True)]
    convert_element_type x1, other arithmetic: 1.25 us -> 0.22 us  [shards(): columns[:, scales * dim:].astype(jnp.bfloat16)]
where the time goes in v8:
time: 87.9 us; the launch traced here: 87.6 us
  blocking collectives  64.7 us (74%)
  starting transfers between devices  7.72 us (9%)
  matrix products  7.06 us (8%)
  Pallas kernels  5.73 us (7%)
  local copies, waits for them, and re-layouts  1.94 us (2%)
    all_gather x1, blocking collectives, shards(): columns = lax.all_gather(item, LINE, axis=0, tiled=True)  50.2 us
    all_to_all x1, blocking collectives, shards(): parts = lax.all_to_all(sums, PLANE, 0, 0, tiled=True)  14.5 us
    all_to_all x1, starting transfers between devices, shards(): rows = lax.all_to_all(row_copies, PLANE, 0, 0, tiled=True)  7.72 us
    dot_general x1, matrix products, shards(): lax.dot_general(rows.reshape(row_count, LANES), columns.astype(jnp.bfloat...  7.06 us
    pallas_call x1, Pallas kernels, shards(): pl.pallas_call(prepare_kernel, out_shape=(jax.ShapeDtypeStruct((peers, se...  2.77 us
    pallas_call x1, Pallas kernels, shards(): pl.pallas_call(lambda *refs: sums_kernel(vecs, segments, *refs), out_shap...  2.26 us
    unnamed x4, local copies, waits for them, and re-layouts  1.94 us
  transfers between devices with their start and end apart: 1, of which 0 were waited for; matrix products, arithmetic and copies ran while one was open for 0% of the time, Pallas kernels for 0%

profile of v8, /device:TPU:1, one launch (start us, length us, event | category | flops | bytes accessed | tf_op | source)
XLA Modules:
  0.0 87.6 jit_solution(14463121828328540672)
XLA Ops:
  0.0 2.8 %prepare.1 = (bf16[16,64,1024]{2,1,0:T(8,128)(2,1)}, bf16[64,1024]{1,0:T(8,128)(2,1)}) custom-call(f32[1,5]{1,0:T(1,128)} %bitcast.15, bf16[5,64,192]{2,1,0:T(8,128)(2,1)} %bitcast.14, bf16[32,64]{1,0:T(8,128)(2,1)} %vectors_hbm.1), custom_call_target="tpu_custom_call" | custom-call | tf_op jit(solution)/shard_map/prepare/pallas_call | solution.py:125
  2.8 0.0 copy-start.1
  2.8 7.7 %all-to-all-start = ((bf16[16,64,1024]{2,1,0:T(8,128)(2,1)}), bf16[16,64,1024]{2,1,0:T(8,128)(2,1)S(1)}, u32[]{:S(2)}, u32[]{:S(2)}) async-start(bf16[16,64,1024]{2,1,0:T(8,128)(2,1)} %get-tuple-element.7), calls=%async_computation | async-start | bytes 4194304 | tf_op jit(solution)/shard_map/all_to_all | solution.py:146
  10.5 0.0 copy-done.1
  10.6 0.1 pad_add_fusion.refs_0_
  10.6 50.2 %all-gather.1 = f16[256,8,1024]{2,1,0:T(8,128)(2,1)S(1)} all-gather(f16[8,8,1024]{2,1,0:T(8,128)(2,1)S(1)} %convert_bitcast_fusion), channel_id=1, replica_groups=mesh['y'=4,'zl'=8,'zh'=2,'x'=4,'core'=2] {'zh','zl','core'}, dimensions={0}, use_global_device_ids=true | all-gather | bytes 4325376 | tf_op jit(solution)/shard_map/all_gather | solution.py:148
  60.9 0.0 copy-start
  60.9 1.9 %copy-done = f16[256,8,1024]{2,1,0:T(8,128)(2,1)} copy-done((f16[256,8,1024]{2,1,0:T(8,128)(2,1)}, f16[256,8,1024]{2,1,0:T(8,128)(2,1)S(1)}, u32[]{:S(2)}) %copy-start) | copy-done | bytes 4194328
  62.8 0.2 slice_convert_fusion.refs_2_
  63.0 0.0 all-to-all-done
  63.0 7.1 %exponential_convert_fusion.refs_1_ = bf16[1024,2048]{1,0:T(8,128)(2,1)S(1)} fusion(bf16[1024,1024]{1,0:T(8,128)(2,1)S(1)} %bitcast.13, f16[256,8,1024]{2,1,0:T(8,128)(2,1)} %copy-done), kind=kOutput, calls=%fused_computation | convolution fusion | flops 4301258752 | bytes 10485760 | tf_op jit(solution)/shard_map/dot_general | solution.py:151
  70.1 2.3 %sums.1 = f32[16,24,128]{2,1,0:T(8,128)S(1)} custom-call(s32[2]{0:T(128)S(1)} %pad_add_fusion.refs_0_, bf16[1024,2048]{1,0:T(8,128)(2,1)S(1)} %exponential_convert_fusion.refs_1_, bf16[2048,64]{1,0:T(8,128)(2,1)S(1)} %slice_convert_fusion.refs_2_), custom_call_target="tpu_custom_call" | custom-call | tf_op jit(solution)/shard_map/sums/pallas_call | solution.py:159
  72.4 14.5 %all_to_all.10.parts_ref = f32[16,24,128]{2,1,0:T(8,128)S(1)} all-to-all(f32[16,24,128]{2,1,0:T(8,128)S(1)} %sums.1), channel_id=1, replica_groups=mesh['y'=4,'zl'=8,'zh'=2,'x'=4,'core'=2] {'y','x'}, dimensions={0} | all-to-all | bytes 393216 | tf_op jit(solution)/shard_map/all_to_all | solution.py:168
  86.9 0.7 finish.1
  (1 shorter events, 0.0 us)
Async XLA Ops:
  2.8 7.7 %copy-start.1 = (bf16[64,1024]{1,0:T(8,128)(2,1)S(1)}, bf16[64,1024]{1,0:T(8,128)(2,1)}, u32[]{:S(2)}) copy-start(bf16[64,1024]{1,0:T(8,128)(2,1)} %get-tuple-element.8) | copy-start | bytes 393220
  2.8 60.3 %all-to-all-start = ((bf16[16,64,1024]{2,1,0:T(8,128)(2,1)}), bf16[16,64,1024]{2,1,0:T(8,128)(2,1)S(1)}, u32[]{:S(2)}, u32[]{:S(2)}) async-start(bf16[16,64,1024]{2,1,0:T(8,128)(2,1)} %get-tuple-element.7), calls=%async_computation | async-start | bytes 4194304 | tf_op jit(solution)/shard_map/all_to_all | solution.py:146
  60.9 1.9 %copy-start = (f16[256,8,1024]{2,1,0:T(8,128)(2,1)}, f16[256,8,1024]{2,1,0:T(8,128)(2,1)S(1)}, u32[]{:S(2)}) copy-start(f16[256,8,1024]{2,1,0:T(8,128)(2,1)S(1)} %all-gather.1) | copy-start | bytes 12582916

commit v9 on v8

--- a/solution.py
+++ b/solution.py
@@ -14,6 +14,7 @@
 LINE = ("zh", "zl", "core")
 LANES = 1024
 PART = 32
+NEAR = 768
 SMEM = pl.BlockSpec(memory_space=pltpu.SMEM)
 VMEM = pl.BlockSpec(memory_space=pltpu.VMEM)
 HBM = pl.BlockSpec(memory_space=pltpu.HBM)
@@ -83,22 +84,33 @@
     keep.wait()
 
 
-def sums_kernel(vecs, width, starts_ref, affinity_ref, tail_ref, out_ref, total_ref):
-    count = tail_ref.shape[0]
+def sums_kernel(vecs, width, starts_ref, near_in, far_in, tail_ref, out_ref, near_ref, far_ref):
     tail = tail_ref[...].astype(jnp.float32)
+    count, lanes = tail_ref.shape[0], 2 * width
+    row_start, column_start = starts_ref[0], starts_ref[1]
+    rows = pl.ds(pl.multiple_of(row_start, width), width)
+
+    def clear_diagonal(part_ref, start, size):
+        @pl.when((column_start >= start) & (column_start < start + size))
+        def _():
+            place = column_start - start
+            base = pl.multiple_of(place // lanes * lanes, lanes)
+            block = part_ref[rows, pl.ds(base, lanes)].astype(jnp.float32)
+            row_place = lax.broadcasted_iota(jnp.int32, block.shape, 0)
+            column_place = lax.broadcasted_iota(jnp.int32, block.shape, 1) + (base - place)
+            kept = jnp.where(row_place == column_place, 0.0, block)
+            part_ref[rows, pl.ds(base, lanes)] = kept.astype(jnp.bfloat16)
+
+    near = near_ref.shape[1]
+    clear_diagonal(near_ref, 0, near)
+    clear_diagonal(far_ref, near, count - near)
     vectors = tail[:, :vecs] * jnp.exp2(tail[:, vecs : 2 * vecs])
     ones = jnp.ones((count, 1), jnp.float32)
     blank = jnp.zeros((count, 127 - vecs), jnp.float32)
     right = jnp.concatenate([vectors, ones, blank], axis=1).astype(jnp.bfloat16)
-    total_ref[...] = jnp.dot(affinity_ref[...], right, preferred_element_type=jnp.float32)
-    own = pl.ds(pl.multiple_of(starts_ref[0], width), width)
-    row_place = lax.broadcasted_iota(jnp.int32, (width, 1), 0)
-    column_place = lax.broadcasted_iota(jnp.int32, (1, count), 1) - starts_ref[1]
-    kept = jnp.where(row_place == column_place, 0.0, affinity_ref[own, :].astype(jnp.float32))
-    total_ref[own, :] = jnp.dot(
-        kept.astype(jnp.bfloat16), right, preferred_element_type=jnp.float32
-    )
-    sums = total_ref[...].T
+    total = jnp.dot(near_ref[...], right[:near], preferred_element_type=jnp.float32)
+    total += jnp.dot(far_ref[...], right[near:], preferred_element_type=jnp.float32)
+    sums = total.T
     half = vecs // 2
     for peer in range(out_ref.shape[0]):
         part = sums[: vecs + 1, peer * width : (peer + 1) * width]
@@ -146,25 +158,37 @@
     rows = lax.all_to_all(row_copies, PLANE, 0, 0, tiled=True)
     item = item.astype(jnp.float16).reshape(segments // 8, 8, LANES)
     columns = lax.all_gather(item, LINE, axis=0, tiled=True)
+    rows, columns = lax.optimization_barrier((rows, columns))
     columns = columns.reshape(-1, LANES)
     row_count = peers * segments
-    cosine = lax.dot_general(
-        rows.reshape(row_count, LANES),
-        columns.astype(jnp.bfloat16),
-        (((1,), (1,)), ((), ())),
-        preferred_element_type=jnp.float32,
-    )
-    affinity = jnp.exp2(cosine * sharpness).astype(jnp.bfloat16)
+    rows = rows.reshape(row_count, LANES)
+
+    def affinity_to(part):
+        cosine = lax.dot_general(
+            rows,
+            part.astype(jnp.bfloat16),
+            (((1,), (1,)), ((), ())),
+            preferred_element_type=jnp.float32,
+        )
+        return jnp.exp2(cosine * sharpness).astype(jnp.bfloat16)
+
+    near = affinity_to(columns[:NEAR])
+    near, late = lax.optimization_barrier((near, columns))
+    far = affinity_to(late[NEAR:])
     starts = jnp.stack([lax.axis_index(PLANE) * segments, lax.axis_index(LINE) * segments])
-    sums = pl.pallas_call(
+    sums, _, _ = pl.pallas_call(
         lambda *refs: sums_kernel(vecs, segments, *refs),
-        out_shape=jax.ShapeDtypeStruct((peers, packed, 2 * segments), jnp.float32),
-        in_specs=[SMEM, VMEM, VMEM],
-        out_specs=VMEM,
-        scratch_shapes=[pltpu.VMEM((row_count, 128), jnp.float32)],
+        out_shape=(
+            jax.ShapeDtypeStruct((peers, packed, 2 * segments), jnp.float32),
+            jax.ShapeDtypeStruct(near.shape, near.dtype),
+            jax.ShapeDtypeStruct(far.shape, far.dtype),
+        ),
+        in_specs=[SMEM, VMEM, VMEM, VMEM],
+        out_specs=(VMEM, VMEM, VMEM),
+        input_output_aliases={1: 1, 2: 2},
         compiler_params=grant(16),
         name="sums",
-    )(starts, affinity, columns[:, scales * dim :].astype(jnp.bfloat16))
+    )(starts, near, far, columns[:, scales * dim :].astype(jnp.bfloat16))
     parts = lax.all_to_all(sums, PLANE, 0, 0, tiled=True)
     return pl.pallas_call(
         finish_kernel,

time: 87.9 us -> 86.8 us (0.987)
  local copies, waits for them, and re-layouts: 1.94 us -> 0.01 us
  blocking collectives: 64.7 us -> 66.3 us
    unnamed x4, local copies, waits for them, and re-layouts: 1.94 us -> 0.01 us
    all_gather x1, blocking collectives: 50.2 us -> 51.8 us  [shards(): columns = lax.all_gather(item, LINE, axis=0, tiled=True)]
    dot_general x1 -> x2, matrix products: 7.06 us -> 6.59 us  [affinity_to(): lax.dot_general(rows, part.astype(jnp.bfloat16), (((1,), (1,)), ((), ()))...]
where the time goes in v9:
time: 86.8 us; the launch traced here: 86.6 us
  blocking collectives  66.3 us (76%)
  starting transfers between devices  7.72 us (9%)
  matrix products  6.59 us (8%)
  Pallas kernels  5.58 us (6%)
    all_gather x1, blocking collectives, shards(): columns = lax.all_gather(item, LINE, axis=0, tiled=True)  51.8 us
    all_to_all x1, blocking collectives, shards(): parts = lax.all_to_all(sums, PLANE, 0, 0, tiled=True)  14.6 us
    all_to_all x1, starting transfers between devices, shards(): rows = lax.all_to_all(row_copies, PLANE, 0, 0, tiled=True)  7.72 us
    dot_general x2, matrix products, affinity_to(): lax.dot_general(rows, part.astype(jnp.bfloat16), (((1,), (1,)), ((), ()))...  6.59 us
    pallas_call x1, Pallas kernels, shards(): pl.pallas_call(prepare_kernel, out_shape=(jax.ShapeDtypeStruct((peers, se...  2.73 us
    pallas_call x1, Pallas kernels, shards(): pl.pallas_call(lambda *refs: sums_kernel(vecs, segments, *refs), out_shap...  2.15 us
  transfers between devices with their start and end apart: 1, of which 0 were waited for; matrix products, arithmetic and copies ran while one was open for 0% of the time, Pallas kernels for 0%

profile of v9, /device:TPU:1, one launch (start us, length us, event | category | flops | bytes accessed | tf_op | source)
XLA Modules:
  0.0 86.6 jit_solution(3897780069665314064)
XLA Ops:
  0.0 2.7 %prepare.1 = (bf16[16,64,1024]{2,1,0:T(8,128)(2,1)}, bf16[64,1024]{1,0:T(8,128)(2,1)}) custom-call(f32[1,5]{1,0:T(1,128)} %bitcast.18, bf16[5,64,192]{2,1,0:T(8,128)(2,1)} %bitcast.17, bf16[32,64]{1,0:T(8,128)(2,1)} %vectors_hbm.1), custom_call_target="tpu_custom_call" | custom-call | tf_op jit(solution)/shard_map/prepare/pallas_call | solution.py:137
  2.7 0.0 copy-start.1
  2.8 7.7 %all-to-all-start = ((bf16[16,64,1024]{2,1,0:T(8,128)(2,1)}), bf16[16,64,1024]{2,1,0:T(8,128)(2,1)S(1)}, u32[]{:S(2)}, u32[]{:S(2)}) async-start(bf16[16,64,1024]{2,1,0:T(8,128)(2,1)} %get-tuple-element.12), calls=%async_computation | async-start | bytes 4194304 | tf_op jit(solution)/shard_map/all_to_all | solution.py:158
  10.5 0.0 copy-done.1
  10.5 0.1 pad_add_fusion.refs_0_
  10.6 51.8 %all-gather.1 = f16[256,8,1024]{2,1,0:T(8,128)(2,1)} all-gather(f16[8,8,1024]{2,1,0:T(8,128)(2,1)S(1)} %convert_bitcast_fusion), channel_id=1, replica_groups=mesh['y'=4,'zl'=8,'zh'=2,'x'=4,'core'=2] {'zh','zl','core'}, dimensions={0}, use_global_device_ids=true | all-gather | bytes 4325376 | tf_op jit(solution)/shard_map/all_gather | solution.py:160
  62.4 0.0 all-to-all-done
  62.4 0.0 copy-start
  62.4 3.4 %exponential_convert_fusion.1.refs_1_ = bf16[1024,768]{1,0:T(8,128)(2,1)S(1)} fusion(bf16[1024,1024]{1,0:T(8,128)(2,1)S(1)} %bitcast.15, f16[256,8,1024]{2,1,0:T(8,128)(2,1)} %all-gather.1), kind=kOutput, calls=%fused_computation.1 | convolution fusion | flops 1612972032 | bytes 5242880 | tf_op jit(solution)/shard_map/dot_general | solution.py:167
  65.8 0.0 copy-done
  65.8 0.2 slice_convert_fusion.refs_3_
  66.0 3.2 %exponential_convert_fusion.refs_2_ = bf16[1024,1280]{1,0:T(8,128)(2,1)S(1)} fusion(bf16[1024,1024]{1,0:T(8,128)(2,1)S(1)} %bitcast.16, f16[2048,1024]{1,0:T(8,128)(2,1)S(1)} %bitcast.14), kind=kOutput, calls=%fused_computation | convolution fusion | flops 2688286720 | bytes 7340032 | tf_op jit(solution)/shard_map/dot_general | solution.py:167
  69.2 2.1 %sums.1 = (f32[16,24,128]{2,1,0:T(8,128)S(1)}, bf16[1024,768]{1,0:T(8,128)(2,1)S(1)}, bf16[1024,1280]{1,0:T(8,128)(2,1)S(1)}) custom-call(s32[2]{0:T(128)S(1)} %pad_add_fusion.refs_0_, bf16[1024,768]{1,0:T(8,128)(2,1)S(1)} %exponential_convert_fusion.1.refs_1_, ...), custom_call_target="tpu_custom_call", output_to_operand_aliasing={{1}: (1, {}), {2}: (2, {})} | custom-call | tf_op jit(solution)/shard_map/sums/pallas_call | solution.py:179
  71.4 14.6 %all_to_all.10.parts_ref = f32[16,24,128]{2,1,0:T(8,128)S(1)} all-to-all(f32[16,24,128]{2,1,0:T(8,128)S(1)} %get-tuple-element.18), channel_id=1, replica_groups=mesh['y'=4,'zl'=8,'zh'=2,'x'=4,'core'=2] {'y','x'}, dimensions={0} | all-to-all | bytes 393216 | tf_op jit(solution)/shard_map/all_to_all | solution.py:192
  85.9 0.7 finish.1
  (1 shorter events, 0.0 us)
Async XLA Ops:
  2.7 7.7 %copy-start.1 = (bf16[64,1024]{1,0:T(8,128)(2,1)S(1)}, bf16[64,1024]{1,0:T(8,128)(2,1)}, u32[]{:S(2)}) copy-start(bf16[64,1024]{1,0:T(8,128)(2,1)} %get-tuple-element.13) | copy-start | bytes 393220
  2.8 59.6 %all-to-all-start = ((bf16[16,64,1024]{2,1,0:T(8,128)(2,1)}), bf16[16,64,1024]{2,1,0:T(8,128)(2,1)S(1)}, u32[]{:S(2)}, u32[]{:S(2)}) async-start(bf16[16,64,1024]{2,1,0:T(8,128)(2,1)} %get-tuple-element.12), calls=%async_computation | async-start | bytes 4194304 | tf_op jit(solution)/shard_map/all_to_all | solution.py:158
  62.4 3.4 %copy-start = (f16[256,8,1024]{2,1,0:T(8,128)(2,1)S(1)}, f16[256,8,1024]{2,1,0:T(8,128)(2,1)}, u32[]{:S(2)}) copy-start(f16[256,8,1024]{2,1,0:T(8,128)(2,1)} %all-gather.1) | copy-start | bytes 12582916

commit v10 on v9

--- a/solution.py
+++ b/solution.py
@@ -14,7 +14,7 @@
 LINE = ("zh", "zl", "core")
 LANES = 1024
 PART = 32
-NEAR = 768
+NEAR = 1024
 SMEM = pl.BlockSpec(memory_space=pltpu.SMEM)
 VMEM = pl.BlockSpec(memory_space=pltpu.VMEM)
 HBM = pl.BlockSpec(memory_space=pltpu.HBM)
@@ -110,10 +110,10 @@
     right = jnp.concatenate([vectors, ones, blank], axis=1).astype(jnp.bfloat16)
     total = jnp.dot(near_ref[...], right[:near], preferred_element_type=jnp.float32)
     total += jnp.dot(far_ref[...], right[near:], preferred_element_type=jnp.float32)
-    sums = total.T
+    sums = total.T[: vecs + 1].astype(jnp.bfloat16)
     half = vecs // 2
     for peer in range(out_ref.shape[0]):
-        part = sums[: vecs + 1, peer * width : (peer + 1) * width]
+        part = sums[:, peer * width : (peer + 1) * width]
         out_ref[peer, :half, :width] = part[:half]
         out_ref[peer, :half, width:] = part[half:vecs]
         out_ref[peer, half : half + 1, :width] = part[vecs:]
@@ -122,7 +122,7 @@
 
 def finish_kernel(parts_ref, out_ref):
     half, width = out_ref.shape[0] // 2, out_ref.shape[1]
-    total = jnp.sum(parts_ref[...], axis=0)
+    total = jnp.sum(parts_ref[...].astype(jnp.float32), axis=0)
     product = total[:half] / total[half : half + 1]
     out_ref[:half] = product[:, :width]
     out_ref[half:] = product[:, width:]
@@ -179,7 +179,7 @@
     sums, _, _ = pl.pallas_call(
         lambda *refs: sums_kernel(vecs, segments, *refs),
         out_shape=(
-            jax.ShapeDtypeStruct((peers, packed, 2 * segments), jnp.float32),
+            jax.ShapeDtypeStruct((peers, packed, 2 * segments), jnp.bfloat16),
             jax.ShapeDtypeStruct(near.shape, near.dtype),
             jax.ShapeDtypeStruct(far.shape, far.dtype),
         ),

time: 86.8 us -> 85.9 us (0.990)
  blocking collectives: 66.3 us -> 65.3 us
    all_to_all x1, blocking collectives: 14.6 us -> 13.6 us  [shards(): parts = lax.all_to_all(sums, PLANE, 0, 0, tiled=True)]
where the time goes in v10:
time: 85.9 us; the launch traced here: 85.7 us
  blocking collectives  65.3 us (76%)
  starting transfers between devices  7.72 us (9%)
  matrix products  6.6 us (8%)
  Pallas kernels  5.61 us (7%)
    all_gather x1, blocking collectives, shards(): columns = lax.all_gather(item, LINE, axis=0, tiled=True)  51.8 us
    all_to_all x1, blocking collectives, shards(): parts = lax.all_to_all(sums, PLANE, 0, 0, tiled=True)  13.6 us
    all_to_all x1, starting transfers between devices, shards(): rows = lax.all_to_all(row_copies, PLANE, 0, 0, tiled=True)  7.72 us
    dot_general x2, matrix products, affinity_to(): lax.dot_general(rows, part.astype(jnp.bfloat16), (((1,), (1,)), ((), ()))...  6.6 us
    pallas_call x1, Pallas kernels, shards(): pl.pallas_call(prepare_kernel, out_shape=(jax.ShapeDtypeStruct((peers, se...  2.73 us
    pallas_call x1, Pallas kernels, shards(): pl.pallas_call(lambda *refs: sums_kernel(vecs, segments, *refs), out_shap...  2.18 us
  transfers between devices with their start and end apart: 1, of which 0 were waited for; matrix products, arithmetic and copies ran while one was open for 0% of the time, Pallas kernels for 0%

profile of v10, /device:TPU:1, one launch (start us, length us, event | category | flops | bytes accessed | tf_op | source)
XLA Modules:
  0.0 85.7 jit_solution(12053497963294842568)
XLA Ops:
  0.0 2.7 %prepare.1 = (bf16[16,64,1024]{2,1,0:T(8,128)(2,1)}, bf16[64,1024]{1,0:T(8,128)(2,1)}) custom-call(f32[1,5]{1,0:T(1,128)} %bitcast.18, bf16[5,64,192]{2,1,0:T(8,128)(2,1)} %bitcast.17, bf16[32,64]{1,0:T(8,128)(2,1)} %vectors_hbm.1), custom_call_target="tpu_custom_call" | custom-call | tf_op jit(solution)/shard_map/prepare/pallas_call | solution.py:137
  2.7 0.0 copy-start.1
  2.8 7.7 %all-to-all-start = ((bf16[16,64,1024]{2,1,0:T(8,128)(2,1)}), bf16[16,64,1024]{2,1,0:T(8,128)(2,1)S(1)}, u32[]{:S(2)}, u32[]{:S(2)}) async-start(bf16[16,64,1024]{2,1,0:T(8,128)(2,1)} %get-tuple-element.12), calls=%async_computation | async-start | bytes 4194304 | tf_op jit(solution)/shard_map/all_to_all | solution.py:158
  10.5 0.0 copy-done.1
  10.5 0.1 pad_add_fusion.refs_0_
  10.6 51.8 %all-gather.1 = f16[256,8,1024]{2,1,0:T(8,128)(2,1)} all-gather(f16[8,8,1024]{2,1,0:T(8,128)(2,1)S(1)} %convert_bitcast_fusion), channel_id=1, replica_groups=mesh['y'=4,'zl'=8,'zh'=2,'x'=4,'core'=2] {'zh','zl','core'}, dimensions={0}, use_global_device_ids=true | all-gather | bytes 4325376 | tf_op jit(solution)/shard_map/all_gather | solution.py:160
  62.4 0.0 all-to-all-done
  62.4 0.0 copy-start
  62.4 4.2 %exponential_convert_fusion.1.refs_1_ = bf16[1024,1024]{1,0:T(8,128)(2,1)S(1)} fusion(bf16[1024,1024]{1,0:T(8,128)(2,1)S(1)} %bitcast.15, f16[256,8,1024]{2,1,0:T(8,128)(2,1)} %all-gather.1), kind=kOutput, calls=%fused_computation.1 | convolution fusion | flops 2150629376 | bytes 6291456 | tf_op jit(solution)/shard_map/dot_general | solution.py:167
  66.5 0.0 copy-done
  66.5 0.2 slice_convert_fusion.refs_3_
  66.8 2.4 %exponential_convert_fusion.refs_2_ = bf16[1024,1024]{1,0:T(8,128)(2,1)S(1)} fusion(bf16[1024,1024]{1,0:T(8,128)(2,1)S(1)} %bitcast.16, f16[2048,1024]{1,0:T(8,128)(2,1)S(1)} %bitcast.14), kind=kOutput, calls=%fused_computation | convolution fusion | flops 2150629376 | bytes 6291456 | tf_op jit(solution)/shard_map/dot_general | solution.py:167
  69.2 2.2 %sums.1 = (bf16[16,24,128]{2,1,0:T(8,128)(2,1)S(1)}, bf16[1024,1024]{1,0:T(8,128)(2,1)S(1)}, bf16[1024,1024]{1,0:T(8,128)(2,1)S(1)}) custom-call(s32[2]{0:T(128)S(1)} %pad_add_fusion.refs_0_, bf16[1024,1024]{1,0:T(8,128)(2,1)S(1)} %exponential_convert_fusion.1.refs_1_, ...), custom_call_target="tpu_custom_call", output_to_operand_aliasing={{1}: (1, {}), {2}: (2, {})} | custom-call | tf_op jit(solution)/shard_map/sums/pallas_call | solution.py:179
  71.4 13.6 %all_to_all.10.parts_ref = bf16[16,24,128]{2,1,0:T(8,128)(2,1)S(1)} all-to-all(bf16[16,24,128]{2,1,0:T(8,128)(2,1)S(1)} %get-tuple-element.18), channel_id=1, replica_groups=mesh['y'=4,'zl'=8,'zh'=2,'x'=4,'core'=2] {'y','x'}, dimensions={0} | all-to-all | bytes 196608 | tf_op jit(solution)/shard_map/all_to_all | solution.py:192
  85.0 0.7 finish.1
  (1 shorter events, 0.0 us)
Async XLA Ops:
  2.7 7.7 %copy-start.1 = (bf16[64,1024]{1,0:T(8,128)(2,1)S(1)}, bf16[64,1024]{1,0:T(8,128)(2,1)}, u32[]{:S(2)}) copy-start(bf16[64,1024]{1,0:T(8,128)(2,1)} %get-tuple-element.13) | copy-start | bytes 393220
  2.8 59.6 %all-to-all-start = ((bf16[16,64,1024]{2,1,0:T(8,128)(2,1)}), bf16[16,64,1024]{2,1,0:T(8,128)(2,1)S(1)}, u32[]{:S(2)}, u32[]{:S(2)}) async-start(bf16[16,64,1024]{2,1,0:T(8,128)(2,1)} %get-tuple-element.12), calls=%async_computation | async-start | bytes 4194304 | tf_op jit(solution)/shard_map/all_to_all | solution.py:158
  62.4 4.2 %copy-start = (f16[256,8,1024]{2,1,0:T(8,128)(2,1)S(1)}, f16[256,8,1024]{2,1,0:T(8,128)(2,1)}, u32[]{:S(2)}) copy-start(f16[256,8,1024]{2,1,0:T(8,128)(2,1)} %all-gather.1) | copy-start | bytes 12582916

commit v11 on v10

--- a/solution.py
+++ b/solution.py
@@ -84,9 +84,16 @@
     keep.wait()
 
 
-def sums_kernel(vecs, width, starts_ref, near_in, far_in, tail_ref, out_ref, near_ref, far_ref):
+def right_kernel(vecs, tail_ref, right_ref):
     tail = tail_ref[...].astype(jnp.float32)
-    count, lanes = tail_ref.shape[0], 2 * width
+    vectors = tail[:, :vecs] * jnp.exp2(tail[:, vecs : 2 * vecs])
+    ones = jnp.ones((tail.shape[0], 1), jnp.float32)
+    blank = jnp.zeros((tail.shape[0], 127 - vecs), jnp.float32)
+    right_ref[...] = jnp.concatenate([vectors, ones, blank], axis=1).astype(jnp.bfloat16)
+
+
+def sums_kernel(vecs, width, starts_ref, near_in, far_in, right_ref, out_ref, near_ref, far_ref):
+    count, lanes = right_ref.shape[0], 2 * width
     row_start, column_start = starts_ref[0], starts_ref[1]
     rows = pl.ds(pl.multiple_of(row_start, width), width)
 
@@ -104,12 +111,8 @@
     near = near_ref.shape[1]
     clear_diagonal(near_ref, 0, near)
     clear_diagonal(far_ref, near, count - near)
-    vectors = tail[:, :vecs] * jnp.exp2(tail[:, vecs : 2 * vecs])
-    ones = jnp.ones((count, 1), jnp.float32)
-    blank = jnp.zeros((count, 127 - vecs), jnp.float32)
-    right = jnp.concatenate([vectors, ones, blank], axis=1).astype(jnp.bfloat16)
-    total = jnp.dot(near_ref[...], right[:near], preferred_element_type=jnp.float32)
-    total += jnp.dot(far_ref[...], right[near:], preferred_element_type=jnp.float32)
+    total = jnp.dot(near_ref[...], right_ref[:near, :], preferred_element_type=jnp.float32)
+    total += jnp.dot(far_ref[...], right_ref[near:, :], preferred_element_type=jnp.float32)
     sums = total.T[: vecs + 1].astype(jnp.bfloat16)
     half = vecs // 2
     for peer in range(out_ref.shape[0]):
@@ -158,10 +161,17 @@
     rows = lax.all_to_all(row_copies, PLANE, 0, 0, tiled=True)
     item = item.astype(jnp.float16).reshape(segments // 8, 8, LANES)
     columns = lax.all_gather(item, LINE, axis=0, tiled=True)
-    rows, columns = lax.optimization_barrier((rows, columns))
     columns = columns.reshape(-1, LANES)
     row_count = peers * segments
     rows = rows.reshape(row_count, LANES)
+    right = pl.pallas_call(
+        lambda *refs: right_kernel(vecs, *refs),
+        out_shape=jax.ShapeDtypeStruct((columns.shape[0], 128), jnp.bfloat16),
+        in_specs=[VMEM],
+        out_specs=VMEM,
+        compiler_params=grant(4),
+        name="right",
+    )(columns[:, scales * dim :].astype(jnp.bfloat16))
 
     def affinity_to(part):
         cosine = lax.dot_general(
@@ -188,7 +198,7 @@
         input_output_aliases={1: 1, 2: 2},
         compiler_params=grant(16),
         name="sums",
-    )(starts, near, far, columns[:, scales * dim :].astype(jnp.bfloat16))
+    )(starts, near, far, right)
     parts = lax.all_to_all(sums, PLANE, 0, 0, tiled=True)
     return pl.pallas_call(
         finish_kernel,

time: 85.9 us -> 86 us (level)
  blocking collectives: 65.3 us -> 63.8 us
  local copies, waits for them, and re-layouts: 0.01 us -> 1.37 us
    all_gather x1, blocking collectives: 51.8 us -> 50.3 us  [shards(): columns = lax.all_gather(item, LINE, axis=0, tiled=True)]
    unnamed x4 -> x6, local copies, waits for them, and re-layouts: 0.01 us -> 1.37 us
where the time goes in v11:
time: 86 us; the launch traced here: 85.8 us
  blocking collectives  63.8 us (74%)
  starting transfers between devices  7.72 us (9%)
  matrix products  6.6 us (8%)
  Pallas kernels  5.85 us (7%)
  local copies, waits for them, and re-layouts  1.37 us (2%)
    all_gather x1, blocking collectives, shards(): columns = lax.all_gather(item, LINE, axis=0, tiled=True)  50.3 us
    all_to_all x1, blocking collectives, shards(): parts = lax.all_to_all(sums, PLANE, 0, 0, tiled=True)  13.5 us
    all_to_all x1, starting transfers between devices, shards(): rows = lax.all_to_all(row_copies, PLANE, 0, 0, tiled=True)  7.72 us
    dot_general x2, matrix products, affinity_to(): lax.dot_general(rows, part.astype(jnp.bfloat16), (((1,), (1,)), ((), ()))...  6.6 us
    pallas_call x1, Pallas kernels, shards(): pl.pallas_call(prepare_kernel, out_shape=(jax.ShapeDtypeStruct((peers, se...  2.77 us
    pallas_call x1, Pallas kernels, shards(): pl.pallas_call(lambda *refs: sums_kernel(vecs, segments, *refs), out_shap...  2.04 us
  transfers between devices with their start and end apart: 1, of which 0 were waited for; matrix products, arithmetic and copies ran while one was open for 0% of the time, Pallas kernels for 0%

profile of v11, /device:TPU:1, one launch (start us, length us, event | category | flops | bytes accessed | tf_op | source)
XLA Modules:
  0.0 85.8 jit_solution(15696946435132398414)
XLA Ops:
  0.0 2.8 %prepare.1 = (bf16[16,64,1024]{2,1,0:T(8,128)(2,1)}, bf16[64,1024]{1,0:T(8,128)(2,1)}) custom-call(f32[1,5]{1,0:T(1,128)} %bitcast.18, bf16[5,64,192]{2,1,0:T(8,128)(2,1)} %bitcast.17, bf16[32,64]{1,0:T(8,128)(2,1)} %vectors_hbm.1), custom_call_target="tpu_custom_call" | custom-call | tf_op jit(solution)/shard_map/prepare/pallas_call | solution.py:140
  2.8 0.0 copy-start.2
  2.8 7.7 %all-to-all-start = ((bf16[16,64,1024]{2,1,0:T(8,128)(2,1)}), bf16[16,64,1024]{2,1,0:T(8,128)(2,1)S(1)}, u32[]{:S(2)}, u32[]{:S(2)}) async-start(bf16[16,64,1024]{2,1,0:T(8,128)(2,1)} %get-tuple-element.10), calls=%async_computation | async-start | bytes 4194304 | tf_op jit(solution)/shard_map/all_to_all | solution.py:161
  10.5 0.0 copy-done.2
  10.6 50.3 %all-gather.1 = f16[256,8,1024]{2,1,0:T(8,128)(2,1)S(1)} all-gather(f16[8,8,1024]{2,1,0:T(8,128)(2,1)S(1)} %convert_bitcast_fusion), channel_id=1, replica_groups=mesh['y'=4,'zl'=8,'zh'=2,'x'=4,'core'=2] {'zh','zl','core'}, dimensions={0}, use_global_device_ids=true | all-gather | bytes 4325376 | tf_op jit(solution)/shard_map/all_gather | solution.py:163
  60.8 0.0 copy-start
  60.8 0.2 slice_convert_fusion.1.refs_0_
  61.1 0.3 right.1.refs_3_
  61.4 1.4 %copy-done = f16[256,8,1024]{2,1,0:T(8,128)(2,1)} copy-done((f16[256,8,1024]{2,1,0:T(8,128)(2,1)}, f16[256,8,1024]{2,1,0:T(8,128)(2,1)S(1)}, u32[]{:S(2)}) %copy-start) | copy-done | bytes 4194328
  62.8 0.1 pad_add_fusion.refs_0_
  62.8 0.0 all-to-all-done
  62.8 0.0 copy-start.1
  62.9 4.2 %exponential_convert_fusion.1.refs_1_ = bf16[1024,1024]{1,0:T(8,128)(2,1)S(1)} fusion(bf16[1024,1024]{1,0:T(8,128)(2,1)S(1)} %bitcast.15, f16[256,8,1024]{2,1,0:T(8,128)(2,1)} %copy-done), kind=kOutput, calls=%fused_computation.1 | convolution fusion | flops 2150629376 | bytes 6291456 | tf_op jit(solution)/shard_map/dot_general | solution.py:177
  67.0 0.0 copy-done.1
  67.0 2.4 %exponential_convert_fusion.refs_2_ = bf16[1024,1024]{1,0:T(8,128)(2,1)S(1)} fusion(bf16[1024,1024]{1,0:T(8,128)(2,1)S(1)} %bitcast.16, f16[2048,1024]{1,0:T(8,128)(2,1)S(1)} %bitcast.14), kind=kOutput, calls=%fused_computation | convolution fusion | flops 2150629376 | bytes 6291456 | tf_op jit(solution)/shard_map/dot_general | solution.py:177
  69.5 2.0 %sums.1 = (bf16[16,24,128]{2,1,0:T(8,128)(2,1)S(1)}, bf16[1024,1024]{1,0:T(8,128)(2,1)S(1)}, bf16[1024,1024]{1,0:T(8,128)(2,1)S(1)}) custom-call(s32[2]{0:T(128)S(1)} %pad_add_fusion.refs_0_, bf16[1024,1024]{1,0:T(8,128)(2,1)S(1)} %exponential_convert_fusion.1.refs_1_, ...), custom_call_target="tpu_custom_call", output_to_operand_aliasing={{1}: (1, {}), {2}: (2, {})} | custom-call | tf_op jit(solution)/shard_map/sums/pallas_call | solution.py:189
  71.5 13.5 %all_to_all.10.parts_ref = bf16[16,24,128]{2,1,0:T(8,128)(2,1)S(1)} all-to-all(bf16[16,24,128]{2,1,0:T(8,128)(2,1)S(1)} %get-tuple-element.14), channel_id=1, replica_groups=mesh['y'=4,'zl'=8,'zh'=2,'x'=4,'core'=2] {'y','x'}, dimensions={0} | all-to-all | bytes 196608 | tf_op jit(solution)/shard_map/all_to_all | solution.py:202
  85.1 0.7 finish.1
  (1 shorter events, 0.0 us)
Async XLA Ops:
  2.8 7.7 %copy-start.2 = (bf16[64,1024]{1,0:T(8,128)(2,1)S(1)}, bf16[64,1024]{1,0:T(8,128)(2,1)}, u32[]{:S(2)}) copy-start(bf16[64,1024]{1,0:T(8,128)(2,1)} %get-tuple-element.11) | copy-start | bytes 393220
  2.8 60.1 %all-to-all-start = ((bf16[16,64,1024]{2,1,0:T(8,128)(2,1)}), bf16[16,64,1024]{2,1,0:T(8,128)(2,1)S(1)}, u32[]{:S(2)}, u32[]{:S(2)}) async-start(bf16[16,64,1024]{2,1,0:T(8,128)(2,1)} %get-tuple-element.10), calls=%async_computation | async-start | bytes 4194304 | tf_op jit(solution)/shard_map/all_to_all | solution.py:161
  60.8 1.9 %copy-start = (f16[256,8,1024]{2,1,0:T(8,128)(2,1)}, f16[256,8,1024]{2,1,0:T(8,128)(2,1)S(1)}, u32[]{:S(2)}) copy-start(f16[256,8,1024]{2,1,0:T(8,128)(2,1)S(1)} %all-gather.1) | copy-start | bytes 12582916
  62.8 4.2 %copy-start.1 = (f16[256,8,1024]{2,1,0:T(8,128)(2,1)S(1)}, f16[256,8,1024]{2,1,0:T(8,128)(2,1)}, u32[]{:S(2)}) copy-start(f16[256,8,1024]{2,1,0:T(8,128)(2,1)} %copy-done) | copy-start | bytes 12582916

commit v12 on v10

--- a/solution.py
+++ b/solution.py
@@ -13,7 +13,7 @@
 PLANE = ("y", "x")
 LINE = ("zh", "zl", "core")
 LANES = 1024
-PART = 32
+PART = 64
 NEAR = 1024
 SMEM = pl.BlockSpec(memory_space=pltpu.SMEM)
 VMEM = pl.BlockSpec(memory_space=pltpu.VMEM)
@@ -84,33 +84,31 @@
     keep.wait()
 
 
-def sums_kernel(vecs, width, starts_ref, near_in, far_in, tail_ref, out_ref, near_ref, far_ref):
+def sums_kernel(vecs, width, starts_ref, near_ref, far_ref, tail_ref, out_ref, total_ref):
     tail = tail_ref[...].astype(jnp.float32)
-    count, lanes = tail_ref.shape[0], 2 * width
-    row_start, column_start = starts_ref[0], starts_ref[1]
-    rows = pl.ds(pl.multiple_of(row_start, width), width)
-
-    def clear_diagonal(part_ref, start, size):
-        @pl.when((column_start >= start) & (column_start < start + size))
-        def _():
-            place = column_start - start
-            base = pl.multiple_of(place // lanes * lanes, lanes)
-            block = part_ref[rows, pl.ds(base, lanes)].astype(jnp.float32)
-            row_place = lax.broadcasted_iota(jnp.int32, block.shape, 0)
-            column_place = lax.broadcasted_iota(jnp.int32, block.shape, 1) + (base - place)
-            kept = jnp.where(row_place == column_place, 0.0, block)
-            part_ref[rows, pl.ds(base, lanes)] = kept.astype(jnp.bfloat16)
-
-    near = near_ref.shape[1]
-    clear_diagonal(near_ref, 0, near)
-    clear_diagonal(far_ref, near, count - near)
+    count, near = tail_ref.shape[0], near_ref.shape[1]
     vectors = tail[:, :vecs] * jnp.exp2(tail[:, vecs : 2 * vecs])
     ones = jnp.ones((count, 1), jnp.float32)
     blank = jnp.zeros((count, 127 - vecs), jnp.float32)
     right = jnp.concatenate([vectors, ones, blank], axis=1).astype(jnp.bfloat16)
-    total = jnp.dot(near_ref[...], right[:near], preferred_element_type=jnp.float32)
-    total += jnp.dot(far_ref[...], right[near:], preferred_element_type=jnp.float32)
-    sums = total.T[: vecs + 1].astype(jnp.bfloat16)
+
+    def product(low, high):
+        total = jnp.dot(low, right[:near], preferred_element_type=jnp.float32)
+        return total + jnp.dot(high, right[near:], preferred_element_type=jnp.float32)
+
+    def without_diagonal(part, start):
+        row_place = lax.broadcasted_iota(jnp.int32, part.shape, 0)
+        column_place = lax.broadcasted_iota(jnp.int32, part.shape, 1) + (start - starts_ref[1])
+        kept = jnp.where(row_place == column_place, 0.0, part.astype(jnp.float32))
+        return kept.astype(jnp.bfloat16)
+
+    own = pl.ds(pl.multiple_of(starts_ref[0], width), width)
+    own_product = product(
+        without_diagonal(near_ref[own, :], 0), without_diagonal(far_ref[own, :], near)
+    )
+    total_ref[...] = product(near_ref[...], far_ref[...])
+    total_ref[own, :] = own_product
+    sums = total_ref[...].T[: vecs + 1].astype(jnp.bfloat16)
     half = vecs // 2
     for peer in range(out_ref.shape[0]):
         part = sums[:, peer * width : (peer + 1) * width]
@@ -176,16 +174,12 @@
     near, late = lax.optimization_barrier((near, columns))
     far = affinity_to(late[NEAR:])
     starts = jnp.stack([lax.axis_index(PLANE) * segments, lax.axis_index(LINE) * segments])
-    sums, _, _ = pl.pallas_call(
+    sums = pl.pallas_call(
         lambda *refs: sums_kernel(vecs, segments, *refs),
-        out_shape=(
-            jax.ShapeDtypeStruct((peers, packed, 2 * segments), jnp.bfloat16),
-            jax.ShapeDtypeStruct(near.shape, near.dtype),
-            jax.ShapeDtypeStruct(far.shape, far.dtype),
-        ),
+        out_shape=jax.ShapeDtypeStruct((peers, packed, 2 * segments), jnp.bfloat16),
         in_specs=[SMEM, VMEM, VMEM, VMEM],
-        out_specs=(VMEM, VMEM, VMEM),
-        input_output_aliases={1: 1, 2: 2},
+        out_specs=VMEM,
+        scratch_shapes=[pltpu.VMEM((row_count, 128), jnp.float32)],
         compiler_params=grant(16),
         name="sums",
     )(starts, near, far, columns[:, scales * dim :].astype(jnp.bfloat16))

time: 85.9 us -> 86.1 us (level)
  no operation moved by 1% of the time
where the time goes in v12:
time: 86.1 us; the launch traced here: 85.9 us
  blocking collectives  65.3 us (76%)
  starting transfers between devices  7.72 us (9%)
  matrix products  6.61 us (8%)
  Pallas kernels  5.8 us (7%)
    all_gather x1, blocking collectives, shards(): columns = lax.all_gather(item, LINE, axis=0, tiled=True)  51.8 us
    all_to_all x1, blocking collectives, shards(): parts = lax.all_to_all(sums, PLANE, 0, 0, tiled=True)  13.5 us
    all_to_all x1, starting transfers between devices, shards(): rows = lax.all_to_all(row_copies, PLANE, 0, 0, tiled=True)  7.72 us
    dot_general x2, matrix products, affinity_to(): lax.dot_general(rows, part.astype(jnp.bfloat16), (((1,), (1,)), ((), ()))...  6.61 us
    pallas_call x1, Pallas kernels, shards(): pl.pallas_call(prepare_kernel, out_shape=(jax.ShapeDtypeStruct((peers, se...  2.68 us
    pallas_call x1, Pallas kernels, shards(): pl.pallas_call(lambda *refs: sums_kernel(vecs, segments, *refs), out_shap...  2.42 us
  transfers between devices with their start and end apart: 1, of which 0 were waited for; matrix products, arithmetic and copies ran while one was open for 0% of the time, Pallas kernels for 0%

profile of v12, /device:TPU:1, one launch (start us, length us, event | category | flops | bytes accessed | tf_op | source)
XLA Modules:
  0.0 85.9 jit_solution(1926763043864626347)
XLA Ops:
  0.0 2.7 %prepare.1 = (bf16[16,64,1024]{2,1,0:T(8,128)(2,1)}, bf16[64,1024]{1,0:T(8,128)(2,1)}) custom-call(f32[1,5]{1,0:T(1,128)} %bitcast.18, bf16[5,64,192]{2,1,0:T(8,128)(2,1)} %bitcast.17, bf16[32,64]{1,0:T(8,128)(2,1)} %vectors_hbm.1), custom_call_target="tpu_custom_call" | custom-call | tf_op jit(solution)/shard_map/prepare/pallas_call | solution.py:135
  2.7 0.0 copy-start.1
  2.7 7.7 %all-to-all-start = ((bf16[16,64,1024]{2,1,0:T(8,128)(2,1)}), bf16[16,64,1024]{2,1,0:T(8,128)(2,1)S(1)}, u32[]{:S(2)}, u32[]{:S(2)}) async-start(bf16[16,64,1024]{2,1,0:T(8,128)(2,1)} %get-tuple-element.11), calls=%async_computation | async-start | bytes 4194304 | tf_op jit(solution)/shard_map/all_to_all | solution.py:156
  10.4 0.0 copy-done.1
  10.5 0.1 pad_add_fusion.refs_0_
  10.6 51.8 %all-gather.1 = f16[256,8,1024]{2,1,0:T(8,128)(2,1)} all-gather(f16[8,8,1024]{2,1,0:T(8,128)(2,1)S(1)} %convert_bitcast_fusion), channel_id=1, replica_groups=mesh['y'=4,'zl'=8,'zh'=2,'x'=4,'core'=2] {'zh','zl','core'}, dimensions={0}, use_global_device_ids=true | all-gather | bytes 4325376 | tf_op jit(solution)/shard_map/all_gather | solution.py:158
  62.3 0.0 all-to-all-done
  62.3 0.0 copy-start
  62.3 4.2 %exponential_convert_fusion.1.refs_1_ = bf16[1024,1024]{1,0:T(8,128)(2,1)S(1)} fusion(bf16[1024,1024]{1,0:T(8,128)(2,1)S(1)} %bitcast.15, f16[256,8,1024]{2,1,0:T(8,128)(2,1)} %all-gather.1), kind=kOutput, calls=%fused_computation.1 | convolution fusion | flops 2150629376 | bytes 6291456 | tf_op jit(solution)/shard_map/dot_general | solution.py:165
  66.5 0.0 copy-done
  66.5 0.2 slice_convert_fusion.refs_3_
  66.7 2.4 %exponential_convert_fusion.refs_2_ = bf16[1024,1024]{1,0:T(8,128)(2,1)S(1)} fusion(bf16[1024,1024]{1,0:T(8,128)(2,1)S(1)} %bitcast.16, f16[2048,1024]{1,0:T(8,128)(2,1)S(1)} %bitcast.14), kind=kOutput, calls=%fused_computation | convolution fusion | flops 2150629376 | bytes 6291456 | tf_op jit(solution)/shard_map/dot_general | solution.py:165
  69.2 2.4 %sums.1 = bf16[16,24,128]{2,1,0:T(8,128)(2,1)S(1)} custom-call(s32[2]{0:T(128)S(1)} %pad_add_fusion.refs_0_, bf16[1024,1024]{1,0:T(8,128)(2,1)S(1)} %exponential_convert_fusion.1.refs_1_, bf16[1024,1024]{1,0:T(8,128)(2,1)S(1)} %exponential_convert_fusion.refs_2_, bf16[2048,64]{1,0:T(8,128)(2,1)S(1)} %slice_convert_fusion.refs_3_), custom_call_target="tpu_custom_call" | custom-call | tf_op jit(solution)/shard_map/sums/pallas_call | solution.py:177
  71.6 13.5 %all_to_all.10.parts_ref = bf16[16,24,128]{2,1,0:T(8,128)(2,1)S(1)} all-to-all(bf16[16,24,128]{2,1,0:T(8,128)(2,1)S(1)} %sums.1), channel_id=1, replica_groups=mesh['y'=4,'zl'=8,'zh'=2,'x'=4,'core'=2] {'y','x'}, dimensions={0} | all-to-all | bytes 196608 | tf_op jit(solution)/shard_map/all_to_all | solution.py:186
  85.2 0.7 finish.1
  (1 shorter events, 0.0 us)
Async XLA Ops:
  2.7 7.7 %copy-start.1 = (bf16[64,1024]{1,0:T(8,128)(2,1)S(1)}, bf16[64,1024]{1,0:T(8,128)(2,1)}, u32[]{:S(2)}) copy-start(bf16[64,1024]{1,0:T(8,128)(2,1)} %get-tuple-element.12) | copy-start | bytes 393220
  2.7 59.6 %all-to-all-start = ((bf16[16,64,1024]{2,1,0:T(8,128)(2,1)}), bf16[16,64,1024]{2,1,0:T(8,128)(2,1)S(1)}, u32[]{:S(2)}, u32[]{:S(2)}) async-start(bf16[16,64,1024]{2,1,0:T(8,128)(2,1)} %get-tuple-element.11), calls=%async_computation | async-start | bytes 4194304 | tf_op jit(solution)/shard_map/all_to_all | solution.py:156
  62.3 4.2 %copy-start = (f16[256,8,1024]{2,1,0:T(8,128)(2,1)S(1)}, f16[256,8,1024]{2,1,0:T(8,128)(2,1)}, u32[]{:S(2)}) copy-start(f16[256,8,1024]{2,1,0:T(8,128)(2,1)} %all-gather.1) | copy-start | bytes 12582916

commit v13 on v12

--- a/solution.py
+++ b/solution.py
@@ -108,7 +108,7 @@
     )
     total_ref[...] = product(near_ref[...], far_ref[...])
     total_ref[own, :] = own_product
-    sums = total_ref[...].T[: vecs + 1].astype(jnp.bfloat16)
+    sums = total_ref[...].T[: vecs + 1]
     half = vecs // 2
     for peer in range(out_ref.shape[0]):
         part = sums[:, peer * width : (peer + 1) * width]
@@ -120,7 +120,7 @@
 
 def finish_kernel(parts_ref, out_ref):
     half, width = out_ref.shape[0] // 2, out_ref.shape[1]
-    total = jnp.sum(parts_ref[...].astype(jnp.float32), axis=0)
+    total = jnp.sum(parts_ref[...], axis=0)
     product = total[:half] / total[half : half + 1]
     out_ref[:half] = product[:, :width]
     out_ref[half:] = product[:, width:]
@@ -176,7 +176,7 @@
     starts = jnp.stack([lax.axis_index(PLANE) * segments, lax.axis_index(LINE) * segments])
     sums = pl.pallas_call(
         lambda *refs: sums_kernel(vecs, segments, *refs),
-        out_shape=jax.ShapeDtypeStruct((peers, packed, 2 * segments), jnp.bfloat16),
+        out_shape=jax.ShapeDtypeStruct((peers, packed, 2 * segments), jnp.float32),
         in_specs=[SMEM, VMEM, VMEM, VMEM],
         out_specs=VMEM,
         scratch_shapes=[pltpu.VMEM((row_count, 128), jnp.float32)],

time: 86.1 us -> 87.1 us (1.012)
  blocking collectives: 65.3 us -> 66.3 us
    all_to_all x1, blocking collectives: 13.5 us -> 14.5 us  [shards(): parts = lax.all_to_all(sums, PLANE, 0, 0, tiled=True)]
where the time goes in v13:
time: 87.1 us; the launch traced here: 86.9 us
  blocking collectives  66.3 us (76%)
  starting transfers between devices  7.72 us (9%)
  matrix products  6.61 us (8%)
  Pallas kernels  5.86 us (7%)
    all_gather x1, blocking collectives, shards(): columns = lax.all_gather(item, LINE, axis=0, tiled=True)  51.8 us
    all_to_all x1, blocking collectives, shards(): parts = lax.all_to_all(sums, PLANE, 0, 0, tiled=True)  14.5 us
    all_to_all x1, starting transfers between devices, shards(): rows = lax.all_to_all(row_copies, PLANE, 0, 0, tiled=True)  7.72 us
    dot_general x2, matrix products, affinity_to(): lax.dot_general(rows, part.astype(jnp.bfloat16), (((1,), (1,)), ((), ()))...  6.61 us
    pallas_call x1, Pallas kernels, shards(): pl.pallas_call(prepare_kernel, out_shape=(jax.ShapeDtypeStruct((peers, se...  2.68 us
    pallas_call x1, Pallas kernels, shards(): pl.pallas_call(lambda *refs: sums_kernel(vecs, segments, *refs), out_shap...  2.48 us
  transfers between devices with their start and end apart: 1, of which 0 were waited for; matrix products, arithmetic and copies ran while one was open for 0% of the time, Pallas kernels for 0%

profile of v13, /device:TPU:1, one launch (start us, length us, event | category | flops | bytes accessed | tf_op | source)
XLA Modules:
  0.0 86.9 jit_solution(10121500792888736041)
XLA Ops:
  0.0 2.7 %prepare.1 = (bf16[16,64,1024]{2,1,0:T(8,128)(2,1)}, bf16[64,1024]{1,0:T(8,128)(2,1)}) custom-call(f32[1,5]{1,0:T(1,128)} %bitcast.18, bf16[5,64,192]{2,1,0:T(8,128)(2,1)} %bitcast.17, bf16[32,64]{1,0:T(8,128)(2,1)} %vectors_hbm.1), custom_call_target="tpu_custom_call" | custom-call | tf_op jit(solution)/shard_map/prepare/pallas_call | solution.py:135
  2.7 0.0 copy-start.1
  2.7 7.7 %all-to-all-start = ((bf16[16,64,1024]{2,1,0:T(8,128)(2,1)}), bf16[16,64,1024]{2,1,0:T(8,128)(2,1)S(1)}, u32[]{:S(2)}, u32[]{:S(2)}) async-start(bf16[16,64,1024]{2,1,0:T(8,128)(2,1)} %get-tuple-element.11), calls=%async_computation | async-start | bytes 4194304 | tf_op jit(solution)/shard_map/all_to_all | solution.py:156
  10.4 0.0 copy-done.1
  10.5 0.1 pad_add_fusion.refs_0_
  10.6 51.8 %all-gather.1 = f16[256,8,1024]{2,1,0:T(8,128)(2,1)} all-gather(f16[8,8,1024]{2,1,0:T(8,128)(2,1)S(1)} %convert_bitcast_fusion), channel_id=1, replica_groups=mesh['y'=4,'zl'=8,'zh'=2,'x'=4,'core'=2] {'zh','zl','core'}, dimensions={0}, use_global_device_ids=true | all-gather | bytes 4325376 | tf_op jit(solution)/shard_map/all_gather | solution.py:158
  62.3 0.0 all-to-all-done
  62.3 0.0 copy-start
  62.3 4.2 %exponential_convert_fusion.1.refs_1_ = bf16[1024,1024]{1,0:T(8,128)(2,1)S(1)} fusion(bf16[1024,1024]{1,0:T(8,128)(2,1)S(1)} %bitcast.15, f16[256,8,1024]{2,1,0:T(8,128)(2,1)} %all-gather.1), kind=kOutput, calls=%fused_computation.1 | convolution fusion | flops 2150629376 | bytes 6291456 | tf_op jit(solution)/shard_map/dot_general | solution.py:165
  66.5 0.0 copy-done
  66.5 0.2 slice_convert_fusion.refs_3_
  66.7 2.4 %exponential_convert_fusion.refs_2_ = bf16[1024,1024]{1,0:T(8,128)(2,1)S(1)} fusion(bf16[1024,1024]{1,0:T(8,128)(2,1)S(1)} %bitcast.16, f16[2048,1024]{1,0:T(8,128)(2,1)S(1)} %bitcast.14), kind=kOutput, calls=%fused_computation | convolution fusion | flops 2150629376 | bytes 6291456 | tf_op jit(solution)/shard_map/dot_general | solution.py:165
  69.2 2.5 %sums.1 = f32[16,24,128]{2,1,0:T(8,128)S(1)} custom-call(s32[2]{0:T(128)S(1)} %pad_add_fusion.refs_0_, bf16[1024,1024]{1,0:T(8,128)(2,1)S(1)} %exponential_convert_fusion.1.refs_1_, bf16[1024,1024]{1,0:T(8,128)(2,1)S(1)} %exponential_convert_fusion.refs_2_, bf16[2048,64]{1,0:T(8,128)(2,1)S(1)} %slice_convert_fusion.refs_3_), custom_call_target="tpu_custom_call" | custom-call | tf_op jit(solution)/shard_map/sums/pallas_call | solution.py:177
  71.7 14.5 %all_to_all.10.parts_ref = f32[16,24,128]{2,1,0:T(8,128)S(1)} all-to-all(f32[16,24,128]{2,1,0:T(8,128)S(1)} %sums.1), channel_id=1, replica_groups=mesh['y'=4,'zl'=8,'zh'=2,'x'=4,'core'=2] {'y','x'}, dimensions={0} | all-to-all | bytes 393216 | tf_op jit(solution)/shard_map/all_to_all | solution.py:186
  86.2 0.7 finish.1
  (1 shorter events, 0.0 us)
Async XLA Ops:
  2.7 7.7 %copy-start.1 = (bf16[64,1024]{1,0:T(8,128)(2,1)S(1)}, bf16[64,1024]{1,0:T(8,128)(2,1)}, u32[]{:S(2)}) copy-start(bf16[64,1024]{1,0:T(8,128)(2,1)} %get-tuple-element.12) | copy-start | bytes 393220
  2.7 59.6 %all-to-all-start = ((bf16[16,64,1024]{2,1,0:T(8,128)(2,1)}), bf16[16,64,1024]{2,1,0:T(8,128)(2,1)S(1)}, u32[]{:S(2)}, u32[]{:S(2)}) async-start(bf16[16,64,1024]{2,1,0:T(8,128)(2,1)} %get-tuple-element.11), calls=%async_computation | async-start | bytes 4194304 | tf_op jit(solution)/shard_map/all_to_all | solution.py:156
  62.3 4.2 %copy-start = (f16[256,8,1024]{2,1,0:T(8,128)(2,1)S(1)}, f16[256,8,1024]{2,1,0:T(8,128)(2,1)}, u32[]{:S(2)}) copy-start(f16[256,8,1024]{2,1,0:T(8,128)(2,1)} %all-gather.1) | copy-start | bytes 12582916

commit v14 on v13

--- a/solution.py
+++ b/solution.py
@@ -84,7 +84,7 @@
     keep.wait()
 
 
-def sums_kernel(vecs, width, starts_ref, near_ref, far_ref, tail_ref, out_ref, total_ref):
+def sums_kernel(vecs, width, starts_ref, near_ref, far_ref, tail_ref, out_ref):
     tail = tail_ref[...].astype(jnp.float32)
     count, near = tail_ref.shape[0], near_ref.shape[1]
     vectors = tail[:, :vecs] * jnp.exp2(tail[:, vecs : 2 * vecs])
@@ -103,12 +103,14 @@
         return kept.astype(jnp.bfloat16)
 
     own = pl.ds(pl.multiple_of(starts_ref[0], width), width)
+    total = product(near_ref[...], far_ref[...])
     own_product = product(
         without_diagonal(near_ref[own, :], 0), without_diagonal(far_ref[own, :], near)
     )
-    total_ref[...] = product(near_ref[...], far_ref[...])
-    total_ref[own, :] = own_product
-    sums = total_ref[...].T[: vecs + 1]
+    place = lax.broadcasted_iota(jnp.int32, (total.shape[0], 1), 0) - starts_ref[0]
+    is_own = (place >= 0) & (place < width)
+    copies = jnp.concatenate([own_product] * (total.shape[0] // width), axis=0)
+    sums = jnp.where(is_own, copies, total).T[: vecs + 1]
     half = vecs // 2
     for peer in range(out_ref.shape[0]):
         part = sums[:, peer * width : (peer + 1) * width]
@@ -179,7 +181,6 @@
         out_shape=jax.ShapeDtypeStruct((peers, packed, 2 * segments), jnp.float32),
         in_specs=[SMEM, VMEM, VMEM, VMEM],
         out_specs=VMEM,
-        scratch_shapes=[pltpu.VMEM((row_count, 128), jnp.float32)],
         compiler_params=grant(16),
         name="sums",
     )(starts, near, far, columns[:, scales * dim :].astype(jnp.bfloat16))

time: 87.1 us -> 86.9 us (level)
  no operation moved by 1% of the time
where the time goes in v14:
time: 86.9 us; the launch traced here: 86.7 us
  blocking collectives  66.3 us (76%)
  starting transfers between devices  7.72 us (9%)
  matrix products  6.61 us (8%)
  Pallas kernels  5.61 us (6%)
    all_gather x1, blocking collectives, shards(): columns = lax.all_gather(item, LINE, axis=0, tiled=True)  51.8 us
    all_to_all x1, blocking collectives, shards(): parts = lax.all_to_all(sums, PLANE, 0, 0, tiled=True)  14.5 us
    all_to_all x1, starting transfers between devices, shards(): rows = lax.all_to_all(row_copies, PLANE, 0, 0, tiled=True)  7.72 us
    dot_general x2, matrix products, affinity_to(): lax.dot_general(rows, part.astype(jnp.bfloat16), (((1,), (1,)), ((), ()))...  6.61 us
    pallas_call x1, Pallas kernels, shards(): pl.pallas_call(prepare_kernel, out_shape=(jax.ShapeDtypeStruct((peers, se...  2.68 us
    pallas_call x1, Pallas kernels, shards(): pl.pallas_call(lambda *refs: sums_kernel(vecs, segments, *refs), out_shap...  2.23 us
  transfers between devices with their start and end apart: 1, of which 0 were waited for; matrix products, arithmetic and copies ran while one was open for 0% of the time, Pallas kernels for 0%

profile of v14, /device:TPU:1, one launch (start us, length us, event | category | flops | bytes accessed | tf_op | source)
XLA Modules:
  0.0 86.7 jit_solution(18207873391081801821)
XLA Ops:
  0.0 2.7 %prepare.1 = (bf16[16,64,1024]{2,1,0:T(8,128)(2,1)}, bf16[64,1024]{1,0:T(8,128)(2,1)}) custom-call(f32[1,5]{1,0:T(1,128)} %bitcast.18, bf16[5,64,192]{2,1,0:T(8,128)(2,1)} %bitcast.17, bf16[32,64]{1,0:T(8,128)(2,1)} %vectors_hbm.1), custom_call_target="tpu_custom_call" | custom-call | tf_op jit(solution)/shard_map/prepare/pallas_call | solution.py:137
  2.7 0.0 copy-start.1
  2.7 7.7 %all-to-all-start = ((bf16[16,64,1024]{2,1,0:T(8,128)(2,1)}), bf16[16,64,1024]{2,1,0:T(8,128)(2,1)S(1)}, u32[]{:S(2)}, u32[]{:S(2)}) async-start(bf16[16,64,1024]{2,1,0:T(8,128)(2,1)} %get-tuple-element.11), calls=%async_computation | async-start | bytes 4194304 | tf_op jit(solution)/shard_map/all_to_all | solution.py:158
  10.4 0.0 copy-done.1
  10.5 0.1 pad_add_fusion.refs_0_
  10.6 51.8 %all-gather.1 = f16[256,8,1024]{2,1,0:T(8,128)(2,1)} all-gather(f16[8,8,1024]{2,1,0:T(8,128)(2,1)S(1)} %convert_bitcast_fusion), channel_id=1, replica_groups=mesh['y'=4,'zl'=8,'zh'=2,'x'=4,'core'=2] {'zh','zl','core'}, dimensions={0}, use_global_device_ids=true | all-gather | bytes 4325376 | tf_op jit(solution)/shard_map/all_gather | solution.py:160
  62.3 0.0 all-to-all-done
  62.3 0.0 copy-start
  62.3 4.2 %exponential_convert_fusion.1.refs_1_ = bf16[1024,1024]{1,0:T(8,128)(2,1)S(1)} fusion(bf16[1024,1024]{1,0:T(8,128)(2,1)S(1)} %bitcast.15, f16[256,8,1024]{2,1,0:T(8,128)(2,1)} %all-gather.1), kind=kOutput, calls=%fused_computation.1 | convolution fusion | flops 2150629376 | bytes 6291456 | tf_op jit(solution)/shard_map/dot_general | solution.py:167
  66.5 0.0 copy-done
  66.5 0.2 slice_convert_fusion.refs_3_
  66.7 2.4 %exponential_convert_fusion.refs_2_ = bf16[1024,1024]{1,0:T(8,128)(2,1)S(1)} fusion(bf16[1024,1024]{1,0:T(8,128)(2,1)S(1)} %bitcast.16, f16[2048,1024]{1,0:T(8,128)(2,1)S(1)} %bitcast.14), kind=kOutput, calls=%fused_computation | convolution fusion | flops 2150629376 | bytes 6291456 | tf_op jit(solution)/shard_map/dot_general | solution.py:167
  69.2 2.2 %sums.1 = f32[16,24,128]{2,1,0:T(8,128)S(1)} custom-call(s32[2]{0:T(128)S(1)} %pad_add_fusion.refs_0_, bf16[1024,1024]{1,0:T(8,128)(2,1)S(1)} %exponential_convert_fusion.1.refs_1_, bf16[1024,1024]{1,0:T(8,128)(2,1)S(1)} %exponential_convert_fusion.refs_2_, bf16[2048,64]{1,0:T(8,128)(2,1)S(1)} %slice_convert_fusion.refs_3_), custom_call_target="tpu_custom_call" | custom-call | tf_op jit(solution)/shard_map/sums/pallas_call | solution.py:179
  71.4 14.5 %all_to_all.10.parts_ref = f32[16,24,128]{2,1,0:T(8,128)S(1)} all-to-all(f32[16,24,128]{2,1,0:T(8,128)S(1)} %sums.1), channel_id=1, replica_groups=mesh['y'=4,'zl'=8,'zh'=2,'x'=4,'core'=2] {'y','x'}, dimensions={0} | all-to-all | bytes 393216 | tf_op jit(solution)/shard_map/all_to_all | solution.py:187
  86.0 0.7 finish.1
  (1 shorter events, 0.0 us)
Async XLA Ops:
  2.7 7.7 %copy-start.1 = (bf16[64,1024]{1,0:T(8,128)(2,1)S(1)}, bf16[64,1024]{1,0:T(8,128)(2,1)}, u32[]{:S(2)}) copy-start(bf16[64,1024]{1,0:T(8,128)(2,1)} %get-tuple-element.12) | copy-start | bytes 393220
  2.7 59.6 %all-to-all-start = ((bf16[16,64,1024]{2,1,0:T(8,128)(2,1)}), bf16[16,64,1024]{2,1,0:T(8,128)(2,1)S(1)}, u32[]{:S(2)}, u32[]{:S(2)}) async-start(bf16[16,64,1024]{2,1,0:T(8,128)(2,1)} %get-tuple-element.11), calls=%async_computation | async-start | bytes 4194304 | tf_op jit(solution)/shard_map/all_to_all | solution.py:158
  62.3 4.2 %copy-start = (f16[256,8,1024]{2,1,0:T(8,128)(2,1)S(1)}, f16[256,8,1024]{2,1,0:T(8,128)(2,1)}, u32[]{:S(2)}) copy-start(f16[256,8,1024]{2,1,0:T(8,128)(2,1)} %all-gather.1) | copy-start | bytes 12582916

commit v15 on v14

--- a/solution.py
+++ b/solution.py
@@ -14,7 +14,7 @@
 LINE = ("zh", "zl", "core")
 LANES = 1024
 PART = 64
-NEAR = 1024
+NEAR = 384
 SMEM = pl.BlockSpec(memory_space=pltpu.SMEM)
 VMEM = pl.BlockSpec(memory_space=pltpu.VMEM)
 HBM = pl.BlockSpec(memory_space=pltpu.HBM)
@@ -84,17 +84,20 @@
     keep.wait()
 
 
-def sums_kernel(vecs, width, starts_ref, near_ref, far_ref, tail_ref, out_ref):
+def right_kernel(vecs, tail_ref, right_ref):
     tail = tail_ref[...].astype(jnp.float32)
-    count, near = tail_ref.shape[0], near_ref.shape[1]
     vectors = tail[:, :vecs] * jnp.exp2(tail[:, vecs : 2 * vecs])
-    ones = jnp.ones((count, 1), jnp.float32)
-    blank = jnp.zeros((count, 127 - vecs), jnp.float32)
-    right = jnp.concatenate([vectors, ones, blank], axis=1).astype(jnp.bfloat16)
+    ones = jnp.ones((tail.shape[0], 1), jnp.float32)
+    blank = jnp.zeros((tail.shape[0], 127 - vecs), jnp.float32)
+    right_ref[...] = jnp.concatenate([vectors, ones, blank], axis=1).astype(jnp.bfloat16)
+
+
+def sums_kernel(vecs, width, starts_ref, near_ref, far_ref, right_ref, out_ref):
+    near = near_ref.shape[1]
 
     def product(low, high):
-        total = jnp.dot(low, right[:near], preferred_element_type=jnp.float32)
-        return total + jnp.dot(high, right[near:], preferred_element_type=jnp.float32)
+        total = jnp.dot(low, right_ref[:near, :], preferred_element_type=jnp.float32)
+        return total + jnp.dot(high, right_ref[near:, :], preferred_element_type=jnp.float32)
 
     def without_diagonal(part, start):
         row_place = lax.broadcasted_iota(jnp.int32, part.shape, 0)
@@ -158,10 +161,17 @@
     rows = lax.all_to_all(row_copies, PLANE, 0, 0, tiled=True)
     item = item.astype(jnp.float16).reshape(segments // 8, 8, LANES)
     columns = lax.all_gather(item, LINE, axis=0, tiled=True)
-    rows, columns = lax.optimization_barrier((rows, columns))
     columns = columns.reshape(-1, LANES)
     row_count = peers * segments
     rows = rows.reshape(row_count, LANES)
+    right = pl.pallas_call(
+        lambda *refs: right_kernel(vecs, *refs),
+        out_shape=jax.ShapeDtypeStruct((columns.shape[0], 128), jnp.bfloat16),
+        in_specs=[VMEM],
+        out_specs=VMEM,
+        compiler_params=grant(4),
+        name="right",
+    )(columns[:, scales * dim :].astype(jnp.bfloat16))
 
     def affinity_to(part):
         cosine = lax.dot_general(
@@ -172,7 +182,8 @@
         )
         return jnp.exp2(cosine * sharpness).astype(jnp.bfloat16)
 
-    near = affinity_to(columns[:NEAR])
+    first = lax.optimization_barrier(columns[:NEAR].astype(jnp.bfloat16))
+    near = affinity_to(first)
     near, late = lax.optimization_barrier((near, columns))
     far = affinity_to(late[NEAR:])
     starts = jnp.stack([lax.axis_index(PLANE) * segments, lax.axis_index(LINE) * segments])
@@ -183,7 +194,7 @@
         out_specs=VMEM,
         compiler_params=grant(16),
         name="sums",
-    )(starts, near, far, columns[:, scales * dim :].astype(jnp.bfloat16))
+    )(starts, near, far, right)
     parts = lax.all_to_all(sums, PLANE, 0, 0, tiled=True)
     return pl.pallas_call(
         finish_kernel,

time: 86.9 us -> 86.9 us (level)
  local copies, waits for them, and re-layouts: 0.01 us -> 2.15 us
  blocking collectives: 66.3 us -> 64.8 us
  matrix products: 6.61 us -> 5.63 us
    unnamed x4 -> x6, local copies, waits for them, and re-layouts: 0.01 us -> 2.15 us
    all_gather x1, blocking collectives: 51.8 us -> 50.3 us  [shards(): columns = lax.all_gather(item, LINE, axis=0, tiled=True)]
    dot_general x2, matrix products: 6.61 us -> 5.63 us  [affinity_to(): lax.dot_general(rows, part.astype(jnp.bfloat16), (((1,), (1,)), ((), ()))...]
where the time goes in v15:
time: 86.9 us; the launch traced here: 86.7 us
  blocking collectives  64.8 us (75%)
  starting transfers between devices  7.72 us (9%)
  Pallas kernels  5.86 us (7%)
  matrix products  5.63 us (6%)
  local copies, waits for them, and re-layouts  2.15 us (2%)
    all_gather x1, blocking collectives, shards(): columns = lax.all_gather(item, LINE, axis=0, tiled=True)  50.3 us
    all_to_all x1, blocking collectives, shards(): parts = lax.all_to_all(sums, PLANE, 0, 0, tiled=True)  14.5 us
    all_to_all x1, starting transfers between devices, shards(): rows = lax.all_to_all(row_copies, PLANE, 0, 0, tiled=True)  7.72 us
    dot_general x2, matrix products, affinity_to(): lax.dot_general(rows, part.astype(jnp.bfloat16), (((1,), (1,)), ((), ()))...  5.63 us
    pallas_call x1, Pallas kernels, shards(): pl.pallas_call(prepare_kernel, out_shape=(jax.ShapeDtypeStruct((peers, se...  2.66 us
    pallas_call x1, Pallas kernels, shards(): pl.pallas_call(lambda *refs: sums_kernel(vecs, segments, *refs), out_shap...  2.16 us
    unnamed x6, local copies, waits for them, and re-layouts  2.15 us
  transfers between devices with their start and end apart: 1, of which 0 were waited for; matrix products, arithmetic and copies ran while one was open for 0% of the time, Pallas kernels for 0%

profile of v15, /device:TPU:1, one launch (start us, length us, event | category | flops | bytes accessed | tf_op | source)
XLA Modules:
  0.0 86.7 jit_solution(6876368077259975453)
XLA Ops:
  0.0 2.7 %prepare.1 = (bf16[16,64,1024]{2,1,0:T(8,128)(2,1)}, bf16[64,1024]{1,0:T(8,128)(2,1)}) custom-call(f32[1,5]{1,0:T(1,128)} %bitcast.18, bf16[5,64,192]{2,1,0:T(8,128)(2,1)} %bitcast.17, bf16[32,64]{1,0:T(8,128)(2,1)} %vectors_hbm.1), custom_call_target="tpu_custom_call" | custom-call | tf_op jit(solution)/shard_map/prepare/pallas_call | solution.py:140
  2.7 0.0 copy-start.2
  2.7 7.7 %all-to-all-start = ((bf16[16,64,1024]{2,1,0:T(8,128)(2,1)}), bf16[16,64,1024]{2,1,0:T(8,128)(2,1)S(1)}, u32[]{:S(2)}, u32[]{:S(2)}) async-start(bf16[16,64,1024]{2,1,0:T(8,128)(2,1)} %get-tuple-element.9), calls=%async_computation | async-start | bytes 4194304 | tf_op jit(solution)/shard_map/all_to_all | solution.py:161
  10.4 0.0 copy-done.2
  10.5 50.3 %all-gather.1 = f16[256,8,1024]{2,1,0:T(8,128)(2,1)S(1)} all-gather(f16[8,8,1024]{2,1,0:T(8,128)(2,1)S(1)} %convert_bitcast_fusion), channel_id=1, replica_groups=mesh['y'=4,'zl'=8,'zh'=2,'x'=4,'core'=2] {'zh','zl','core'}, dimensions={0}, use_global_device_ids=true | all-gather | bytes 4325376 | tf_op jit(solution)/shard_map/all_gather | solution.py:163
  60.7 0.0 copy-start
  60.7 0.1 fusion.2
  60.8 0.2 slice_convert_fusion.1.refs_0_
  61.1 0.3 right.1.refs_3_
  61.4 1.2 %copy-done = f16[256,8,1024]{2,1,0:T(8,128)(2,1)} copy-done((f16[256,8,1024]{2,1,0:T(8,128)(2,1)}, f16[256,8,1024]{2,1,0:T(8,128)(2,1)S(1)}, u32[]{:S(2)}) %copy-start) | copy-done | bytes 4194328
  62.6 0.1 pad_add_fusion.refs_0_
  62.7 0.0 all-to-all-done
  62.7 0.0 copy-start.1
  62.7 1.3 %exponential_convert_fusion.1.refs_1_ = bf16[1024,384]{1,0:T(8,128)(2,1)S(1)} fusion(bf16[1024,1024]{1,0:T(8,128)(2,1)S(1)} %bitcast.15, bf16[384,1024]{1,0:T(8,128)(2,1)S(1)} %fusion.2), kind=kOutput, calls=%fused_computation.3 | convolution fusion | flops 806092800 | bytes 3670016 | tf_op jit(solution)/shard_map/dot_general | solution.py:177
  64.0 0.9 %copy-done.1 = f16[256,8,1024]{2,1,0:T(8,128)(2,1)S(1)} copy-done((f16[256,8,1024]{2,1,0:T(8,128)(2,1)S(1)}, f16[256,8,1024]{2,1,0:T(8,128)(2,1)}, u32[]{:S(2)}) %copy-start.1) | copy-done | bytes 4194328
  64.9 4.4 %exponential_convert_fusion.refs_2_ = bf16[1024,1664]{1,0:T(8,128)(2,1)S(1)} fusion(bf16[1024,1024]{1,0:T(8,128)(2,1)S(1)} %bitcast.16, f16[2048,1024]{1,0:T(8,128)(2,1)S(1)} %bitcast.14), kind=kOutput, calls=%fused_computation | convolution fusion | flops 3494772736 | bytes 8912896 | tf_op jit(solution)/shard_map/dot_general | solution.py:177
  69.3 2.2 %sums.1 = f32[16,24,128]{2,1,0:T(8,128)S(1)} custom-call(s32[2]{0:T(128)S(1)} %pad_add_fusion.refs_0_, bf16[1024,384]{1,0:T(8,128)(2,1)S(1)} %exponential_convert_fusion.1.refs_1_, bf16[1024,1664]{1,0:T(8,128)(2,1)S(1)} %exponential_convert_fusion.refs_2_, bf16[2048,128]{1,0:T(8,128)(2,1)S(1)} %right.1.refs_3_), custom_call_target="tpu_custom_call" | custom-call | tf_op jit(solution)/shard_map/sums/pallas_call | solution.py:190
  71.4 14.5 %all_to_all.10.parts_ref = f32[16,24,128]{2,1,0:T(8,128)S(1)} all-to-all(f32[16,24,128]{2,1,0:T(8,128)S(1)} %sums.1), channel_id=1, replica_groups=mesh['y'=4,'zl'=8,'zh'=2,'x'=4,'core'=2] {'y','x'}, dimensions={0} | all-to-all | bytes 393216 | tf_op jit(solution)/shard_map/all_to_all | solution.py:198
  86.0 0.7 finish.1
  (1 shorter events, 0.0 us)
Async XLA Ops:
  2.7 7.7 %copy-start.2 = (bf16[64,1024]{1,0:T(8,128)(2,1)S(1)}, bf16[64,1024]{1,0:T(8,128)(2,1)}, u32[]{:S(2)}) copy-start(bf16[64,1024]{1,0:T(8,128)(2,1)} %get-tuple-element.10) | copy-start | bytes 393220
  2.7 60.0 %all-to-all-start = ((bf16[16,64,1024]{2,1,0:T(8,128)(2,1)}), bf16[16,64,1024]{2,1,0:T(8,128)(2,1)S(1)}, u32[]{:S(2)}, u32[]{:S(2)}) async-start(bf16[16,64,1024]{2,1,0:T(8,128)(2,1)} %get-tuple-element.9), calls=%async_computation | async-start | bytes 4194304 | tf_op jit(solution)/shard_map/all_to_all | solution.py:161
  60.7 1.9 %copy-start = (f16[256,8,1024]{2,1,0:T(8,128)(2,1)}, f16[256,8,1024]{2,1,0:T(8,128)(2,1)S(1)}, u32[]{:S(2)}) copy-start(f16[256,8,1024]{2,1,0:T(8,128)(2,1)S(1)} %all-gather.1) | copy-start | bytes 12582916
  62.7 2.2 %copy-start.1 = (f16[256,8,1024]{2,1,0:T(8,128)(2,1)S(1)}, f16[256,8,1024]{2,1,0:T(8,128)(2,1)}, u32[]{:S(2)}) copy-start(f16[256,8,1024]{2,1,0:T(8,128)(2,1)} %copy-done) | copy-start | bytes 12582916

commit v16 on v15

--- a/solution.py
+++ b/solution.py
@@ -92,28 +92,27 @@
     right_ref[...] = jnp.concatenate([vectors, ones, blank], axis=1).astype(jnp.bfloat16)
 
 
-def sums_kernel(vecs, width, starts_ref, near_ref, far_ref, right_ref, out_ref):
-    near = near_ref.shape[1]
-
-    def product(low, high):
-        total = jnp.dot(low, right_ref[:near, :], preferred_element_type=jnp.float32)
-        return total + jnp.dot(high, right_ref[near:, :], preferred_element_type=jnp.float32)
-
-    def without_diagonal(part, start):
-        row_place = lax.broadcasted_iota(jnp.int32, part.shape, 0)
-        column_place = lax.broadcasted_iota(jnp.int32, part.shape, 1) + (start - starts_ref[1])
-        kept = jnp.where(row_place == column_place, 0.0, part.astype(jnp.float32))
-        return kept.astype(jnp.bfloat16)
-
+def product_of(part_ref, right_ref, starts_ref, width, start):
+    right = right_ref[start : start + part_ref.shape[1], :]
     own = pl.ds(pl.multiple_of(starts_ref[0], width), width)
-    total = product(near_ref[...], far_ref[...])
-    own_product = product(
-        without_diagonal(near_ref[own, :], 0), without_diagonal(far_ref[own, :], near)
-    )
+    total = jnp.dot(part_ref[...], right, preferred_element_type=jnp.float32)
+    strip = part_ref[own, :]
+    row_place = lax.broadcasted_iota(jnp.int32, strip.shape, 0)
+    column_place = lax.broadcasted_iota(jnp.int32, strip.shape, 1) + (start - starts_ref[1])
+    kept = jnp.where(row_place == column_place, 0.0, strip.astype(jnp.float32))
+    masked = jnp.dot(kept.astype(jnp.bfloat16), right, preferred_element_type=jnp.float32)
     place = lax.broadcasted_iota(jnp.int32, (total.shape[0], 1), 0) - starts_ref[0]
-    is_own = (place >= 0) & (place < width)
-    copies = jnp.concatenate([own_product] * (total.shape[0] // width), axis=0)
-    sums = jnp.where(is_own, copies, total).T[: vecs + 1]
+    copies = jnp.concatenate([masked] * (total.shape[0] // width), axis=0)
+    return jnp.where((place >= 0) & (place < width), copies, total)
+
+
+def first_kernel(width, starts_ref, near_ref, right_ref, out_ref):
+    out_ref[...] = product_of(near_ref, right_ref, starts_ref, width, 0)
+
+
+def sums_kernel(vecs, width, near, starts_ref, first_ref, far_ref, right_ref, out_ref):
+    total = first_ref[...] + product_of(far_ref, right_ref, starts_ref, width, near)
+    sums = total.T[: vecs + 1]
     half = vecs // 2
     for peer in range(out_ref.shape[0]):
         part = sums[:, peer * width : (peer + 1) * width]
@@ -184,17 +183,25 @@
 
     first = lax.optimization_barrier(columns[:NEAR].astype(jnp.bfloat16))
     near = affinity_to(first)
-    near, late = lax.optimization_barrier((near, columns))
+    starts = jnp.stack([lax.axis_index(PLANE) * segments, lax.axis_index(LINE) * segments])
+    first_sums = pl.pallas_call(
+        lambda *refs: first_kernel(segments, *refs),
+        out_shape=jax.ShapeDtypeStruct((row_count, 128), jnp.float32),
+        in_specs=[SMEM, VMEM, VMEM],
+        out_specs=VMEM,
+        compiler_params=grant(8),
+        name="first",
+    )(starts, near, right)
+    first_sums, late = lax.optimization_barrier((first_sums, columns))
     far = affinity_to(late[NEAR:])
-    starts = jnp.stack([lax.axis_index(PLANE) * segments, lax.axis_index(LINE) * segments])
     sums = pl.pallas_call(
-        lambda *refs: sums_kernel(vecs, segments, *refs),
+        lambda *refs: sums_kernel(vecs, segments, NEAR, *refs),
         out_shape=jax.ShapeDtypeStruct((peers, packed, 2 * segments), jnp.float32),
         in_specs=[SMEM, VMEM, VMEM, VMEM],
         out_specs=VMEM,
         compiler_params=grant(16),
         name="sums",
-    )(starts, near, far, right)
+    )(starts, first_sums, far, right)
     parts = lax.all_to_all(sums, PLANE, 0, 0, tiled=True)
     return pl.pallas_call(
         finish_kernel,

time: 86.9 us -> 86.8 us (level)
  local copies, waits for them, and re-layouts: 2.15 us -> 1.25 us
    unnamed x6, local copies, waits for them, and re-layouts: 2.15 us -> 1.25 us
    pallas_call x1 -> x2, Pallas kernels: 2.16 us -> 2.95 us  [the longest x1 1.93 us: shards(): pl.pallas_call(lambda *refs: sums_kernel(vecs, segments, NEAR, *refs), ou...]
where the time goes in v16:
time: 86.8 us; the launch traced here: 86.6 us
  blocking collectives  64.8 us (75%)
  starting transfers between devices  7.72 us (9%)
  Pallas kernels  6.66 us (8%)
  matrix products  5.65 us (7%)
  local copies, waits for them, and re-layouts  1.25 us (1%)
    all_gather x1, blocking collectives, shards(): columns = lax.all_gather(item, LINE, axis=0, tiled=True)  50.3 us
    all_to_all x1, blocking collectives, shards(): parts = lax.all_to_all(sums, PLANE, 0, 0, tiled=True)  14.5 us
    all_to_all x1, starting transfers between devices, shards(): rows = lax.all_to_all(row_copies, PLANE, 0, 0, tiled=True)  7.72 us
    dot_general x2, matrix products, affinity_to(): lax.dot_general(rows, part.astype(jnp.bfloat16), (((1,), (1,)), ((), ()))...  5.65 us
    pallas_call x1, Pallas kernels, shards(): pl.pallas_call(prepare_kernel, out_shape=(jax.ShapeDtypeStruct((peers, se...  2.66 us
    pallas_call x1, Pallas kernels, shards(): pl.pallas_call(lambda *refs: sums_kernel(vecs, segments, NEAR, *refs), ou...  1.93 us
  transfers between devices with their start and end apart: 1, of which 0 were waited for; matrix products, arithmetic and copies ran while one was open for 0% of the time, Pallas kernels for 0%

profile of v16, /device:TPU:1, one launch (start us, length us, event | category | flops | bytes accessed | tf_op | source)
XLA Modules:
  0.0 86.6 jit_solution(2550657569231417527)
XLA Ops:
  0.0 2.7 %prepare.1 = (bf16[16,64,1024]{2,1,0:T(8,128)(2,1)}, bf16[64,1024]{1,0:T(8,128)(2,1)}) custom-call(f32[1,5]{1,0:T(1,128)} %bitcast.18, bf16[5,64,192]{2,1,0:T(8,128)(2,1)} %bitcast.17, bf16[32,64]{1,0:T(8,128)(2,1)} %vectors_hbm.1), custom_call_target="tpu_custom_call" | custom-call | tf_op jit(solution)/shard_map/prepare/pallas_call | solution.py:139
  2.7 0.0 copy-start.2
  2.7 7.7 %all-to-all-start = ((bf16[16,64,1024]{2,1,0:T(8,128)(2,1)}), bf16[16,64,1024]{2,1,0:T(8,128)(2,1)S(1)}, u32[]{:S(2)}, u32[]{:S(2)}) async-start(bf16[16,64,1024]{2,1,0:T(8,128)(2,1)} %get-tuple-element.9), calls=%async_computation | async-start | bytes 4194304 | tf_op jit(solution)/shard_map/all_to_all | solution.py:160
  10.4 0.0 copy-done.2
  10.5 50.3 %all-gather.1 = f16[256,8,1024]{2,1,0:T(8,128)(2,1)S(1)} all-gather(f16[8,8,1024]{2,1,0:T(8,128)(2,1)S(1)} %convert_bitcast_fusion), channel_id=1, replica_groups=mesh['y'=4,'zl'=8,'zh'=2,'x'=4,'core'=2] {'zh','zl','core'}, dimensions={0}, use_global_device_ids=true | all-gather | bytes 4325376 | tf_op jit(solution)/shard_map/all_gather | solution.py:162
  60.7 0.0 copy-start
  60.7 0.2 slice_convert_fusion.1.refs_0_
  60.9 0.3 right.1.refs_2_.refs_3_
  61.3 0.1 fusion.2
  61.4 1.2 %copy-done = f16[256,8,1024]{2,1,0:T(8,128)(2,1)} copy-done((f16[256,8,1024]{2,1,0:T(8,128)(2,1)}, f16[256,8,1024]{2,1,0:T(8,128)(2,1)S(1)}, u32[]{:S(2)}) %copy-start) | copy-done | bytes 4194328
  62.6 0.1 pad_add_fusion.refs_0_
  62.7 0.0 all-to-all-done
  62.7 0.0 copy-start.1
  62.7 1.3 %exponential_convert_fusion.1.refs_1_ = bf16[1024,384]{1,0:T(8,128)(2,1)S(1)} fusion(bf16[1024,1024]{1,0:T(8,128)(2,1)S(1)} %bitcast.15, bf16[384,1024]{1,0:T(8,128)(2,1)S(1)} %fusion.2), kind=kOutput, calls=%fused_computation.3 | convolution fusion | flops 806092800 | bytes 3670016 | tf_op jit(solution)/shard_map/dot_general | solution.py:176
  64.0 1.0 %first.1.refs_1_ = f32[1024,128]{1,0:T(8,128)S(1)} custom-call(s32[2]{0:T(128)S(1)} %pad_add_fusion.refs_0_, bf16[1024,384]{1,0:T(8,128)(2,1)S(1)} %exponential_convert_fusion.1.refs_1_, bf16[2048,128]{1,0:T(8,128)(2,1)S(1)} %right.1.refs_2_.refs_3_), custom_call_target="tpu_custom_call" | custom-call | tf_op jit(solution)/shard_map/first/pallas_call | solution.py:187
  65.0 0.0 copy-done.1
  65.0 4.4 %exponential_convert_fusion.refs_2_ = bf16[1024,1664]{1,0:T(8,128)(2,1)S(1)} fusion(bf16[1024,1024]{1,0:T(8,128)(2,1)S(1)} %bitcast.16, f16[2048,1024]{1,0:T(8,128)(2,1)S(1)} %bitcast.14), kind=kOutput, calls=%fused_computation | convolution fusion | flops 3494772736 | bytes 8912896 | tf_op jit(solution)/shard_map/dot_general | solution.py:176
  69.4 1.9 %sums.1 = f32[16,24,128]{2,1,0:T(8,128)S(1)} custom-call(s32[2]{0:T(128)S(1)} %pad_add_fusion.refs_0_, f32[1024,128]{1,0:T(8,128)S(1)} %first.1.refs_1_, bf16[1024,1664]{1,0:T(8,128)(2,1)S(1)} %exponential_convert_fusion.refs_2_, bf16[2048,128]{1,0:T(8,128)(2,1)S(1)} %right.1.refs_2_.refs_3_), custom_call_target="tpu_custom_call" | custom-call | tf_op jit(solution)/shard_map/sums/pallas_call | solution.py:197
  71.4 14.5 %all_to_all.10.parts_ref = f32[16,24,128]{2,1,0:T(8,128)S(1)} all-to-all(f32[16,24,128]{2,1,0:T(8,128)S(1)} %sums.1), channel_id=1, replica_groups=mesh['y'=4,'zl'=8,'zh'=2,'x'=4,'core'=2] {'y','x'}, dimensions={0} | all-to-all | bytes 393216 | tf_op jit(solution)/shard_map/all_to_all | solution.py:205
  85.9 0.7 finish.1
  (1 shorter events, 0.0 us)
Async XLA Ops:
  2.7 7.7 %copy-start.2 = (bf16[64,1024]{1,0:T(8,128)(2,1)S(1)}, bf16[64,1024]{1,0:T(8,128)(2,1)}, u32[]{:S(2)}) copy-start(bf16[64,1024]{1,0:T(8,128)(2,1)} %get-tuple-element.10) | copy-start | bytes 393220
  2.7 60.0 %all-to-all-start = ((bf16[16,64,1024]{2,1,0:T(8,128)(2,1)}), bf16[16,64,1024]{2,1,0:T(8,128)(2,1)S(1)}, u32[]{:S(2)}, u32[]{:S(2)}) async-start(bf16[16,64,1024]{2,1,0:T(8,128)(2,1)} %get-tuple-element.9), calls=%async_computation | async-start | bytes 4194304 | tf_op jit(solution)/shard_map/all_to_all | solution.py:160
  60.7 1.9 %copy-start = (f16[256,8,1024]{2,1,0:T(8,128)(2,1)}, f16[256,8,1024]{2,1,0:T(8,128)(2,1)S(1)}, u32[]{:S(2)}) copy-start(f16[256,8,1024]{2,1,0:T(8,128)(2,1)S(1)} %all-gather.1) | copy-start | bytes 12582916
  62.7 2.3 %copy-start.1 = (f16[256,8,1024]{2,1,0:T(8,128)(2,1)S(1)}, f16[256,8,1024]{2,1,0:T(8,128)(2,1)}, u32[]{:S(2)}) copy-start(f16[256,8,1024]{2,1,0:T(8,128)(2,1)} %copy-done) | copy-start | bytes 12582916

commit v17 on v15

--- a/solution.py
+++ b/solution.py
@@ -14,7 +14,7 @@
 LINE = ("zh", "zl", "core")
 LANES = 1024
 PART = 64
-NEAR = 384
+NEAR = 448
 SMEM = pl.BlockSpec(memory_space=pltpu.SMEM)
 VMEM = pl.BlockSpec(memory_space=pltpu.VMEM)
 HBM = pl.BlockSpec(memory_space=pltpu.HBM)

time: 86.9 us -> 87 us (level)
  transfers between devices with their start and end apart: 1 -> 1, of which waited for: 0 -> 0; matrix products, arithmetic and copies ran while one was open for 0% -> 1% of each run, Pallas kernels for 0% -> 0%
where the time goes in v17:
time: 87 us; the launch traced here: 86.7 us
  blocking collectives  64.8 us (74%)
  starting transfers between devices  7.72 us (9%)
  Pallas kernels  5.93 us (7%)
  matrix products  5.63 us (6%)
  local copies, waits for them, and re-layouts  2.05 us (2%)
    all_gather x1, blocking collectives, shards(): columns = lax.all_gather(item, LINE, axis=0, tiled=True)  50.3 us
    all_to_all x1, blocking collectives, shards(): parts = lax.all_to_all(sums, PLANE, 0, 0, tiled=True)  14.5 us
    all_to_all x1, starting transfers between devices, shards(): rows = lax.all_to_all(row_copies, PLANE, 0, 0, tiled=True)  7.72 us
    dot_general x2, matrix products, affinity_to(): lax.dot_general(rows, part.astype(jnp.bfloat16), (((1,), (1,)), ((), ()))...  5.63 us
    pallas_call x1, Pallas kernels, shards(): pl.pallas_call(prepare_kernel, out_shape=(jax.ShapeDtypeStruct((peers, se...  2.66 us
    pallas_call x1, Pallas kernels, shards(): pl.pallas_call(lambda *refs: sums_kernel(vecs, segments, *refs), out_shap...  2.22 us
    unnamed x6, local copies, waits for them, and re-layouts  2.05 us
  transfers between devices with their start and end apart: 1, of which 0 were waited for; matrix products, arithmetic and copies ran while one was open for 1% of the time, Pallas kernels for 0%

profile of v17, /device:TPU:1, one launch (start us, length us, event | category | flops | bytes accessed | tf_op | source)
XLA Modules:
  0.0 86.7 jit_solution(12828170570014444744)
XLA Ops:
  0.0 2.7 %prepare.1 = (bf16[16,64,1024]{2,1,0:T(8,128)(2,1)}, bf16[64,1024]{1,0:T(8,128)(2,1)}) custom-call(f32[1,5]{1,0:T(1,128)} %bitcast.18, bf16[5,64,192]{2,1,0:T(8,128)(2,1)} %bitcast.17, bf16[32,64]{1,0:T(8,128)(2,1)} %vectors_hbm.1), custom_call_target="tpu_custom_call" | custom-call | tf_op jit(solution)/shard_map/prepare/pallas_call | solution.py:140
  2.7 0.0 copy-start.2
  2.7 7.7 %all-to-all-start = ((bf16[16,64,1024]{2,1,0:T(8,128)(2,1)}), bf16[16,64,1024]{2,1,0:T(8,128)(2,1)S(1)}, u32[]{:S(2)}, u32[]{:S(2)}) async-start(bf16[16,64,1024]{2,1,0:T(8,128)(2,1)} %get-tuple-element.9), calls=%async_computation | async-start | bytes 4194304 | tf_op jit(solution)/shard_map/all_to_all | solution.py:161
  10.4 0.0 copy-done.2
  10.5 50.3 %all-gather.1 = f16[256,8,1024]{2,1,0:T(8,128)(2,1)S(1)} all-gather(f16[8,8,1024]{2,1,0:T(8,128)(2,1)S(1)} %convert_bitcast_fusion), channel_id=1, replica_groups=mesh['y'=4,'zl'=8,'zh'=2,'x'=4,'core'=2] {'zh','zl','core'}, dimensions={0}, use_global_device_ids=true | all-gather | bytes 4325376 | tf_op jit(solution)/shard_map/all_gather | solution.py:163
  60.7 0.0 copy-start
  60.7 0.2 fusion.2
  60.9 0.2 slice_convert_fusion.1.refs_0_
  61.1 0.3 right.1.refs_3_
  61.5 1.2 %copy-done = f16[256,8,1024]{2,1,0:T(8,128)(2,1)} copy-done((f16[256,8,1024]{2,1,0:T(8,128)(2,1)}, f16[256,8,1024]{2,1,0:T(8,128)(2,1)S(1)}, u32[]{:S(2)}) %copy-start) | copy-done | bytes 4194328
  62.6 0.1 pad_add_fusion.refs_0_
  62.7 0.0 all-to-all-done
  62.7 0.0 copy-start.1
  62.7 1.3 %exponential_convert_fusion.1.refs_1_ = bf16[1024,448]{1,0:T(8,128)(2,1)S(1)} fusion(bf16[1024,1024]{1,0:T(8,128)(2,1)S(1)} %bitcast.15, bf16[448,1024]{1,0:T(8,128)(2,1)S(1)} %fusion.2), kind=kOutput, calls=%fused_computation.3 | convolution fusion | flops 940441600 | bytes 3932160 | tf_op jit(solution)/shard_map/dot_general | solution.py:177
  64.0 0.9 %copy-done.1 = f16[256,8,1024]{2,1,0:T(8,128)(2,1)S(1)} copy-done((f16[256,8,1024]{2,1,0:T(8,128)(2,1)S(1)}, f16[256,8,1024]{2,1,0:T(8,128)(2,1)}, u32[]{:S(2)}) %copy-start.1) | copy-done | bytes 4194328
  64.9 4.3 %exponential_convert_fusion.refs_2_ = bf16[1024,1600]{1,0:T(8,128)(2,1)S(1)} fusion(bf16[1024,1024]{1,0:T(8,128)(2,1)S(1)} %bitcast.16, f16[2048,1024]{1,0:T(8,128)(2,1)S(1)} %bitcast.14), kind=kOutput, calls=%fused_computation | convolution fusion | flops 3360358400 | bytes 8650752 | tf_op jit(solution)/shard_map/dot_general | solution.py:177
  69.3 2.2 %sums.1 = f32[16,24,128]{2,1,0:T(8,128)S(1)} custom-call(s32[2]{0:T(128)S(1)} %pad_add_fusion.refs_0_, bf16[1024,448]{1,0:T(8,128)(2,1)S(1)} %exponential_convert_fusion.1.refs_1_, bf16[1024,1600]{1,0:T(8,128)(2,1)S(1)} %exponential_convert_fusion.refs_2_, bf16[2048,128]{1,0:T(8,128)(2,1)S(1)} %right.1.refs_3_), custom_call_target="tpu_custom_call" | custom-call | tf_op jit(solution)/shard_map/sums/pallas_call | solution.py:190
  71.5 14.5 %all_to_all.10.parts_ref = f32[16,24,128]{2,1,0:T(8,128)S(1)} all-to-all(f32[16,24,128]{2,1,0:T(8,128)S(1)} %sums.1), channel_id=1, replica_groups=mesh['y'=4,'zl'=8,'zh'=2,'x'=4,'core'=2] {'y','x'}, dimensions={0} | all-to-all | bytes 393216 | tf_op jit(solution)/shard_map/all_to_all | solution.py:198
  86.0 0.7 finish.1
  (1 shorter events, 0.0 us)
Async XLA Ops:
  2.7 7.7 %copy-start.2 = (bf16[64,1024]{1,0:T(8,128)(2,1)S(1)}, bf16[64,1024]{1,0:T(8,128)(2,1)}, u32[]{:S(2)}) copy-start(bf16[64,1024]{1,0:T(8,128)(2,1)} %get-tuple-element.10) | copy-start | bytes 393220
  2.7 60.0 %all-to-all-start = ((bf16[16,64,1024]{2,1,0:T(8,128)(2,1)}), bf16[16,64,1024]{2,1,0:T(8,128)(2,1)S(1)}, u32[]{:S(2)}, u32[]{:S(2)}) async-start(bf16[16,64,1024]{2,1,0:T(8,128)(2,1)} %get-tuple-element.9), calls=%async_computation | async-start | bytes 4194304 | tf_op jit(solution)/shard_map/all_to_all | solution.py:161
  60.7 1.9 %copy-start = (f16[256,8,1024]{2,1,0:T(8,128)(2,1)}, f16[256,8,1024]{2,1,0:T(8,128)(2,1)S(1)}, u32[]{:S(2)}) copy-start(f16[256,8,1024]{2,1,0:T(8,128)(2,1)S(1)} %all-gather.1) | copy-start | bytes 12582916
  62.7 2.2 %copy-start.1 = (f16[256,8,1024]{2,1,0:T(8,128)(2,1)S(1)}, f16[256,8,1024]{2,1,0:T(8,128)(2,1)}, u32[]{:S(2)}) copy-start(f16[256,8,1024]{2,1,0:T(8,128)(2,1)} %copy-done) | copy-start | bytes 12582916

commit v18 on v17

--- a/solution.py
+++ b/solution.py
@@ -14,7 +14,7 @@
 LINE = ("zh", "zl", "core")
 LANES = 1024
 PART = 64
-NEAR = 448
+NEAR = 256
 SMEM = pl.BlockSpec(memory_space=pltpu.SMEM)
 VMEM = pl.BlockSpec(memory_space=pltpu.VMEM)
 HBM = pl.BlockSpec(memory_space=pltpu.HBM)

time: 87 us -> 86.9 us (level)
  transfers between devices with their start and end apart: 1 -> 1, of which waited for: 0 -> 0; matrix products, arithmetic and copies ran while one was open for 1% -> 0% of each run, Pallas kernels for 0% -> 0%
where the time goes in v18:
time: 86.9 us; the launch traced here: 86.7 us
  blocking collectives  64.8 us (75%)
  starting transfers between devices  7.72 us (9%)
  Pallas kernels  5.85 us (7%)
  matrix products  5.11 us (6%)
  local copies, waits for them, and re-layouts  2.71 us (3%)
    all_gather x1, blocking collectives, shards(): columns = lax.all_gather(item, LINE, axis=0, tiled=True)  50.3 us
    all_to_all x1, blocking collectives, shards(): parts = lax.all_to_all(sums, PLANE, 0, 0, tiled=True)  14.5 us
    all_to_all x1, starting transfers between devices, shards(): rows = lax.all_to_all(row_copies, PLANE, 0, 0, tiled=True)  7.72 us
    dot_general x2, matrix products, affinity_to(): lax.dot_general(rows, part.astype(jnp.bfloat16), (((1,), (1,)), ((), ()))...  5.11 us
    unnamed x6, local copies, waits for them, and re-layouts  2.71 us
    pallas_call x1, Pallas kernels, shards(): pl.pallas_call(prepare_kernel, out_shape=(jax.ShapeDtypeStruct((peers, se...  2.66 us
    pallas_call x1, Pallas kernels, shards(): pl.pallas_call(lambda *refs: sums_kernel(vecs, segments, *refs), out_shap...  2.14 us
  transfers between devices with their start and end apart: 1, of which 0 were waited for; matrix products, arithmetic and copies ran while one was open for 0% of the time, Pallas kernels for 0%

profile of v18, /device:TPU:1, one launch (start us, length us, event | category | flops | bytes accessed | tf_op | source)
XLA Modules:
  0.0 86.7 jit_solution(12669250621797327779)
XLA Ops:
  0.0 2.7 %prepare.1 = (bf16[16,64,1024]{2,1,0:T(8,128)(2,1)}, bf16[64,1024]{1,0:T(8,128)(2,1)}) custom-call(f32[1,5]{1,0:T(1,128)} %bitcast.18, bf16[5,64,192]{2,1,0:T(8,128)(2,1)} %bitcast.17, bf16[32,64]{1,0:T(8,128)(2,1)} %vectors_hbm.1), custom_call_target="tpu_custom_call" | custom-call | tf_op jit(solution)/shard_map/prepare/pallas_call | solution.py:140
  2.7 0.0 copy-start.2
  2.7 7.7 %all-to-all-start = ((bf16[16,64,1024]{2,1,0:T(8,128)(2,1)}), bf16[16,64,1024]{2,1,0:T(8,128)(2,1)S(1)}, u32[]{:S(2)}, u32[]{:S(2)}) async-start(bf16[16,64,1024]{2,1,0:T(8,128)(2,1)} %get-tuple-element.9), calls=%async_computation | async-start | bytes 4194304 | tf_op jit(solution)/shard_map/all_to_all | solution.py:161
  10.4 0.0 copy-done.2
  10.5 50.3 %all-gather.1 = f16[256,8,1024]{2,1,0:T(8,128)(2,1)S(1)} all-gather(f16[8,8,1024]{2,1,0:T(8,128)(2,1)S(1)} %convert_bitcast_fusion), channel_id=1, replica_groups=mesh['y'=4,'zl'=8,'zh'=2,'x'=4,'core'=2] {'zh','zl','core'}, dimensions={0}, use_global_device_ids=true | all-gather | bytes 4325376 | tf_op jit(solution)/shard_map/all_gather | solution.py:163
  60.7 0.0 copy-start
  60.7 0.1 fusion.4
  60.8 0.2 slice_convert_fusion.refs_0_
  61.0 0.3 right.1.refs_3_
  61.4 1.3 %copy-done = f16[256,8,1024]{2,1,0:T(8,128)(2,1)} copy-done((f16[256,8,1024]{2,1,0:T(8,128)(2,1)}, f16[256,8,1024]{2,1,0:T(8,128)(2,1)S(1)}, u32[]{:S(2)}) %copy-start) | copy-done | bytes 4194328
  62.6 0.1 pad_add_fusion.refs_0_
  62.7 0.0 all-to-all-done
  62.7 0.0 copy-start.1
  62.7 0.7 fusion.3.refs_1_
  63.5 1.4 %copy-done.1 = f16[256,8,1024]{2,1,0:T(8,128)(2,1)S(1)} copy-done((f16[256,8,1024]{2,1,0:T(8,128)(2,1)S(1)}, f16[256,8,1024]{2,1,0:T(8,128)(2,1)}, u32[]{:S(2)}) %copy-start.1) | copy-done | bytes 4194328
  64.9 4.4 %exponential_convert_fusion.refs_2_ = bf16[1024,1792]{1,0:T(8,128)(2,1)S(1)} fusion(bf16[1024,1024]{1,0:T(8,128)(2,1)S(1)} %bitcast.16, f16[2048,1024]{1,0:T(8,128)(2,1)S(1)} %bitcast.14), kind=kOutput, calls=%fused_computation | convolution fusion | flops 3763601408 | bytes 9437184 | tf_op jit(solution)/shard_map/dot_general | solution.py:177
  69.3 2.1 %sums.1 = f32[16,24,128]{2,1,0:T(8,128)S(1)} custom-call(s32[2]{0:T(128)S(1)} %pad_add_fusion.refs_0_, bf16[1024,256]{1,0:T(8,128)(2,1)S(1)} %fusion.3.refs_1_, bf16[1024,1792]{1,0:T(8,128)(2,1)S(1)} %exponential_convert_fusion.refs_2_, bf16[2048,128]{1,0:T(8,128)(2,1)S(1)} %right.1.refs_3_), custom_call_target="tpu_custom_call" | custom-call | tf_op jit(solution)/shard_map/sums/pallas_call | solution.py:190
  71.4 14.5 %all_to_all.10.parts_ref = f32[16,24,128]{2,1,0:T(8,128)S(1)} all-to-all(f32[16,24,128]{2,1,0:T(8,128)S(1)} %sums.1), channel_id=1, replica_groups=mesh['y'=4,'zl'=8,'zh'=2,'x'=4,'core'=2] {'y','x'}, dimensions={0} | all-to-all | bytes 393216 | tf_op jit(solution)/shard_map/all_to_all | solution.py:198
  86.0 0.7 finish.1
  (1 shorter events, 0.0 us)
Async XLA Ops:
  2.7 7.7 %copy-start.2 = (bf16[64,1024]{1,0:T(8,128)(2,1)S(1)}, bf16[64,1024]{1,0:T(8,128)(2,1)}, u32[]{:S(2)}) copy-start(bf16[64,1024]{1,0:T(8,128)(2,1)} %get-tuple-element.10) | copy-start | bytes 393220
  2.7 60.0 %all-to-all-start = ((bf16[16,64,1024]{2,1,0:T(8,128)(2,1)}), bf16[16,64,1024]{2,1,0:T(8,128)(2,1)S(1)}, u32[]{:S(2)}, u32[]{:S(2)}) async-start(bf16[16,64,1024]{2,1,0:T(8,128)(2,1)} %get-tuple-element.9), calls=%async_computation | async-start | bytes 4194304 | tf_op jit(solution)/shard_map/all_to_all | solution.py:161
  60.7 1.9 %copy-start = (f16[256,8,1024]{2,1,0:T(8,128)(2,1)}, f16[256,8,1024]{2,1,0:T(8,128)(2,1)S(1)}, u32[]{:S(2)}) copy-start(f16[256,8,1024]{2,1,0:T(8,128)(2,1)S(1)} %all-gather.1) | copy-start | bytes 12582916
  62.7 2.2 %copy-start.1 = (f16[256,8,1024]{2,1,0:T(8,128)(2,1)S(1)}, f16[256,8,1024]{2,1,0:T(8,128)(2,1)}, u32[]{:S(2)}) copy-start(f16[256,8,1024]{2,1,0:T(8,128)(2,1)} %copy-done) | copy-start | bytes 12582916
